TPU v7x, 32 devices: a whole 2x2x4 slice. The times are simulated.
32 devices in a mesh: ctx: 16 (over z, y, x), head: 2 (over core).
Axes of the slice: x: 2, y: 2, z: 4, core: 2. Of those that a mesh axis runs over, the one named last changes fastest.
Arguments:
- layer_in: float32 [2048, 768], P('ctx'), may hold values from -6 to 6
- encoded: bfloat16 [1024, 768], P('ctx'), may hold values from -6 to 6
- self_query: bfloat16 [768, 768], P('ctx', 'head'), may hold values from -0.02734375 to 0.02734375
- self_key: bfloat16 [768, 768], P('ctx', 'head'), may hold values from -0.21875 to 0.21875
- self_value: bfloat16 [768, 768], P('ctx', 'head'), may hold values from -0.21875 to 0.21875
- self_out: bfloat16 [768, 768], P('head', 'ctx'), may hold values from -4 to 4
- cross_query: bfloat16 [768, 768], P('ctx', 'head'), may hold values from -0.02734375 to 0.02734375
- cross_key: bfloat16 [768, 768], P('ctx', 'head'), may hold values from -0.21875 to 0.21875
- cross_value: bfloat16 [768, 768], P('ctx', 'head'), may hold values from -0.21875 to 0.21875
- cross_out: bfloat16 [768, 768], P('head', 'ctx'), may hold values from -4 to 4
- gate_proj: bfloat16 [768, 2048], P('ctx', 'head'), may hold values from -0.21875 to 0.21875
- up_proj: bfloat16 [768, 2048], P('ctx', 'head'), may hold values from -0.21875 to 0.21875
- down_proj: bfloat16 [2048, 768], P('head', 'ctx'), may hold values from -0.125 to 0.125
- norm_gains: float32 [3, 768], replicated, may hold values from 0.5 to 1.5
- position_bias: float32 [32, 12], P(None, 'head'), may hold values from -4 to 4
- bucket_ids: int32 [2048], replicated, may hold values from 0 to 31, never falling along the last dimension, each value on 1 to 1024 neighbouring positions
- block_order: int32 [16], replicated, may hold values from 0 to 15, each once
- out_grad: float32 [2048, 768], P('ctx'), may hold values from -6 to 6
Outputs:
- layer_out: float32 [2048, 768], P('ctx')
- input_grad: float32 [2048, 768], P('ctx')
- encoded_grad: float32 [1024, 768], P('ctx')
- self_query_grad: float32 [768, 768], P('ctx', 'head')
- self_key_grad: float32 [768, 768], P('ctx', 'head')
- self_value_grad: float32 [768, 768], P('ctx', 'head')
- self_out_grad: float32 [768, 768], P('head', 'ctx')
- cross_query_grad: float32 [768, 768], P('ctx', 'head')
- cross_key_grad: float32 [768, 768], P('ctx', 'head')
- cross_value_grad: float32 [768, 768], P('ctx', 'head')
- cross_out_grad: float32 [768, 768], P('head', 'ctx')
- gate_proj_grad: float32 [768, 2048], P('ctx', 'head')
- up_proj_grad: float32 [768, 2048], P('ctx', 'head')
- down_proj_grad: float32 [2048, 768], P('head', 'ctx')
- norm_gains_grad: float32 [3, 768], replicated
- position_bias_grad: float32 [32, 12], P(None, 'head')
Inputs may be any that keep to these rules, and one draw needn't show every extreme that they name: Never falls along the distance; bucket_ids[0] = 0 and the last value is 31. `block_order`: each block number appears once.
All inputs are finite; a program needn't handle non-finite values.
Results may differ from a plain program's by a relative error of at most 0.04.
Values may be sent and summed in bfloat16 or wider, within the bound.
A program may use at most 192 MiB of HBM per device.

v0:
```python
import math

import jax
import jax.numpy as jnp
from jax import lax
from jax.sharding import PartitionSpec as P

EPS = 1e-06
NEG = -1e30
HIGH = lax.Precision.HIGHEST


def as_sent(shard):

    def short(part):
        return part.astype(jnp.bfloat16) if part.dtype == jnp.float32 else part

    return jax.tree.map(short, shard)


def rms_scale(rows, gain):
    return rows * lax.rsqrt(jnp.mean(rows * rows, axis=-1, keepdims=True) + EPS) * gain


def geglu(gate, upper):
    return jax.nn.gelu(gate, approximate=True) * upper


def times(left, right):
    return jnp.dot(left, right, preferred_element_type=jnp.float32)


def left_times(left, right):
    return lax.dot_general(
        left, right, (((0,), (0,)), ((), ())), preferred_element_type=jnp.float32
    )


def right_times(left, right):
    return lax.dot_general(
        left, right, (((1,), (1,)), ((), ())), preferred_element_type=jnp.float32
    )


def join_heads(parts):
    return jax.tree.map(lambda part: part.astype(jnp.float32), lax.psum(as_sent(parts), "head"))


def gather_self(keys_own, values_own):
    return (
        lax.all_gather(keys_own, "ctx", axis=0, tiled=True),
        lax.all_gather(values_own, "ctx", axis=0, tiled=True),
    )


def gather_cross(memory_keys, memory_values):
    return (
        lax.all_gather(memory_keys, "ctx", axis=0, tiled=True),
        lax.all_gather(memory_values, "ctx", axis=0, tiled=True),
    )


def bias_scores(steps, bias_table):
    rises = bias_table[1:] - bias_table[:-1]
    return bias_table[0][:, None, None] + jnp.einsum("qkb,bh->hqk", steps, rises, precision=HIGH)


def bias_grads(score_grad, steps):
    above = jnp.einsum("hqk,qkb->bh", score_grad, steps, precision=HIGH)
    total = jnp.sum(score_grad, axis=(1, 2))
    upper_rows = jnp.concatenate((total[None], above), axis=0)
    lower_rows = jnp.concatenate((above, jnp.zeros((1, above.shape[1]), jnp.float32)), axis=0)
    return upper_rows - lower_rows


def delta_of(mixed, mixed_grad, head_count):
    tok_rows, total_width = mixed.shape
    width = total_width // head_count
    product = mixed.astype(jnp.float32).reshape(tok_rows, head_count, width) * mixed_grad.astype(
        jnp.float32
    ).reshape(tok_rows, head_count, width)
    return jnp.transpose(jnp.sum(product, axis=-1))


def attend_fold(queries, head_count, parts_fn, bias_table):
    tok_rows = queries.shape[0]
    width = queries.shape[1] // head_count
    query3 = queries.reshape(tok_rows, head_count, width)

    def fold(state, pieces, start):
        key_piece, value_piece = pieces
        count = key_piece.shape[0]
        block = math.gcd(count, 512)

        def fold_step(index, inner):
            summed, run_max, run_sum = inner
            key3 = lax.dynamic_slice_in_dim(key_piece, index * block, block, 0).reshape(
                block, head_count, width
            )
            value3 = lax.dynamic_slice_in_dim(value_piece, index * block, block, 0).reshape(
                block, head_count, width
            )
            scores = jnp.einsum("qhe,khe->hqk", query3, key3, preferred_element_type=jnp.float32)
            if parts_fn is not None:
                steps, valid = parts_fn(index * block, block)
                scores = jnp.where(valid[None], scores + bias_scores(steps, bias_table), NEG)
            new_max = jnp.maximum(run_max, jnp.max(scores, axis=-1))
            ratio = jnp.exp(run_max - new_max)
            weights = jnp.exp(scores - new_max[..., None])
            run_sum = run_sum * ratio + jnp.sum(weights, axis=-1)
            summed = summed * ratio[..., None] + jnp.einsum(
                "hqk,khe->hqe",
                weights.astype(jnp.bfloat16),
                value3,
                preferred_element_type=jnp.float32,
            )
            return (summed, new_max, run_sum)

        return lax.fori_loop(0, count // block, fold_step, state)

    return fold


def finish(state):
    summed, run_max, run_sum = state
    head_count, tok_rows, width = summed.shape
    mixed = jnp.transpose(summed / run_sum[..., None], (1, 0, 2)).reshape(
        tok_rows, head_count * width
    )
    return (mixed.astype(jnp.bfloat16), run_max + jnp.log(run_sum))


def attend_back(
    queries, mixed_grad, lse, delta, keys_all, values_all, head_count, parts_fn, bias_table
):
    tok_rows, total_width = queries.shape
    width = total_width // head_count
    query3 = queries.reshape(tok_rows, head_count, width)
    grad3 = mixed_grad.reshape(tok_rows, head_count, width)
    count = keys_all.shape[0]
    block = math.gcd(count, 512)

    def attend_step(carry, index):
        query_grad, bias_grad = carry
        key3 = lax.dynamic_slice_in_dim(keys_all, index * block, block, 0).reshape(
            block, head_count, width
        )
        value3 = lax.dynamic_slice_in_dim(values_all, index * block, block, 0).reshape(
            block, head_count, width
        )
        scores = jnp.einsum("qhe,khe->hqk", query3, key3, preferred_element_type=jnp.float32)
        if parts_fn is not None:
            steps, valid = parts_fn(index * block, block)
            scores = jnp.where(valid[None], scores + bias_scores(steps, bias_table), NEG)
        weights = jnp.exp(scores - lse[..., None])
        weight_grad = jnp.einsum("qhe,khe->hqk", grad3, value3, preferred_element_type=jnp.float32)
        score_grad = weights * (weight_grad - delta[..., None])
        if parts_fn is not None:
            bias_grad = bias_grad + bias_grads(score_grad, steps)
        score_low = score_grad.astype(jnp.bfloat16)
        query_grad = query_grad + jnp.einsum(
            "hqk,khe->qhe", score_low, key3, preferred_element_type=jnp.float32
        )
        stacked = None
        value_term = jnp.einsum(
            "hqk,qhe->khe", weights.astype(jnp.bfloat16), grad3, preferred_element_type=jnp.float32
        )
        key_term = jnp.einsum("hqk,qhe->khe", score_low, query3, preferred_element_type=jnp.float32)
        stacked = jnp.concatenate(
            (key_term.reshape(block, total_width), value_term.reshape(block, total_width)), axis=1
        )
        return ((query_grad, bias_grad), stacked)

    start = (
        jnp.zeros((tok_rows, head_count, width), jnp.float32),
        jnp.zeros(bias_table.shape, jnp.float32),
    )
    (query_grad, bias_grad), terms = lax.scan(attend_step, start, jnp.arange(count // block))
    query_grad = query_grad.reshape(tok_rows, total_width).astype(jnp.bfloat16)
    terms = terms.reshape(count, 2 * total_width)
    return (query_grad, bias_grad, terms)


def per_device(
    layer_in,
    encoded,
    self_query,
    self_key,
    self_value,
    self_out,
    cross_query,
    cross_key,
    cross_value,
    cross_out,
    gate_proj,
    up_proj,
    down_proj,
    norm_gains,
    position_bias,
    bucket_ids,
    block_order,
    out_grad,
):
    low = jnp.bfloat16
    tok_rows = layer_in.shape[0]
    bucket_count, head_count = position_bias.shape
    block_count = block_order.shape[0]
    full_weights = (
        lax.all_gather(self_query, "ctx", axis=0, tiled=True),
        lax.all_gather(self_key, "ctx", axis=0, tiled=True),
        lax.all_gather(self_value, "ctx", axis=0, tiled=True),
        lax.all_gather(self_out, "ctx", axis=1, tiled=True),
        lax.all_gather(cross_query, "ctx", axis=0, tiled=True),
        lax.all_gather(cross_key, "ctx", axis=0, tiled=True),
        lax.all_gather(cross_value, "ctx", axis=0, tiled=True),
        lax.all_gather(cross_out, "ctx", axis=1, tiled=True),
        lax.all_gather(gate_proj, "ctx", axis=0, tiled=True),
        lax.all_gather(up_proj, "ctx", axis=0, tiled=True),
        lax.all_gather(down_proj, "ctx", axis=1, tiled=True),
    )
    (
        query_full,
        key_full,
        value_full,
        output_full,
        probe_full,
        lookup_full,
        recall_full,
        merge_full,
        gate_full,
        upward_full,
        down_full,
    ) = full_weights
    boundaries = jnp.arange(1, bucket_count, dtype=jnp.int32)
    starts = jnp.sum((bucket_ids[None, :] < boundaries[:, None]).astype(jnp.int32), axis=1)
    block_ids = jnp.arange(block_count, dtype=jnp.int32)
    here = lax.axis_index("ctx")
    own_block = jnp.sum(jnp.where(block_ids == here, block_order, 0))
    query_pos = own_block * tok_rows + jnp.arange(tok_rows, dtype=jnp.int32)

    def position_of(rows_index):
        slot = rows_index // tok_rows
        owner = jnp.sum(
            jnp.where(slot[:, None] == block_ids[None, :], block_order[None, :], 0), axis=1
        )
        return owner * tok_rows + rows_index % tok_rows

    def pair_parts(first_pos, second_pos):
        dist = first_pos[:, None] - second_pos[None, :]
        steps = (dist[:, :, None] >= starts[None, None, :]).astype(jnp.float32)
        return (steps, dist >= 0)

    def causal_parts(key_start, count):
        return pair_parts(query_pos, position_of(key_start + jnp.arange(count, dtype=jnp.int32)))

    normed_one = rms_scale(layer_in, norm_gains[0]).astype(low)
    queries = times(normed_one, query_full).astype(low)
    keys_own = times(normed_one, key_full).astype(low)
    values_own = times(normed_one, value_full).astype(low)
    memory_keys = times(encoded, lookup_full).astype(low)
    memory_values = times(encoded, recall_full).astype(low)
    total_width = queries.shape[1]
    width = total_width // head_count
    start_state = (
        jnp.zeros((head_count, tok_rows, width), jnp.float32),
        jnp.full((head_count, tok_rows), NEG, jnp.float32),
        jnp.zeros((head_count, tok_rows), jnp.float32),
    )
    self_fold = attend_fold(queries, head_count, causal_parts, position_bias)
    self_state = self_fold(
        start_state,
        (
            lax.all_gather(keys_own, "ctx", axis=0, tiled=True),
            lax.all_gather(values_own, "ctx", axis=0, tiled=True),
        ),
        jnp.int32(0),
    )
    mixed_one, lse_one = finish(self_state)
    after_self = layer_in + join_heads(times(mixed_one, output_full))
    normed_two = rms_scale(after_self, norm_gains[1]).astype(low)
    probes = times(normed_two, probe_full).astype(low)
    cross_fold = attend_fold(probes, head_count, None, position_bias)
    cross_state = cross_fold(
        start_state,
        (
            lax.all_gather(memory_keys, "ctx", axis=0, tiled=True),
            lax.all_gather(memory_values, "ctx", axis=0, tiled=True),
        ),
        jnp.int32(0),
    )
    mixed_two, lse_two = finish(cross_state)
    after_cross = after_self + join_heads(times(mixed_two, merge_full))
    normed_three = rms_scale(after_cross, norm_gains[2]).astype(low)
    gate_pre = times(normed_three, gate_full)
    upper = times(normed_three, upward_full)
    activated = geglu(gate_pre, upper).astype(low)
    layer_out = after_cross + join_heads(times(activated, down_full))
    grad_rows = out_grad.astype(low)
    down_wgrad = left_times(activated, grad_rows)
    act_grad = right_times(grad_rows, down_full)
    geglu_out, geglu_pull = jax.vjp(geglu, gate_pre, upper)
    gate_grad, upper_grad = geglu_pull(act_grad)
    gate_grad = gate_grad.astype(low)
    upper_grad = upper_grad.astype(low)
    gate_wgrad = left_times(normed_three, gate_grad)
    up_wgrad = left_times(normed_three, upper_grad)
    normed_three_grad = join_heads(
        right_times(gate_grad, gate_full) + right_times(upper_grad, upward_full)
    )
    norm_out, norm_pull = jax.vjp(rms_scale, after_cross, norm_gains[2])
    cross_extra, gain_three = norm_pull(normed_three_grad)
    cross_grad = out_grad + cross_extra
    cross_rows = cross_grad.astype(low)
    merge_wgrad = left_times(mixed_two, cross_rows)
    mixed_two_grad = right_times(cross_rows, merge_full).astype(low)
    delta_two = delta_of(mixed_two, mixed_two_grad, head_count)
    memory_all = gather_cross(memory_keys, memory_values)
    probe_grad, unused_bias, cross_terms = attend_back(
        probes,
        mixed_two_grad,
        lse_two,
        delta_two,
        memory_all[0],
        memory_all[1],
        head_count,
        None,
        position_bias,
    )
    cross_terms = lax.psum_scatter(cross_terms, "ctx", scatter_dimension=0, tiled=True)
    memory_key_grad = cross_terms[:, :total_width].astype(low)
    memory_value_grad = cross_terms[:, total_width:].astype(low)
    probe_wgrad = left_times(normed_two, probe_grad)
    lookup_wgrad = left_times(encoded, memory_key_grad)
    recall_wgrad = left_times(encoded, memory_value_grad)
    normed_two_grad, encoded_grad = join_heads(
        (
            right_times(probe_grad, probe_full),
            right_times(memory_key_grad, lookup_full) + right_times(memory_value_grad, recall_full),
        )
    )
    norm_out, norm_pull = jax.vjp(rms_scale, after_self, norm_gains[1])
    self_extra, gain_two = norm_pull(normed_two_grad)
    self_grad = cross_grad + self_extra
    self_rows = self_grad.astype(low)
    output_wgrad = left_times(mixed_one, self_rows)
    mixed_one_grad = right_times(self_rows, output_full).astype(low)
    delta_one = delta_of(mixed_one, mixed_one_grad, head_count)
    sequence_all = gather_self(keys_own, values_own)
    query_grad, bias_grad, self_terms = attend_back(
        queries,
        mixed_one_grad,
        lse_one,
        delta_one,
        sequence_all[0],
        sequence_all[1],
        head_count,
        causal_parts,
        position_bias,
    )
    self_terms = lax.psum_scatter(self_terms, "ctx", scatter_dimension=0, tiled=True)
    key_grad = self_terms[:, :total_width].astype(low)
    value_grad = self_terms[:, total_width:].astype(low)
    query_wgrad = left_times(normed_one, query_grad)
    key_wgrad = left_times(normed_one, key_grad)
    value_wgrad = left_times(normed_one, value_grad)
    normed_one_grad = join_heads(
        right_times(query_grad, query_full)
        + right_times(key_grad, key_full)
        + right_times(value_grad, value_full)
    )
    norm_out, norm_pull = jax.vjp(rms_scale, layer_in, norm_gains[0])
    input_extra, gain_one = norm_pull(normed_one_grad)
    input_grad = self_grad + input_extra
    weight_sums = (
        lax.psum_scatter(query_wgrad, "ctx", scatter_dimension=0, tiled=True),
        lax.psum_scatter(key_wgrad, "ctx", scatter_dimension=0, tiled=True),
        lax.psum_scatter(value_wgrad, "ctx", scatter_dimension=0, tiled=True),
        lax.psum_scatter(output_wgrad, "ctx", scatter_dimension=1, tiled=True),
        lax.psum_scatter(probe_wgrad, "ctx", scatter_dimension=0, tiled=True),
        lax.psum_scatter(lookup_wgrad, "ctx", scatter_dimension=0, tiled=True),
        lax.psum_scatter(recall_wgrad, "ctx", scatter_dimension=0, tiled=True),
        lax.psum_scatter(merge_wgrad, "ctx", scatter_dimension=1, tiled=True),
        lax.psum_scatter(gate_wgrad, "ctx", scatter_dimension=0, tiled=True),
        lax.psum_scatter(up_wgrad, "ctx", scatter_dimension=0, tiled=True),
        lax.psum_scatter(down_wgrad, "ctx", scatter_dimension=1, tiled=True),
    )
    gains_sum, bias_sum = lax.psum((jnp.stack((gain_one, gain_two, gain_three)), bias_grad), "ctx")
    return (layer_out, input_grad, encoded_grad) + tuple(weight_sums) + (gains_sum, bias_sum)


def solution(mesh):
    placed = (
        P("ctx", None),
        P("ctx", None),
        P("ctx", "head"),
        P("ctx", "head"),
        P("ctx", "head"),
        P("head", "ctx"),
        P("ctx", "head"),
        P("ctx", "head"),
        P("ctx", "head"),
        P("head", "ctx"),
        P("ctx", "head"),
        P("ctx", "head"),
        P("head", "ctx"),
        P(),
        P(None, "head"),
        P(),
        P(),
        P("ctx", None),
    )
    return jax.shard_map(
        per_device,
        mesh=mesh,
        in_specs=placed,
        out_specs=(
            P("ctx", None),
            P("ctx", None),
            P("ctx", None),
            P("ctx", "head"),
            P("ctx", "head"),
            P("ctx", "head"),
            P("head", "ctx"),
            P("ctx", "head"),
            P("ctx", "head"),
            P("ctx", "head"),
            P("head", "ctx"),
            P("ctx", "head"),
            P("ctx", "head"),
            P("head", "ctx"),
            P(),
            P(None, "head"),
        ),
        check_vma=False,
    )
```

profile of v0, /device:TPU:0, one launch (start us, length us, event | category | flops | bytes accessed | tf_op | source)
XLA Modules:
  0.0 2517.2 jit_solution(4990660504476210054)
XLA Ops:
  9.3 45.9 %all_gather.49 = bf16[768,384]{1,0:T(8,128)(2,1)S(1)} all-gather(bf16[48,384]{1,0:T(8,128)(2,1)} %param.29), channel_id=1, replica_groups=mesh['ctx'=16,'head'=2] {'ctx'}, dimensions={0}, use_global_device_ids=true | all-gather | bytes 626688 | tf_op jit(solution)/shard_map/all_gather | solution.py:210
  57.5 40.5 %all_gather.52 = bf16[768,384]{1,0:T(8,128)(2,1)S(1)} all-gather(bf16[48,384]{1,0:T(8,128)(2,1)S(1)} %copy-done.70), channel_id=1, replica_groups=mesh['ctx'=16,'head'=2] {'ctx'}, dimensions={0}, use_global_device_ids=true | all-gather | bytes 626688 | tf_op jit(solution)/shard_map/all_gather | solution.py:211
  99.8 42.4 %all_gather.51 = bf16[768,384]{1,0:T(8,128)(2,1)S(1)} all-gather(bf16[48,384]{1,0:T(8,128)(2,1)S(1)} %copy-done.71), channel_id=1, replica_groups=mesh['ctx'=16,'head'=2] {'ctx'}, dimensions={0}, use_global_device_ids=true | all-gather | bytes 626688 | tf_op jit(solution)/shard_map/all_gather | solution.py:209
  143.3 40.6 %all_gather.58 = bf16[768,384]{1,0:T(8,128)(2,1)S(1)} all-gather(bf16[48,384]{1,0:T(8,128)(2,1)S(1)} %copy-done.72), channel_id=1, replica_groups=mesh['ctx'=16,'head'=2] {'ctx'}, dimensions={0}, use_global_device_ids=true | all-gather | bytes 626688 | tf_op jit(solution)/shard_map/all_gather | solution.py:215
  184.9 40.9 %all_gather.59 = bf16[1024,384]{1,0:T(8,128)(2,1)S(1)} all-gather(bf16[64,384]{1,0:T(8,128)(2,1)S(1)} %convolution_convert_fusion.10), channel_id=1, replica_groups=mesh['ctx'=16,'head'=2] {'ctx'}, dimensions={0}, use_global_device_ids=true | all-gather | bytes 835584 | tf_op jit(solution)/shard_map/all_gather | solution.py:287
  227.0 40.1 %all_gather.55 = bf16[768,384]{1,0:T(8,128)(2,1)S(1)} all-gather(bf16[48,384]{1,0:T(8,128)(2,1)S(1)} %copy-done.73), channel_id=1, replica_groups=mesh['ctx'=16,'head'=2] {'ctx'}, dimensions={0}, use_global_device_ids=true | all-gather | bytes 626688 | tf_op jit(solution)/shard_map/all_gather | solution.py:214
  268.1 41.8 %all_gather.56 = bf16[1024,384]{1,0:T(8,128)(2,1)S(1)} all-gather(bf16[64,384]{1,0:T(8,128)(2,1)S(1)} %convolution_convert_fusion.11), channel_id=1, replica_groups=mesh['ctx'=16,'head'=2] {'ctx'}, dimensions={0}, use_global_device_ids=true | all-gather | bytes 835584 | tf_op jit(solution)/shard_map/all_gather | solution.py:286
  312.7 42.0 %all_gather.54 = bf16[384,768]{0,1:T(8,128)(2,1)} all-gather(bf16[384,48]{0,1:T(8,128)(2,1)S(1)} %copy-done.74), channel_id=1, replica_groups=mesh['ctx'=16,'head'=2] {'ctx'}, dimensions={1}, use_global_device_ids=true | all-gather | bytes 626688 | tf_op jit(solution)/shard_map/all_gather | solution.py:212
  354.7 41.9 %all_gather.57 = bf16[768,384]{1,0:T(8,128)(2,1)} all-gather(bf16[48,384]{1,0:T(8,128)(2,1)S(1)} %copy-done.75), channel_id=1, replica_groups=mesh['ctx'=16,'head'=2] {'ctx'}, dimensions={0}, use_global_device_ids=true | all-gather | bytes 626688 | tf_op jit(solution)/shard_map/all_gather | solution.py:213
  401.9 45.4 %while.68 = (s32[]{:T(128)}, f32[6,128,64]{1,2,0:T(8,128)}, f32[6,128]{1,0:T(8,128)S(1)}, f32[6,128]{1,0:T(8,128)S(1)}, s32[16]{0:T(128)S(1)}, /*index=5*/bf16[2...) while((s32[]{:T(128)}, f32[6,128,64]{1,2,0:T(8,128)}, ...), condition=%wide.region_7.8_spmd.clone, body=%wide.region_3.7_spmd.clone.sunk | while | flops 252504448 | bytes 16679691 | solution.py:119
  414.9 4.0 fusion.246
  437.6 4.0 fusion.246
  451.1 39.7 %all_gather.60 = bf16[384,768]{0,1:T(8,128)(2,1)S(1)} all-gather(bf16[384,48]{0,1:T(8,128)(2,1)S(1)} %copy-done.76), channel_id=1, replica_groups=mesh['ctx'=16,'head'=2] {'ctx'}, dimensions={1}, use_global_device_ids=true | all-gather | bytes 626688 | tf_op jit(solution)/shard_map/all_gather | solution.py:216
  492.6 4.6 while.69
  500.6 12.6 all-reduce.11.cloned.1.call-done
  514.4 60.6 %all-gather.12.cloned.1.call-done = bf16[768,1024]{1,0:T(8,128)(2,1)} async-done(((bf16[48,1024]{1,0:T(8,128)(2,1)}), bf16[768,1024]{1,0:T(8,128)(2,1)}) %all-gather.12.cloned.1.call-update) | async-done | bytes 1572880 | tf_op jit(solution)/shard_map/all_gather | solution.py:218
  576.8 57.5 %all-gather.10.cloned.1.call-done = bf16[768,1024]{1,0:T(8,128)(2,1)} async-done(((bf16[48,1024]{1,0:T(8,128)(2,1)}), bf16[768,1024]{1,0:T(8,128)(2,1)}) %all-gather.10.cloned.1.call-update) | async-done | bytes 1572880 | tf_op jit(solution)/shard_map/all_gather | solution.py:217
  636.2 57.7 %all-gather.14.cloned.1.call-done = bf16[1024,768]{0,1:T(8,128)(2,1)} async-done(((bf16[1024,48]{0,1:T(8,128)(2,1)}), bf16[1024,768]{0,1:T(8,128)(2,1)}) %all-gather.14.cloned.1.call-update) | async-done | bytes 1572880 | tf_op jit(solution)/shard_map/all_gather | solution.py:219
  699.8 16.9 all-reduce.13.cloned.1.call-done
  719.6 13.2 while.70
  735.6 18.8 all-reduce.15.cloned.1.call-done
  757.3 121.5 %while.71 = (s32[]{:T(128)}, f32[128,6,64]{0,2,1:T(8,128)}, f32[32,6]{0,1:T(8,128)S(1)}, f32[4,512,768]{2,1,0:T(8,128)}, s32[4]{0:T(128)S(1)}, /*index=5*/bf16[2...) while((s32[]{:T(128)}, f32[128,6,64]{0,2,1:T(8,128)}, ...), condition=%wide.region_28.29_spmd.clone, body=%wide.region_25.28_spmd.clone.sunk | while | flops 552934784 | bytes 47343756 | solution.py:178
  762.3 6.3 copy.192
  768.6 5.3 fusion.283
  780.2 4.2 fusion.287
  792.7 6.3 copy.192
  799.0 5.3 fusion.283
  810.6 4.2 fusion.287
  823.1 6.3 copy.192
  829.4 5.3 fusion.283
  841.0 4.2 fusion.287
  853.5 6.3 copy.192
  859.8 5.3 fusion.283
  871.3 4.2 fusion.287
  883.6 9.1 reduce-scatter.20.cloned.1.call-done
  895.0 149.1 %reduce-scatter.18.cloned.1.call-done = f32[128,768]{1,0:T(8,128)} async-done(((f32[2048,768]{1,0:T(8,128)}), f32[128,768]{1,0:T(8,128)}) %reduce-scatter.18.cloned.1.call-update) | async-done | bytes 393232 | tf_op jit(solution)/shard_map/reduce_scatter | solution.py:360
  1071.7 75.2 %all-reduce.1 = (f32[3,768]{1,0:T(4,128)}, f32[32,6]{0,1:T(8,128)}) all-reduce(f32[3,768]{1,0:T(4,128)S(1)} %pad_maximum_fusion, f32[32,6]{0,1:T(8,128)S(1)} %get-tuple-element.710), channel_id=1, replica_groups=mesh['ctx'=16,'head'=2] {'ctx'}, use_global_device_ids=true, to_apply=%region_48.49 | all-reduce | flops 2496 | bytes 19968 | tf_op jit(solution)/shard_map/psum | solution.py:387
  1148.9 47.6 %reduce-scatter.32.cloned.1.call-done = f32[384,48]{0,1:T(8,128)} async-done(((f32[384,768]{0,1:T(8,128)}), f32[384,48]{0,1:T(8,128)}) %reduce-scatter.32.cloned.1.call-update) | async-done | bytes 73744 | tf_op jit(solution)/shard_map/reduce_scatter | solution.py:382
  1196.5 129.2 %reduce-scatter.30.cloned.1.call-done = f32[48,384]{1,0:T(8,128)} async-done(((f32[768,384]{1,0:T(8,128)}), f32[48,384]{1,0:T(8,128)}) %reduce-scatter.30.cloned.1.call-update) | async-done | bytes 73744 | tf_op jit(solution)/shard_map/reduce_scatter | solution.py:379
  1325.7 129.1 %reduce-scatter.28.cloned.1.call-done = f32[384,48]{0,1:T(8,128)} async-done(((f32[384,768]{0,1:T(8,128)}), f32[384,48]{0,1:T(8,128)}) %reduce-scatter.28.cloned.1.call-update) | async-done | bytes 73744 | tf_op jit(solution)/shard_map/reduce_scatter | solution.py:378
  1454.8 129.2 %reduce-scatter.22.cloned.1.call-done = f32[48,384]{1,0:T(8,128)} async-done(((f32[768,384]{1,0:T(8,128)}), f32[48,384]{1,0:T(8,128)}) %reduce-scatter.22.cloned.1.call-update) | async-done | bytes 73744 | tf_op jit(solution)/shard_map/reduce_scatter | solution.py:375
  1584.0 136.5 %reduce-scatter.38.cloned.1.call-done = f32[1024,48]{0,1:T(8,128)} async-done(((f32[1024,768]{0,1:T(8,128)}), f32[1024,48]{0,1:T(8,128)}) %reduce-scatter.38.cloned.1.call-update) | async-done | bytes 196624 | tf_op jit(solution)/shard_map/reduce_scatter | solution.py:385
  1720.5 136.5 %reduce-scatter.36.cloned.1.call-done = f32[48,1024]{1,0:T(8,128)} async-done(((f32[768,1024]{1,0:T(8,128)}), f32[48,1024]{1,0:T(8,128)}) %reduce-scatter.36.cloned.1.call-update) | async-done | bytes 196624 | tf_op jit(solution)/shard_map/reduce_scatter | solution.py:384
  1857.0 136.5 %reduce-scatter.34.cloned.1.call-done = f32[48,1024]{1,0:T(8,128)} async-done(((f32[768,1024]{1,0:T(8,128)}), f32[48,1024]{1,0:T(8,128)}) %reduce-scatter.34.cloned.1.call-update) | async-done | bytes 196624 | tf_op jit(solution)/shard_map/reduce_scatter | solution.py:383
  1993.5 129.0 %reduce-scatter.40.cloned.1.call-done = f32[48,384]{1,0:T(8,128)} async-done(((f32[768,384]{1,0:T(8,128)}), f32[48,384]{1,0:T(8,128)}) %reduce-scatter.40.cloned.1.call-update) | async-done | bytes 73744
  2122.5 129.4 %reduce-scatter.42.cloned.1.call-done = f32[48,384]{1,0:T(8,128)} async-done(((f32[768,384]{1,0:T(8,128)}), f32[48,384]{1,0:T(8,128)}) %reduce-scatter.42.cloned.1.call-update) | async-done | bytes 73744
  2251.9 129.3 %reduce-scatter.24.cloned.1.call-done = f32[48,384]{1,0:T(8,128)} async-done(((f32[768,384]{1,0:T(8,128)}), f32[48,384]{1,0:T(8,128)}) %reduce-scatter.24.cloned.1.call-update) | async-done | bytes 73744 | tf_op jit(solution)/shard_map/reduce_scatter | solution.py:376
  2381.2 129.3 %reduce-scatter.26.cloned.1.call-done = f32[48,384]{1,0:T(8,128)} async-done(((f32[768,384]{1,0:T(8,128)}), f32[48,384]{1,0:T(8,128)}) %reduce-scatter.26.cloned.1.call-update) | async-done | bytes 73744 | tf_op jit(solution)/shard_map/reduce_scatter | solution.py:377
  (562 shorter events, 190.6 us)
Async XLA Ops:
  7.2 177.5 %copy-start = (bf16[64,768]{1,0:T(8,128)(2,1)S(1)}, bf16[64,768]{1,0:T(8,128)(2,1)}, u32[]{:S(2)}) copy-start(bf16[64,768]{1,0:T(8,128)(2,1)} %param.27) | copy-start | bytes 294916
  7.2 50.3 %copy-start.70 = (bf16[48,384]{1,0:T(8,128)(2,1)S(1)}, bf16[48,384]{1,0:T(8,128)(2,1)}, u32[]{:S(2)}) copy-start(bf16[48,384]{1,0:T(8,128)(2,1)} %param.30) | copy-start | bytes 110596
  7.2 389.4 %all-gather.6.cloned.1.call-start = ((), (), s32[]{:S(2)}) async-start(), calls=%async_computation.13 | async-start | bytes 1671168 | tf_op jit(solution)/shard_map/all_gather | solution.py:273
  8.4 46.8 %copy-start.81 = (f32[128]{0:T(128)}, f32[128]{0:T(128)S(1)}, u32[]{:S(2)}) copy-start(f32[128]{0:T(128)S(1)} %multiply_reduce_fusion.2) | copy-start | bytes 1540
  8.4 91.4 %copy-start.79 = (f32[128]{0:T(128)}, f32[128]{0:T(128)S(1)}, u32[]{:S(2)}) copy-start(f32[128]{0:T(128)S(1)} %fusion.100) | copy-start | bytes 1540
  9.2 90.5 %copy-start.67 = (f32[768]{0:T(1024)}, f32[768]{0:T(1024)S(1)}, u32[]{:S(2)}) copy-start(f32[768]{0:T(1024)S(1)} %get-tuple-element.1119) | copy-start | bytes 9220
  55.2 44.7 %copy-start.71 = (bf16[48,384]{1,0:T(8,128)(2,1)S(1)}, bf16[48,384]{1,0:T(8,128)(2,1)}, u32[]{:S(2)}) copy-start(bf16[48,384]{1,0:T(8,128)(2,1)} %param.28) | copy-start | bytes 110596
  56.5 85.7 %copy-start.16 = (bf16[128,768]{1,0:T(8,128)(2,1)}, bf16[128,768]{1,0:T(8,128)(2,1)S(1)}, u32[]{:S(2)}) copy-start(bf16[128,768]{1,0:T(8,128)(2,1)S(1)} %multiply_convert_fusion.5) | copy-start | bytes 589828
  57.5 85.6 %copy-start.77 = (f32[32,6]{0,1:T(8,128)S(1)}, f32[32,6]{0,1:T(8,128)}, u32[]{:S(2)}) copy-start(f32[32,6]{0,1:T(8,128)} %param.40) | copy-start | bytes 2308
  57.5 85.8 %copy-start.72 = (bf16[48,384]{1,0:T(8,128)(2,1)S(1)}, bf16[48,384]{1,0:T(8,128)(2,1)}, u32[]{:S(2)}) copy-start(bf16[48,384]{1,0:T(8,128)(2,1)} %param.34) | copy-start | bytes 110596
  57.5 341.8 %all-gather.8.cloned.1.call-start = ((), (), s32[]{:S(2)}) async-start(), calls=%async_computation.14 | async-start | bytes 1671168 | tf_op jit(solution)/shard_map/all_gather | solution.py:274
  99.8 391.0 %all-reduce.9.cloned.1.call-start = ((), (), s32[]{:S(2)}) async-start(), calls=%async_computation.15 | async-start | bytes 393216 | tf_op jit(solution)/shard_map/psum | solution.py:46
  184.7 42.3 %copy-start.73 = (bf16[48,384]{1,0:T(8,128)(2,1)S(1)}, bf16[48,384]{1,0:T(8,128)(2,1)}, u32[]{:S(2)}) copy-start(bf16[48,384]{1,0:T(8,128)(2,1)} %param.33) | copy-start | bytes 110596
  267.9 43.2 %copy-start.69 = (s32[16]{0:T(128)S(1)}, s32[16]{0:T(128)}, u32[]{:S(2)}) copy-start(s32[16]{0:T(128)} %param.42) | copy-start | bytes 196
  267.9 44.5 %copy-start.78 = (s32[2048]{0:T(1024)S(1)}, s32[2048]{0:T(1024)}, u32[]{:S(2)}) copy-start(s32[2048]{0:T(1024)} %param.41) | copy-start | bytes 24580
  267.9 44.8 %copy-start.74 = (bf16[384,48]{0,1:T(8,128)(2,1)S(1)}, bf16[384,48]{0,1:T(8,128)(2,1)}, u32[]{:S(2)}) copy-start(bf16[384,48]{0,1:T(8,128)(2,1)} %param.31) | copy-start | bytes 110596
  268.1 86.6 %copy-start.75 = (bf16[48,384]{1,0:T(8,128)(2,1)S(1)}, bf16[48,384]{1,0:T(8,128)(2,1)}, u32[]{:S(2)}) copy-start(bf16[48,384]{1,0:T(8,128)(2,1)} %param.32) | copy-start | bytes 110596
  401.9 49.2 %copy-start.76 = (bf16[384,48]{0,1:T(8,128)(2,1)S(1)}, bf16[384,48]{0,1:T(8,128)(2,1)}, u32[]{:S(2)}) copy-start(bf16[384,48]{0,1:T(8,128)(2,1)} %param.35) | copy-start | bytes 110596
  447.3 43.5 %copy-start.12 = (f32[128,768]{1,0:T(8,128)S(1)}, f32[128,768]{1,0:T(8,128)}, u32[]{:S(2)}) copy-start(f32[128,768]{1,0:T(8,128)} %param.26) | copy-start | bytes 1179652
  447.3 44.8 %copy-start.47 = (bf16[768,384]{1,0:T(8,128)(2,1)S(1)}, bf16[768,384]{1,0:T(8,128)(2,1)}, u32[]{:S(2)}) copy-start(bf16[768,384]{1,0:T(8,128)(2,1)} %all_gather.57) | copy-start | bytes 1769476
  451.0 41.5 %copy-start.18 = (f32[6,128,64]{1,2,0:T(8,128)S(1)}, f32[6,128,64]{1,2,0:T(8,128)}, u32[]{:S(2)}) copy-start(f32[6,128,64]{1,2,0:T(8,128)} %custom-call.3) | copy-start | bytes 589828
  451.1 62.2 %all-reduce.11.cloned.1.call-start = ((), (), s32[]{:S(2)}) async-start(), calls=%async_computation.16 | async-start | bytes 393216 | tf_op jit(solution)/shard_map/psum | solution.py:46
  498.3 76.8 %all-gather.12.cloned.1.call-start = ((), (), s32[]{:S(2)}) async-start(), calls=%async_computation.18 | async-start | bytes 1671168 | tf_op jit(solution)/shard_map/all_gather | solution.py:218
  498.9 135.5 %all-gather.10.cloned.1.call-start = ((), (), s32[]{:S(2)}) async-start(), calls=%async_computation.17 | async-start | bytes 1671168 | tf_op jit(solution)/shard_map/all_gather | solution.py:217
  499.4 194.4 %all-gather.14.cloned.1.call-start = ((), (), s32[]{:S(2)}) async-start(), calls=%async_computation.19 | async-start | bytes 1671168 | tf_op jit(solution)/shard_map/all_gather | solution.py:219
  500.2 216.4 %all-reduce.13.cloned.1.call-start = ((), (), s32[]{:S(2)}) async-start(), calls=%async_computation.20 | async-start | bytes 393216 | tf_op jit(solution)/shard_map/psum | solution.py:46
  514.3 203.5 %copy-start.14 = (f32[128,768]{1,0:T(8,128)}, f32[128,768]{1,0:T(8,128)S(1)}, u32[]{:S(2)}) copy-start(f32[128,768]{1,0:T(8,128)S(1)} %get-tuple-element.1221) | copy-start | bytes 1179652
  514.4 121.7 %copy-start.48 = (bf16[128,768]{1,0:T(8,128)(2,1)}, bf16[128,768]{1,0:T(8,128)(2,1)S(1)}, u32[]{:S(2)}) copy-start(bf16[128,768]{1,0:T(8,128)(2,1)S(1)} %multiply_convert_fusion.3) | copy-start | bytes 589828
  576.8 117.0 %copy-start.50 = (f32[128,768]{1,0:T(8,128)S(1)}, f32[128,768]{1,0:T(8,128)}, u32[]{:S(2)}) copy-start(f32[128,768]{1,0:T(8,128)} %param.43) | copy-start | bytes 1179652
  699.7 54.7 %all-reduce.15.cloned.1.call-start = ((), (), s32[]{:S(2)}) async-start(), calls=%async_computation.21 | async-start | bytes 393216 | tf_op jit(solution)/shard_map/psum | solution.py:46
  734.9 157.8 %reduce-scatter.20.cloned.1.call-start = ((), (), s32[]{:S(2)}) async-start(), calls=%async_computation.23 | async-start | bytes 3342336 | tf_op jit(solution)/shard_map/reduce_scatter | solution.py:329
  735.6 308.5 %reduce-scatter.18.cloned.1.call-start = ((), (), s32[]{:S(2)}) async-start(), calls=%async_computation.22 | async-start | bytes 6684672 | tf_op jit(solution)/shard_map/reduce_scatter | solution.py:360
  878.9 190.1 %all-reduce.17.cloned.1.call-start = ((), (), s32[]{:S(2)}) async-start(), calls=%async_computation.35 | async-start | bytes 983040 | tf_op jit(solution)/shard_map/psum | solution.py:46
  883.6 161.4 %copy-start.46 = (bf16[768,384]{1,0:T(8,128)(2,1)S(1)}, bf16[768,384]{1,0:T(8,128)(2,1)}, u32[]{:S(2)}) copy-start(bf16[768,384]{1,0:T(8,128)(2,1)} %copy-done.45) | copy-start | bytes 1769476
  894.0 151.4 %copy-start.35 = (bf16[768,384]{1,0:T(8,128)(2,1)S(1)}, bf16[768,384]{1,0:T(8,128)(2,1)}, u32[]{:S(2)}) copy-start(bf16[768,384]{1,0:T(8,128)(2,1)} %copy-done.34) | copy-start | bytes 1769476
  1046.5 150.1 %reduce-scatter.32.cloned.1.call-start = ((), (), s32[]{:S(2)}) async-start(), calls=%async_computation.29 | async-start | bytes 1253376 | tf_op jit(solution)/shard_map/reduce_scatter | solution.py:382
  1048.0 277.7 %reduce-scatter.30.cloned.1.call-start = ((), (), s32[]{:S(2)}) async-start(), calls=%async_computation.28 | async-start | bytes 1253376 | tf_op jit(solution)/shard_map/reduce_scatter | solution.py:379
  1049.5 405.2 %reduce-scatter.28.cloned.1.call-start = ((), (), s32[]{:S(2)}) async-start(), calls=%async_computation.27 | async-start | bytes 1253376 | tf_op jit(solution)/shard_map/reduce_scatter | solution.py:378
  1051.0 533.0 %reduce-scatter.22.cloned.1.call-start = ((), (), s32[]{:S(2)}) async-start(), calls=%async_computation.24 | async-start | bytes 1253376 | tf_op jit(solution)/shard_map/reduce_scatter | solution.py:375
  1052.5 668.0 %reduce-scatter.38.cloned.1.call-start = ((), (), s32[]{:S(2)}) async-start(), calls=%async_computation.32 | async-start | bytes 3342336 | tf_op jit(solution)/shard_map/reduce_scatter | solution.py:385
  1054.9 802.0 %reduce-scatter.36.cloned.1.call-start = ((), (), s32[]{:S(2)}) async-start(), calls=%async_computation.31 | async-start | bytes 3342336 | tf_op jit(solution)/shard_map/reduce_scatter | solution.py:384
  1058.3 935.2 %reduce-scatter.34.cloned.1.call-start = ((), (), s32[]{:S(2)}) async-start(), calls=%async_computation.30 | async-start | bytes 3342336 | tf_op jit(solution)/shard_map/reduce_scatter | solution.py:383
  1061.5 1061.0 %reduce-scatter.40.cloned.1.call-start = ((), (), s32[]{:S(2)}) async-start(), calls=%async_computation.33 | async-start | bytes 1253376
  1064.1 1187.7 %reduce-scatter.42.cloned.1.call-start = ((), (), s32[]{:S(2)}) async-start(), calls=%async_computation.34 | async-start | bytes 1253376
  1066.0 1315.2 %reduce-scatter.24.cloned.1.call-start = ((), (), s32[]{:S(2)}) async-start(), calls=%async_computation.25 | async-start | bytes 1253376 | tf_op jit(solution)/shard_map/reduce_scatter | solution.py:376
  1067.4 79.4 %copy-start.82 = (f32[128]{0:T(128)S(1)}, f32[128]{0:T(128)}, u32[]{:S(2)}) copy-start(f32[128]{0:T(128)} %copy-done.81) | copy-start | bytes 1540
  1067.4 79.4 %copy-start.15 = (f32[128,768]{1,0:T(8,128)S(1)}, f32[128,768]{1,0:T(8,128)}, u32[]{:S(2)}) copy-start(f32[128,768]{1,0:T(8,128)} %copy-done.14) | copy-start | bytes 1179652
  1067.4 1443.1 %reduce-scatter.26.cloned.1.call-start = ((), (), s32[]{:S(2)}) async-start(), calls=%async_computation.26 | async-start | bytes 1253376 | tf_op jit(solution)/shard_map/reduce_scatter | solution.py:377
  (92 other events, 291.7 us)
Sparse Core Ops, SparseCore 0:
  57.6 55.5 all-gather.5
  116.5 59.7 all-gather.7
  451.2 14.8 all-reduce.8
  498.4 14.7 all-reduce.10
  515.8 59.1 all-gather.11
  577.7 56.6 all-gather.9
  637.1 56.6 all-gather.13
  699.8 16.7 all-reduce.12
  735.1 19.2 all-reduce.14
  759.2 133.4 reduce-scatter.19
  898.0 146.0 reduce-scatter.17
  1047.0 17.8 all-reduce.16
  1070.2 126.2 reduce-scatter.31
  1201.7 123.9 reduce-scatter.29
  1330.8 123.9 reduce-scatter.27
  1460.0 123.9 reduce-scatter.21
  1589.4 131.0 reduce-scatter.37
  1725.9 131.0 reduce-scatter.35
  1862.5 130.9 reduce-scatter.33
  1998.7 123.7 reduce-scatter.39
  2127.8 123.9 reduce-scatter.41
  2257.2 123.9 reduce-scatter.23
  2386.5 123.9 reduce-scatter.25
where the time goes:
time: 2530 us; the launch traced here: 2520 us
  waiting for transfers between devices  1750 us (69%)
  blocking collectives  491 us (19%)
  matrix products  126 us (5%)
  local copies, waits for them, and re-layouts  103 us (4%)
  other arithmetic  28.6 us (1%)
    unnamed x25, waiting for transfers between devices  261 us
    reduce_scatter x1, waiting for transfers between devices, per_device(): lax.psum_scatter(self_terms, 'ctx', scatter_dimension=0, tiled=True)  149 us
    reduce_scatter x1, waiting for transfers between devices, per_device(): lax.psum_scatter(gate_wgrad, 'ctx', scatter_dimension=0, tiled=True)  137 us
    reduce_scatter x1, waiting for transfers between devices, per_device(): lax.psum_scatter(down_wgrad, 'ctx', scatter_dimension=1, tiled=True)  137 us
    reduce_scatter x1, waiting for transfers between devices, per_device(): lax.psum_scatter(up_wgrad, 'ctx', scatter_dimension=0, tiled=True)  136 us
    reduce_scatter x1, waiting for transfers between devices, per_device(): lax.psum_scatter(value_wgrad, 'ctx', scatter_dimension=0, tiled=True)  129 us
    reduce_scatter x1, waiting for transfers between devices, per_device(): lax.psum_scatter(key_wgrad, 'ctx', scatter_dimension=0, tiled=True)  129 us
    reduce_scatter x1, waiting for transfers between devices, per_device(): lax.psum_scatter(query_wgrad, 'ctx', scatter_dimension=0, tiled=True)  129 us
  transfers between devices with their start and end apart: 23, of which 19 were waited for; matrix products, arithmetic and copies ran while one was open for 6% of the time, Pallas kernels for 0%

commit v1 on v0

--- a/solution.py
+++ b/solution.py
@@ -1,13 +1,1050 @@
+import functools
 import math
 
 import jax
 import jax.numpy as jnp
 from jax import lax
+from jax.experimental import pallas as pl
+from jax.experimental.pallas import tpu as pltpu
 from jax.sharding import PartitionSpec as P
 
 EPS = 1e-06
 NEG = -1e30
 HIGH = lax.Precision.HIGHEST
+LOW = jnp.bfloat16
+F32 = jnp.float32
+MESH = pl.DeviceIdType.MESH
+VMEM_LIMIT = 66_000_000
+
+
+def dot(left, right, **kw):
+    return jnp.dot(left, right, preferred_element_type=F32, **kw)
+
+
+def dot_nt(left, right, **kw):
+    return lax.dot_general(left, right, (((1,), (1,)), ((), ())), preferred_element_type=F32, **kw)
+
+
+def dot_tn(left, right, **kw):
+    return lax.dot_general(left, right, (((0,), (0,)), ((), ())), preferred_element_type=F32, **kw)
+
+
+def rms_forward(rows, gain):
+    return rows * lax.rsqrt(jnp.mean(rows * rows, axis=-1, keepdims=True) + EPS) * gain
+
+
+def rms_backward(rows, gain, grad):
+    scale = lax.rsqrt(jnp.mean(rows * rows, axis=-1, keepdims=True) + EPS)
+    scaled = gain * grad
+    inner = jnp.mean(scaled * rows, axis=-1, keepdims=True)
+    row_grad = scale * scaled - rows * (scale * scale * scale * inner)
+    gain_grad = jnp.sum(grad * rows * scale, axis=0, keepdims=True)
+    return row_grad, gain_grad
+
+
+def aligned(value, step):
+    return value if isinstance(value, int) else pl.multiple_of(value, step)
+
+
+class Place:
+    def __init__(self, count):
+        self.count = count
+        self.here = lax.axis_index("ctx")
+        self.core = lax.axis_index("head")
+        self.other = 1 - self.core
+        self.plane = lax.rem(self.here, 4)
+        self.level = self.here // 4
+        self.fx = self.flip(self.here, 0)
+        self.fy = self.flip(self.here, 1)
+        self.fxy = self.flip(self.fx, 1)
+        self.above = [lax.rem(self.here + 4 * k, count) for k in range(4)]
+        self.below = [lax.rem(self.here + count - 4 * k, count) for k in range(4)]
+
+    def flip(self, index, axis):
+        if axis == 0:
+            return index + 1 - 2 * lax.rem(index, 2)
+        return index + 2 - 4 * lax.rem(index // 2, 2)
+
+    def near(self, half):
+        return (self.fx, self.fy) if half == 0 else (self.fy, self.fx)
+
+    def greet(self, chips, partner):
+        barrier = pltpu.get_barrier_semaphore()
+        total = len(chips) + (1 if partner else 0)
+        for chip in chips:
+            pl.semaphore_signal(
+                barrier, inc=1, device_id=(chip, self.core), device_id_type=MESH
+            )
+        if partner:
+            pl.semaphore_signal(
+                barrier, inc=1, device_id=(self.here, self.other), device_id_type=MESH
+            )
+        pl.semaphore_wait(barrier, total)
+
+
+class Wire:
+    def __init__(self, place, send_sem, recv_sem):
+        self.place, self.send_sem, self.recv_sem = place, send_sem, recv_sem
+        self.sent = []
+        self.used = 0
+
+    def slots(self, count):
+        base = self.used
+        self.used += count
+        assert self.used <= self.send_sem.shape[0], self.used
+        return base
+
+    def copy(self, src, dst, slot, chip, core):
+        return pltpu.make_async_remote_copy(
+            src_ref=src,
+            dst_ref=dst,
+            send_sem=self.send_sem.at[slot],
+            recv_sem=self.recv_sem.at[slot],
+            device_id=(chip, core),
+            device_id_type=MESH,
+        )
+
+    def send(self, src, dst, slot, chip=None, core=None):
+        chip = self.place.here if chip is None else chip
+        core = self.place.core if core is None else core
+        made = self.copy(src, dst, slot, chip, core)
+        made.start()
+        self.sent.append(made)
+
+    def swap(self, src, dst, slot):
+        self.send(src, dst, slot, None, self.place.other)
+
+    def got(self, dst, slot):
+        place = self.place
+        self.copy(dst, dst, slot, place.here, place.other).wait_recv()
+
+    def drain(self):
+        for made in self.sent:
+            made.wait_send()
+        self.sent = []
+
+
+class Gather:
+    def __init__(self, wire, view, share, halves=2):
+        self.wire, self.view, self.share = wire, view, share
+        self.base = [wire.slots(15) for _ in range(halves)]
+        self.side = [wire.slots(16) for _ in range(halves)] if share else None
+        self.halves = range(halves)
+
+    def _out(self, half, block, slot, chip):
+        ref = self.view(half, block)
+        self.wire.send(ref, ref, self.base[half] + slot, chip)
+
+    def _in(self, half, block, slot):
+        self.wire.got(self.view(half, block), self.base[half] + slot)
+        if self.share:
+            ref = self.view(half, block)
+            self.wire.swap(ref, ref, self.side[half] + slot)
+
+    def start(self):
+        place = self.wire.place
+        for half in self.halves:
+            near, far = place.near(half)
+            for k in (1, 2, 3):
+                self._out(half, place.here, k - 1, place.above[k])
+            self._out(half, place.here, 3, near)
+            self._out(half, place.here, 7, far)
+
+    def pass_level(self):
+        place = self.wire.place
+        for k in (1, 2, 3):
+            for half in self.halves:
+                near, far = place.near(half)
+                self._in(half, place.below[k], k - 1)
+                self._out(half, place.below[k], 3 + k, near)
+                self._out(half, place.below[k], 7 + k, far)
+
+    def pass_near(self):
+        place = self.wire.place
+        for k in range(4):
+            for half in self.halves:
+                _, far = place.near(half)
+                block = place.flip(place.below[k], half)
+                self._in(half, block, 3 + k)
+                self._out(half, block, 11 + k, far)
+
+    def finish(self):
+        place = self.wire.place
+        for k in range(4):
+            for half in self.halves:
+                block = place.flip(place.below[k], 1 - half)
+                self._in(half, block, 7 + k)
+                self._in(half, place.flip(block, half), 11 + k)
+
+    def finish_share(self):
+        if not self.share:
+            return
+        place = self.wire.place
+        for k in range(4):
+            for half in self.halves:
+                block = place.below[k]
+                if k:
+                    self._share_in(half, block, k - 1)
+                self._share_in(half, place.flip(block, half), 3 + k)
+                block = place.flip(block, 1 - half)
+                self._share_in(half, block, 7 + k)
+                self._share_in(half, place.flip(block, half), 11 + k)
+
+    def _share_in(self, half, block, slot):
+        self.wire.got(self.share(half, block), self.side[half] + slot)
+
+
+class Scatter:
+    def __init__(self, wire, view, buf, out, halves=2):
+        self.wire, self.view, self.out = wire, view, out
+        self.far_buf = lambda half, slot: buf.at[half, slot]
+        self.near_buf = lambda half, slot: buf.at[half, 8 + slot]
+        self.level_buf = lambda half, slot: buf.at[half, 12 + slot]
+        self.base = [wire.slots(15) for _ in range(halves)]
+        self.halves = range(halves)
+
+    def start(self, ready=None):
+        place = self.wire.place
+        for k in (1, 2, 3, 0):
+            if ready is not None:
+                ready(k)
+            for half in self.halves:
+                _, far = place.near(half)
+                away = place.flip(place.below[k], 1 - half)
+                for pair, block in ((1, place.flip(away, half)), (0, away)):
+                    slot = 2 * k + pair
+                    self.wire.send(
+                        self.view(half, block),
+                        self.far_buf(half, slot),
+                        self.base[half] + slot,
+                        far,
+                    )
+
+    def pass_near(self):
+        place = self.wire.place
+        for k in (1, 2, 3, 0):
+            for half in self.halves:
+                near, _ = place.near(half)
+                block = place.flip(place.below[k], half)
+                slot = 2 * k + 1
+                self.wire.got(self.far_buf(half, slot), self.base[half] + slot)
+                ref = self.view(half, block)
+                ref[...] = (
+                    ref[...].astype(F32) + self.far_buf(half, slot)[...].astype(F32)
+                ).astype(LOW)
+                self.wire.send(ref, self.near_buf(half, k), self.base[half] + 8 + k, near)
+
+    def pass_level(self):
+        place = self.wire.place
+        for k in (1, 2, 3):
+            for half in self.halves:
+                self._add(half, k)
+                ref = self.view(half, place.below[k])
+                self.wire.send(
+                    ref, self.level_buf(half, k - 1), self.base[half] + 11 + k, place.below[k]
+                )
+
+    def _add(self, half, k):
+        place = self.wire.place
+        self.wire.got(self.far_buf(half, 2 * k), self.base[half] + 2 * k)
+        self.wire.got(self.near_buf(half, k), self.base[half] + 8 + k)
+        ref = self.view(half, place.below[k])
+        total = (
+            ref[...].astype(F32)
+            + self.far_buf(half, 2 * k)[...].astype(F32)
+            + self.near_buf(half, k)[...].astype(F32)
+        )
+        if k:
+            ref[...] = total.astype(LOW)
+        return total
+
+    def finish(self):
+        for half in self.halves:
+            total = self._add(half, 0)
+            for k in (1, 2, 3):
+                self.wire.got(self.level_buf(half, k - 1), self.base[half] + 11 + k)
+                total = total + self.level_buf(half, k - 1)[...].astype(F32)
+            self.out(half, total)
+
+
+def lane_split(rows):
+    lane = lax.broadcasted_iota(jnp.int32, rows.shape, 1)
+    low = lane < rows.shape[1] // 2
+    zero = jnp.zeros_like(rows)
+    return jnp.concatenate((jnp.where(low, rows, zero), jnp.where(low, zero, rows)), axis=0)
+
+
+def lane_join(rows):
+    count, width = rows.shape[0] // 2, rows.shape[1]
+    lane = lax.broadcasted_iota(jnp.int32, (count, width), 1)
+    return jnp.where(lane < width // 2, rows[:count], rows[count:])
+
+
+def pair_attend(tok, pairs, chunk, q_ref, kv_ref, s_ref, e_ref, rl_ref, mixed_ref, bias_ref):
+    keys = kv_ref.shape[0]
+    total = pairs * 128
+
+    def one_pair(j, carry):
+        cols = pl.ds(aligned(j * 128, 128), 128)
+        q_cat = lane_split(q_ref[:, cols])
+
+        def score(c, top):
+            rows = pl.ds(aligned(c * chunk, chunk), chunk)
+            s = dot_nt(q_cat, kv_ref[rows, cols])
+            if bias_ref is not None:
+                tiles = []
+                for half in range(2):
+                    row = []
+                    for b in range(chunk // tok):
+                        vec = bias_ref[c * (chunk // tok) + b, pl.ds(2 * j + half, 1), :]
+                        wide = jnp.broadcast_to(vec, (tok, 2 * tok))
+                        row.append(pltpu.roll(wide, 0, 1, stride=1, stride_axis=0)[:, :tok])
+                    tiles.append(jnp.concatenate(row, axis=1))
+                s = s + jnp.concatenate(tiles, axis=0)
+            s_ref[:, rows] = s
+            for b in range(chunk // 128):
+                top = jnp.maximum(top, s[:, b * 128 : (b + 1) * 128])
+            return top
+
+        top = lax.fori_loop(0, keys // chunk, score, jnp.full((2 * tok, 128), NEG, F32))
+        peak = jnp.max(top, axis=1, keepdims=True)
+
+        def weigh(c, state):
+            acc, run = state
+            rows = pl.ds(aligned(c * chunk, chunk), chunk)
+            e = jnp.exp(s_ref[:, rows] - peak)
+            for b in range(chunk // 128):
+                run = run + e[:, b * 128 : (b + 1) * 128]
+            low = e.astype(LOW)
+            e_ref[j, :, rows] = low
+            value = kv_ref[rows, pl.ds(aligned(total + j * 128, 128), 128)]
+            return (acc + dot(low, value), run)
+
+        zero = jnp.zeros((2 * tok, 128), F32)
+        acc, run = lax.fori_loop(0, keys // chunk, weigh, (zero, zero))
+        rl = 1.0 / jnp.sum(run, axis=1, keepdims=True)
+        rl_ref[j] = rl
+        mixed_ref[:, cols] = lane_join(acc * rl).astype(LOW)
+        return carry
+
+    lax.fori_loop(0, pairs, one_pair, 0)
+
+
+def pair_attend_back(
+    tok, pairs, chunk, q_ref, kv_ref, e_ref, rl_ref, mixed_ref, grad_ref, q_grad_ref, kv_grad_ref, diag_ref
+):
+    keys = kv_ref.shape[0]
+    total = pairs * 128
+    flip = (
+        lax.broadcasted_iota(jnp.int32, (tok, tok), 0)
+        + lax.broadcasted_iota(jnp.int32, (tok, tok), 1)
+        == tok - 1
+    ).astype(LOW)
+
+    def one_pair(j, carry):
+        cols = pl.ds(aligned(j * 128, 128), 128)
+        vcols = pl.ds(aligned(total + j * 128, 128), 128)
+        q_cat = lane_split(q_ref[:, cols])
+        rl = rl_ref[j]
+        grad = lane_split(grad_ref[:, cols].astype(F32))
+        mixed = lane_split(mixed_ref[:, cols].astype(F32))
+        grad_cat = (grad * rl).astype(LOW)
+        delta = jnp.sum(grad * mixed, axis=1, keepdims=True) * rl
+
+        def piece(c, q_grad):
+            rows = pl.ds(aligned(c * chunk, chunk), chunk)
+            low_e = e_ref[j, :, rows]
+            key = kv_ref[rows, cols]
+            dp = dot_nt(grad_cat, kv_ref[rows, vcols])
+            ds = (low_e.astype(F32) * (dp - delta)).astype(LOW)
+            if diag_ref is not None:
+                for half in range(2):
+                    turned = dot(flip, ds[half * tok : (half + 1) * tok])
+                    for b in range(chunk // tok):
+                        tile = turned[:, b * tok : (b + 1) * tok]
+                        wide = jnp.concatenate((tile, jnp.zeros_like(tile)), axis=1)
+                        wide = pltpu.roll(wide, tok + 1, 1, stride=1, stride_axis=0)
+                        diag_ref[c * (chunk // tok) + b, pl.ds(2 * j + half, 1), :] = jnp.sum(
+                            wide, axis=0, keepdims=True
+                        )
+            kv_grad_ref[rows, cols] = dot_tn(ds, q_cat).astype(LOW)
+            kv_grad_ref[rows, vcols] = dot_tn(low_e, grad_cat).astype(LOW)
+            return q_grad + dot(ds, key)
+
+        q_grad = lax.fori_loop(0, keys // chunk, piece, jnp.zeros((2 * tok, 128), F32))
+        q_grad_ref[:, cols] = lane_join(q_grad).astype(LOW)
+        return carry
+
+    lax.fori_loop(0, pairs, one_pair, 0)
+
+
+def bucket_masks(ids_ref, block, buckets):
+    ids = ids_ref[pl.ds(block, 1), :]
+    row = lax.broadcasted_iota(jnp.int32, (buckets, ids.shape[1]), 0)
+    return ids, (row == ids).astype(F32)
+
+
+def bias_vectors(ids_ref, table_ref, bias_ref):
+    def one(block, carry):
+        ids, mask = bucket_masks(ids_ref, block, table_ref.shape[1])
+        vec = dot(table_ref[...], mask, precision=HIGH)
+        bias_ref[block] = jnp.where(ids >= 0, vec, NEG)
+        return carry
+
+    lax.fori_loop(0, ids_ref.shape[0], one, 0)
+
+
+def bucket_sums(ids_ref, diag_ref, buckets):
+    def one(block, total):
+        _, mask = bucket_masks(ids_ref, block, buckets)
+        return total + dot_nt(diag_ref[block], mask, precision=HIGH)
+
+    start = jnp.zeros((diag_ref.shape[1], buckets), F32)
+    return lax.fori_loop(0, ids_ref.shape[0], one, start)
+
+
+def rows_loop(count, step, body):
+    def one(index, carry):
+        body(pl.ds(aligned(index * step, step), step))
+        return carry
+
+    lax.fori_loop(0, count // step, one, 0)
+
+
+GELU_A = 0.7978845608028654
+GELU_B = 0.044715
+
+
+def gelu_parts(value):
+    square = value * value
+    wave = jnp.tanh(GELU_A * (value + GELU_B * value * square))
+    half = 0.5 * (1.0 + wave)
+    slope = half + 0.5 * value * (1.0 - wave * wave) * (GELU_A * (1.0 + 3.0 * GELU_B * square))
+    return value * half, slope
+
+
+def core_sum(wire, part, out_buf, in_buf):
+    slot = wire.slots(1)
+    out_buf[...] = part.astype(LOW)
+    wire.swap(out_buf, in_buf, slot)
+    wire.got(in_buf, slot)
+    return out_buf[...].astype(F32) + in_buf[...].astype(F32)
+
+
+class PlaneSum:
+    def __init__(self, wire, tok, part, core_buf, plane_buf, whole):
+        self.wire, self.tok = wire, tok
+        self.part, self.core_buf, self.plane_buf, self.whole = part, core_buf, plane_buf, whole
+        self.base = wire.slots(8)
+        self.half = whole.shape[1] // 2
+
+    def cols(self, core):
+        return pl.ds(aligned(core * self.half, 128), self.half)
+
+    def start(self):
+        place, wire = self.wire.place, self.wire
+        away = self.cols(place.other)
+        for k, chip in ((1, place.fx), (2, place.fy), (3, place.fxy), (0, place.here)):
+            rows = pl.ds(aligned(lax.rem(chip, 4) * self.tok, self.tok), self.tok)
+            wire.swap(self.part.at[rows, away], self.core_buf.at[rows, :], self.base + k)
+
+    def middle(self):
+        place, wire = self.wire.place, self.wire
+        mine = self.cols(place.core)
+        for k, chip in ((1, place.fx), (2, place.fy), (3, place.fxy), (0, place.here)):
+            rows = pl.ds(aligned(lax.rem(chip, 4) * self.tok, self.tok), self.tok)
+            wire.got(self.core_buf.at[rows, :], self.base + k)
+            total = self.part[rows, mine].astype(F32) + self.core_buf[rows, :].astype(F32)
+            if k:
+                self.core_buf[rows, :] = total.astype(LOW)
+                wire.send(
+                    self.core_buf.at[rows, :], self.plane_buf.at[k - 1], self.base + 3 + k, chip
+                )
+            else:
+                self.own = total
+
+    def finish(self):
+        place, wire = self.wire.place, self.wire
+        total = self.own
+        for k in (1, 2, 3):
+            wire.got(self.plane_buf.at[k - 1], self.base + 3 + k)
+            total = total + self.plane_buf[k - 1].astype(F32)
+        mine = self.cols(place.core)
+        self.whole[:, mine] = total.astype(LOW)
+        slot = self.base + 7
+        wire.swap(self.whole.at[:, mine], self.whole.at[:, mine], slot)
+        wire.got(self.whole.at[:, self.cols(place.other)], slot)
+
+
+class PlaneGather:
+    def __init__(self, wire, tok, ref):
+        self.wire, self.tok, self.ref = wire, tok, ref
+        self.half = ref.shape[1] // 2
+        self.base = wire.slots(6)
+
+    def view(self, chip, core):
+        rows = pl.ds(aligned(lax.rem(chip, 4) * self.tok, self.tok), self.tok)
+        return self.ref.at[rows, pl.ds(aligned(core * self.half, 128), self.half)]
+
+    def start(self):
+        place = self.wire.place
+        own = self.view(place.here, place.core)
+        for k, chip in enumerate((place.fx, place.fy, place.fxy)):
+            self.wire.send(own, own, self.base + k, chip)
+
+    def share(self):
+        place = self.wire.place
+        for k, chip in enumerate((place.fx, place.fy, place.fxy)):
+            ref = self.view(chip, place.core)
+            self.wire.got(ref, self.base + k)
+            self.wire.swap(ref, ref, self.base + 3 + k)
+
+    def finish(self):
+        place = self.wire.place
+        for k, chip in enumerate((place.fx, place.fy, place.fxy)):
+            self.wire.got(self.view(chip, place.other), self.base + 3 + k)
+
+
+class Sizes:
+    def __init__(self, ctx, tok, enc, model, wide, units):
+        self.ctx, self.tok, self.enc, self.model, self.wide = ctx, tok, enc, model, wide
+        self.rows = model // ctx
+        self.quarter = units // 4
+        self.pairs = wide // 128
+        self.levels = ctx // 4
+        self.attn_cols = 8 * wide
+        self.mlp_cols = 3 * units
+        self.part = 3 * self.quarter
+        names = ("q", "k", "v", "o", "cq", "ck", "cv", "co")
+        self.col = {name: slice(i * wide, (i + 1) * wide) for i, name in enumerate(names)}
+        self.col["kv"] = slice(wide, 3 * wide)
+        self.col["ckv"] = slice(5 * wide, 7 * wide)
+
+
+def named(kernel, names):
+    def body(*refs):
+        kernel(**dict(zip(names, refs, strict=True)))
+
+    return body
+
+
+def call(kernel, size, ins, outs, scratch, collective_id, any_inputs=()):
+    names = list(ins) + list(outs) + list(scratch)
+    made = pl.pallas_call(
+        named(functools.partial(kernel, size), names),
+        out_shape=tuple(jax.ShapeDtypeStruct(*spec) for spec in outs.values()),
+        in_specs=[
+            pl.BlockSpec(memory_space=pl.ANY if name in any_inputs else pltpu.VMEM) for name in ins
+        ],
+        out_specs=tuple(pl.BlockSpec(memory_space=pltpu.VMEM) for _ in outs),
+        scratch_shapes=list(scratch.values()),
+        compiler_params=pltpu.CompilerParams(
+            collective_id=collective_id, has_side_effects=True, vmem_limit_bytes=VMEM_LIMIT
+        ),
+    )
+    return dict(zip(outs, made(*ins.values()), strict=True))
+
+
+def wire_sems(count):
+    return {
+        "send_sem": pltpu.SemaphoreType.DMA((count,)),
+        "recv_sem": pltpu.SemaphoreType.DMA((count,)),
+    }
+
+
+def gather_kernel(
+    size, layer_in, encoded, gains, out_grad, wa, wm, WA, WM, X, E, GR, local, send_sem, recv_sem
+):
+    place = Place(size.ctx)
+    wire = Wire(place, send_sem, recv_sem)
+    chips = place.above[1:] + [place.fx, place.fy, place.fxy]
+    tok, enc, rows, half_d = size.tok, size.enc, size.rows, size.model // 2
+
+    def block_rows(block, count):
+        return pl.ds(aligned(block * count, 16), count)
+
+    place.greet(chips, True)
+    X[block_rows(place.here, tok), :] = rms_forward(layer_in[...], gains[0:1]).astype(LOW)
+    E[block_rows(place.here, enc), :] = encoded[...]
+    GR[block_rows(place.plane, tok), :] = out_grad[...].astype(LOW)
+    copies = (
+        pltpu.make_async_copy(wa, WA.at[block_rows(place.here, rows), :], local.at[0]),
+        pltpu.make_async_copy(
+            wm.at[:, pl.ds(aligned(place.plane * size.part, 128), size.part)],
+            WM.at[block_rows(place.here, rows), :],
+            local.at[1],
+        ),
+    )
+    for made in copies:
+        made.start()
+
+    def token_view(ref, count, core):
+        def view(half, block):
+            return ref.at[
+                pl.ds(aligned(block * count + half * (count // 2), 16), count // 2),
+                pl.ds(aligned(core * half_d, 128), half_d),
+            ]
+
+        return view
+
+    def weight_view(first, last):
+        step = (last - first) // 2
+
+        def view(half, block):
+            return WA.at[
+                block_rows(block, rows), first + half * step : first + (half + 1) * step
+            ]
+
+        return view
+
+    gx = Gather(wire, token_view(X, tok, place.core), token_view(X, tok, place.other))
+    ge = Gather(wire, token_view(E, enc, place.core), token_view(E, enc, place.other))
+    gs = Gather(wire, weight_view(0, 4 * size.wide), None)
+    gc = Gather(wire, weight_view(4 * size.wide, 8 * size.wide), None)
+    gg = PlaneGather(wire, tok, GR)
+    plane_base, level_base = wire.slots(3), wire.slots(3)
+
+    gx.start()
+    ge.start()
+    for made in copies:
+        made.wait()
+    gs.start()
+    for k, chip in enumerate((place.fx, place.fy, place.fxy)):
+        wire.send(
+            wm.at[:, pl.ds(aligned(lax.rem(chip, 4) * size.part, 128), size.part)],
+            WM.at[block_rows(place.here, rows), :],
+            plane_base + k,
+            chip,
+        )
+    gx.pass_level()
+    ge.pass_level()
+    gx.pass_near()
+    gs.pass_level()
+    ge.pass_near()
+    gc.start()
+    for k, chip in enumerate((place.fx, place.fy, place.fxy)):
+        wire.got(WM.at[block_rows(chip, rows), :], plane_base + k)
+    own = WM.at[block_rows(place.level, 4 * rows), :]
+    for k in (1, 2, 3):
+        wire.send(own, own, level_base + k - 1, place.above[k])
+    gs.pass_near()
+    gx.finish()
+    ge.finish()
+    gc.pass_level()
+    gg.start()
+    gs.finish()
+    gc.pass_near()
+    gg.share()
+    gc.finish()
+    for k in (1, 2, 3):
+        level = place.below[k] // 4
+        wire.got(WM.at[block_rows(level, 4 * rows), :], level_base + k - 1)
+    gx.finish_share()
+    ge.finish_share()
+    gg.finish()
+    wire.drain()
+
+
+def compute_kernel(
+    size, layer_in, gains, out_grad, ids, table, WA, WM, X, E, GR,
+    layer_out, PW, PM, XG, EG, self_grad, SM,
+    q, kv, mkv, probes, s, e1, e2, rl1, rl2, mixed1, mixed2, bias, diag,
+    after_self, after_cross, cross_grad, n2, N3, act, GU, PN, PO, low, mixed_grad, q_grad,
+    kv_grad, mkv_grad, ca, cb, pn_core, pn_plane, pn_whole, po_core, po_plane, po_whole,
+    send_sem, recv_sem,
+):
+    place = Place(size.ctx)
+    wire = Wire(place, send_sem, recv_sem)
+    place.greet([place.fx, place.fy, place.fxy], True)
+    tok, col, model, wide = size.tok, size.col, size.model, size.wide
+    here_rows = pl.ds(aligned(place.here * tok, 16), tok)
+    ctx_tok, ctx_enc = X.shape[0], E.shape[0]
+    quarter = size.quarter
+
+    def project(rows):
+        kv[rows, :] = dot(X[rows, :], WA[:, col["kv"]]).astype(LOW)
+
+    def project_enc(rows):
+        mkv[rows, :] = dot(E[rows, :], WA[:, col["ckv"]]).astype(LOW)
+
+    bias_vectors(ids, table, bias)
+    diag[...] = jnp.zeros_like(diag)
+    q[...] = dot(X[here_rows, :], WA[:, col["q"]]).astype(LOW)
+    rows_loop(ctx_tok, 256, project)
+    pair_attend(tok, size.pairs, 512, q, kv, s, e1, rl1, mixed1, bias)
+    part = dot_nt(mixed1[...], WA[:, col["o"]])
+    after_self[...] = layer_in[...] + core_sum(wire, part, ca.at[0], cb.at[0])
+    n2[...] = rms_forward(after_self[...], gains[1:2]).astype(LOW)
+    rows_loop(ctx_enc, 256, project_enc)
+    probes[...] = dot(n2[...], WA[:, col["cq"]]).astype(LOW)
+    pair_attend(tok, size.pairs, 512, probes, mkv, s, e2, rl2, mixed2, None)
+    part = dot_nt(mixed2[...], WA[:, col["co"]])
+    after_cross[...] = after_self[...] + core_sum(wire, part, ca.at[1], cb.at[1])
+    spread = PlaneGather(wire, tok, N3)
+    plane_rows = pl.ds(aligned(place.plane * tok, 16), tok)
+    N3[plane_rows, :] = rms_forward(after_cross[...], gains[2:3]).astype(LOW)
+    spread.start()
+    spread.share()
+    spread.finish()
+
+    def units(rows):
+        pre = dot(N3[rows, :], WM[:, : 2 * quarter])
+        gate, upper = pre[:, :quarter], pre[:, quarter:]
+        value, slope = gelu_parts(gate)
+        act[rows, :] = (value * upper).astype(LOW)
+        grad = dot(GR[rows, :], WM[:, 2 * quarter :])
+        GU[rows, :quarter] = (grad * upper * slope).astype(LOW)
+        GU[rows, quarter:] = (grad * value).astype(LOW)
+        PN[rows, :] = dot_nt(GU[rows, :], WM[:, : 2 * quarter]).astype(LOW)
+
+    rows_loop(4 * tok, 128, units)
+    sum_n = PlaneSum(wire, tok, PN, pn_core, pn_plane, pn_whole)
+    sum_o = PlaneSum(wire, tok, PO, po_core, po_plane, po_whole)
+    sum_n.start()
+
+    def back_out(rows):
+        PO[rows, :] = dot_nt(act[rows, :], WM[:, 2 * quarter :]).astype(LOW)
+
+    rows_loop(4 * tok, 128, back_out)
+    sum_n.middle()
+    sum_o.start()
+
+    def unit_grads(cols):
+        PM[cols, : 2 * quarter] = dot_tn(N3[:, cols], GU[...]).astype(LOW)
+        PM[cols, 2 * quarter :] = dot_tn(GR[:, cols], act[...]).astype(LOW)
+
+    rows_loop(model, 128, unit_grads)
+    sum_n.finish()
+    sum_o.middle()
+    extra, gain_three = rms_backward(after_cross[...], gains[2:3], pn_whole[...].astype(F32))
+    cross_grad[...] = out_grad[...] + extra
+    low[...] = cross_grad[...].astype(LOW)
+    mixed_grad[...] = dot(low[...], WA[:, col["co"]]).astype(LOW)
+
+    def out_grads(left, right, target):
+        def body(cols):
+            PW[cols, target] = dot_tn(left[:, cols], right[...]).astype(LOW)
+
+        rows_loop(model, 128, body)
+
+    out_grads(low, mixed2, col["co"])
+    pair_attend_back(
+        tok, size.pairs, 512, probes, mkv, e2, rl2, mixed2, mixed_grad, q_grad, mkv_grad, None
+    )
+    part = dot_nt(q_grad[...], WA[:, col["cq"]])
+    slot = wire.slots(1)
+    ca[2] = part.astype(LOW)
+    wire.swap(ca.at[2], cb.at[2], slot)
+    out_grads(n2, q_grad, col["cq"])
+    out_grads(E, mkv_grad, col["ckv"])
+
+    def enc_rows(rows):
+        EG[rows, :] = dot_nt(mkv_grad[rows, :], WA[:, col["ckv"]]).astype(LOW)
+
+    rows_loop(ctx_enc, 256, enc_rows)
+    sum_o.finish()
+    layer_out[...] = after_cross[...] + po_whole[...].astype(F32)
+    wire.got(cb.at[2], slot)
+    n_grad = ca[2].astype(F32) + cb[2].astype(F32)
+    extra, gain_two = rms_backward(after_self[...], gains[1:2], n_grad)
+    self_grad[...] = cross_grad[...] + extra
+    low[...] = self_grad[...].astype(LOW)
+    mixed_grad[...] = dot(low[...], WA[:, col["o"]]).astype(LOW)
+    out_grads(low, mixed1, col["o"])
+    pair_attend_back(
+        tok, size.pairs, 512, q, kv, e1, rl1, mixed1, mixed_grad, q_grad, kv_grad, diag
+    )
+    n2[...] = X[here_rows, :]
+    out_grads(n2, q_grad, col["q"])
+    out_grads(X, kv_grad, col["kv"])
+
+    def tok_rows(rows):
+        XG[rows, :] = dot_nt(kv_grad[rows, :], WA[:, col["kv"]]).astype(LOW)
+
+    rows_loop(ctx_tok, 256, tok_rows)
+    own = dot_nt(q_grad[...], WA[:, col["q"]]) + XG[here_rows, :].astype(F32)
+    XG[here_rows, :] = own.astype(LOW)
+    sums = bucket_sums(ids, diag, table.shape[1])
+    SM[...] = jnp.zeros_like(SM)
+    SM[1:2, :] = gain_two
+    SM[2:3, :] = gain_three
+    SM[8:16, :128] = jnp.concatenate(
+        (sums, jnp.zeros((8, 128 - sums.shape[1]), F32)), axis=1
+    )
+    wire.drain()
+
+
+def scatter_kernel(
+    size, layer_in, gains, self_grad, pw, pm, xg, eg, SM,
+    WG, MG, input_grad, enc_grad, totals,
+    PW, PM, XG, EG, bs, bc, bx, be, px, pe, NG, NE, ml, ps, mb, s1, s2, sr, sl,
+    local, send_sem, recv_sem,
+):
+    place = Place(size.ctx)
+    wire = Wire(place, send_sem, recv_sem)
+    copies = [
+        pltpu.make_async_copy(src, dst, local.at[i])
+        for i, (src, dst) in enumerate(((xg, XG), (eg, EG), (pm, PM), (pw, PW)))
+    ]
+    for made in copies:
+        made.start()
+    chips = place.above[1:] + [place.fx, place.fy, place.fxy]
+    place.greet(chips, True)
+    tok, enc, rows, half_d = size.tok, size.enc, size.rows, size.model // 2
+    mine = pl.ds(aligned(place.core * half_d, 128), half_d)
+    away = pl.ds(aligned(place.other * half_d, 128), half_d)
+
+    def block_rows(block, count):
+        return pl.ds(aligned(block * count, 16), count)
+
+    def token_view(ref, count):
+        def view(half, block):
+            return ref.at[
+                pl.ds(aligned(block * count + half * (count // 2), 16), count // 2), mine
+            ]
+
+        return view
+
+    def token_out(ref, count):
+        def out(half, total):
+            ref[half * (count // 2) : (half + 1) * (count // 2), mine] = total
+
+        return out
+
+    def weight_stream(first, last, buf):
+        step = (last - first) // 2
+
+        def view(half, block):
+            return PW.at[
+                block_rows(block, rows), first + half * step : first + (half + 1) * step
+            ]
+
+        def out(half, total):
+            WG[:, first + half * step : first + (half + 1) * step] = total
+
+        return Scatter(wire, view, buf, out)
+
+    def pair_sum(ref, recv, count):
+        base = wire.slots(size.levels)
+        span = 4 * count
+
+        def start():
+            for k in (1, 2, 3, 0):
+                at = block_rows(place.below[k] // 4, span)
+                wire.swap(ref.at[at, away], recv.at[at, :], base + k)
+
+        def ready(k):
+            at = block_rows(place.below[k] // 4, span)
+            wire.got(recv.at[at, :], base + k)
+            ref[at, mine] = (ref[at, mine].astype(F32) + recv[at, :].astype(F32)).astype(LOW)
+
+        return start, ready
+
+    sx = Scatter(wire, token_view(XG, tok), bx, token_out(NG, tok))
+    se = Scatter(wire, token_view(EG, enc), be, token_out(NE, enc))
+    sw = weight_stream(0, 4 * size.wide, bs)
+    sc = weight_stream(4 * size.wide, 8 * size.wide, bc)
+    x_start, x_ready = pair_sum(XG, px, tok)
+    e_start, e_ready = pair_sum(EG, pe, enc)
+    level_base, plane_base = wire.slots(3), wire.slots(3)
+    copies[0].wait()
+    x_start()
+    copies[1].wait()
+    e_start()
+    sx.start(x_ready)
+    se.start(e_ready)
+    copies[2].wait()
+    for k in (1, 2, 3):
+        wire.send(
+            PM.at[block_rows(place.above[k] // 4, 4 * rows), :],
+            ml.at[k - 1],
+            level_base + k - 1,
+            place.above[k],
+        )
+    copies[3].wait()
+    sw.start()
+    sx.pass_near()
+    se.pass_near()
+    sx.pass_level()
+    sc.start()
+    se.pass_level()
+    sw.pass_near()
+    sx.finish()
+    x_slot, e_slot = wire.slots(1), wire.slots(1)
+    wire.swap(NG.at[:, mine], NG.at[:, mine], x_slot)
+    se.finish()
+    wire.swap(NE.at[:, mine], NE.at[:, mine], e_slot)
+    sw.pass_level()
+    sc.pass_near()
+    total = PM[block_rows(place.level, 4 * rows), :].astype(F32)
+    for k in (1, 2, 3):
+        wire.got(ml.at[k - 1], level_base + k - 1)
+        total = total + ml[k - 1].astype(F32)
+    ps[...] = total.astype(LOW)
+    my_cols = pl.ds(aligned(place.plane * size.part, 128), size.part)
+    for k, chip in enumerate((place.fx, place.fy, place.fxy)):
+        wire.send(
+            ps.at[block_rows(lax.rem(chip, 4), rows), :], mb.at[:, my_cols], plane_base + k, chip
+        )
+    mb[:, my_cols] = ps[block_rows(place.plane, rows), :]
+    wire.got(NG.at[:, away], x_slot)
+    extra, gain_one = rms_backward(layer_in[...], gains[0:1], NG[...])
+    input_grad[...] = self_grad[...] + extra
+    s1[...] = SM[...]
+    s1[0:1, :] = gain_one
+    small = wire.slots(5)
+    wire.send(s1, sr.at[0], small, place.fx)
+    sc.pass_level()
+    wire.got(sr.at[0], small)
+    s2[...] = s1[...] + sr[0]
+    wire.send(s2, sr.at[1], small + 1, place.fy)
+    wire.got(NE.at[:, away], e_slot)
+    enc_grad[...] = NE[...]
+    sw.finish()
+    wire.got(sr.at[1], small + 1)
+    sl[pl.ds(place.level, 1)] = (s2[...] + sr[1])[None]
+    for k in (1, 2, 3):
+        wire.send(
+            sl.at[place.level], sl.at[place.level], small + 1 + k, place.above[k]
+        )
+    sc.finish()
+    for k, chip in enumerate((place.fx, place.fy, place.fxy)):
+        cols = pl.ds(aligned(lax.rem(chip, 4) * size.part, 128), size.part)
+        wire.got(mb.at[:, cols], plane_base + k)
+    MG[...] = mb[...].astype(F32)
+    for k in (1, 2, 3):
+        wire.got(sl.at[place.below[k] // 4], small + 1 + k)
+    totals[...] = (sl[0] + sl[1]) + (sl[2] + sl[3])
+    wire.drain()
+
+
+def quick_device(
+    layer_in, encoded, self_query, self_key, self_value, self_out, cross_query, cross_key,
+    cross_value, cross_out, gate_proj, up_proj, down_proj, norm_gains, position_bias,
+    bucket_ids, block_order, out_grad,
+):
+    tok, model = layer_in.shape
+    enc = encoded.shape[0]
+    wide, units = self_query.shape[1], gate_proj.shape[1]
+    ctx = block_order.shape[0]
+    buckets, heads = position_bias.shape
+    size = Sizes(ctx, tok, enc, model, wide, units)
+    rows, quarter = size.rows, size.quarter
+
+    wa = jnp.concatenate(
+        (
+            self_query, self_key, self_value, self_out.T,
+            cross_query, cross_key, cross_value, cross_out.T,
+        ),
+        axis=1,
+    )
+    wm = jnp.concatenate(
+        [
+            piece[:, p * quarter : (p + 1) * quarter]
+            for p in range(4)
+            for piece in (gate_proj, up_proj, down_proj.T)
+        ],
+        axis=1,
+    )
+    boundaries = jnp.arange(1, buckets, dtype=jnp.int32)
+    starts = jnp.sum((bucket_ids[None, :] < boundaries[:, None]).astype(jnp.int32), axis=1)
+    here = lax.axis_index("ctx")
+    own_block = jnp.sum(jnp.where(jnp.arange(ctx) == here, block_order, 0))
+    lane = jnp.arange(2 * tok, dtype=jnp.int32)
+    shift = jnp.where(lane < tok, lane, lane - 2 * tok)
+    dist = (own_block - block_order)[:, None] * tok - shift[None, :]
+    ids = jnp.sum((dist[:, :, None] >= starts[None, None, :]).astype(jnp.int32), axis=-1)
+    ids = jnp.where(dist >= 0, ids, -1)
+    table = jnp.concatenate((position_bias.T, jnp.zeros((8 - heads, buckets), F32)), axis=0)
+
+    tok_all, enc_all, tok4 = ctx * tok, ctx * enc, 4 * tok
+    pairs = size.pairs
+    got = call(
+        gather_kernel,
+        size,
+        {"layer_in": layer_in, "encoded": encoded, "gains": norm_gains, "out_grad": out_grad,
+         "wa": wa, "wm": wm},
+        {"WA": ((model, size.attn_cols), LOW), "WM": ((model, size.part), LOW),
+         "X": ((tok_all, model), LOW), "E": ((enc_all, model), LOW), "GR": ((tok4, model), LOW)},
+        {"local": pltpu.SemaphoreType.DMA((2,)), **wire_sems(256)},
+        1,
+    )
+
+    def vmem(*shape, dtype=LOW):
+        return pltpu.VMEM(shape, dtype)
+
+    done = call(
+        compute_kernel,
+        size,
+        {"layer_in": layer_in, "gains": norm_gains, "out_grad": out_grad, "ids": ids,
+         "table": table, "WA": got["WA"], "WM": got["WM"], "X": got["X"], "E": got["E"],
+         "GR": got["GR"]},
+        {"layer_out": ((tok, model), F32), "PW": ((model, size.attn_cols), LOW),
+         "PM": ((model, size.part), LOW), "XG": ((tok_all, model), LOW),
+         "EG": ((enc_all, model), LOW), "self_grad": ((tok, model), F32),
+         "SM": ((16, model), F32)},
+        {"q": vmem(tok, wide), "kv": vmem(tok_all, 2 * wide), "mkv": vmem(enc_all, 2 * wide),
+         "probes": vmem(tok, wide), "s": vmem(2 * tok, tok_all, dtype=F32),
+         "e1": vmem(pairs, 2 * tok, tok_all), "e2": vmem(pairs, 2 * tok, enc_all),
+         "rl1": vmem(pairs, 2 * tok, 1, dtype=F32), "rl2": vmem(pairs, 2 * tok, 1, dtype=F32),
+         "mixed1": vmem(tok, wide), "mixed2": vmem(tok, wide),
+         "bias": vmem(ctx, 8, 2 * tok, dtype=F32), "diag": vmem(ctx, 8, 2 * tok, dtype=F32),
+         "after_self": vmem(tok, model, dtype=F32), "after_cross": vmem(tok, model, dtype=F32),
+         "cross_grad": vmem(tok, model, dtype=F32), "n2": vmem(tok, model),
+         "N3": vmem(tok4, model), "act": vmem(tok4, quarter), "GU": vmem(tok4, 2 * quarter),
+         "PN": vmem(tok4, model), "PO": vmem(tok4, model), "low": vmem(tok, model),
+         "mixed_grad": vmem(tok, wide), "q_grad": vmem(tok, wide),
+         "kv_grad": vmem(tok_all, 2 * wide), "mkv_grad": vmem(enc_all, 2 * wide),
+         "ca": vmem(3, tok, model), "cb": vmem(3, tok, model),
+         "pn_core": vmem(tok4, model // 2), "pn_plane": vmem(3, tok, model // 2),
+         "pn_whole": vmem(tok, model), "po_core": vmem(tok4, model // 2),
+         "po_plane": vmem(3, tok, model // 2), "po_whole": vmem(tok, model), **wire_sems(32)},
+        2,
+    )
+    last = call(
+        scatter_kernel,
+        size,
+        {"layer_in": layer_in, "gains": norm_gains, "self_grad": done["self_grad"],
+         "pw": done["PW"], "pm": done["PM"], "xg": done["XG"], "eg": done["EG"], "SM": done["SM"]},
+        {"WG": ((rows, size.attn_cols), F32), "MG": ((rows, size.mlp_cols), F32),
+         "input_grad": ((tok, model), F32), "enc_grad": ((enc, model), F32),
+         "totals": ((16, model), F32)},
+        {"PW": vmem(model, size.attn_cols), "PM": vmem(model, size.part),
+         "XG": vmem(tok_all, model), "EG": vmem(enc_all, model),
+         "bs": vmem(2, 15, rows, 2 * wide), "bc": vmem(2, 15, rows, 2 * wide),
+         "bx": vmem(2, 15, tok // 2, model // 2), "be": vmem(2, 15, enc // 2, model // 2),
+         "px": vmem(tok_all, model // 2), "pe": vmem(enc_all, model // 2),
+         "NG": vmem(tok, model, dtype=F32), "NE": vmem(enc, model, dtype=F32),
+         "ml": vmem(3, 4 * rows, size.part), "ps": vmem(4 * rows, size.part),
+         "mb": vmem(rows, size.mlp_cols), "s1": vmem(16, model, dtype=F32),
+         "s2": vmem(16, model, dtype=F32), "sr": vmem(2, 16, model, dtype=F32),
+         "sl": vmem(4, 16, model, dtype=F32), "local": pltpu.SemaphoreType.DMA((4,)),
+         **wire_sems(160)},
+        3,
+        any_inputs=("pw", "pm", "xg", "eg"),
+    )
+    wg, mg, totals = last["WG"], last["MG"], last["totals"]
+    grads = [wg[:, size.col[name]] for name in ("q", "k", "v", "o", "cq", "ck", "cv", "co")]
+    mlp = mg.reshape(rows, 4, 3, quarter)
+    gate, upward, down = (mlp[:, :, i].reshape(rows, units) for i in range(3))
+    return (
+        done["layer_out"],
+        last["input_grad"],
+        last["enc_grad"],
+        *grads[:3],
+        grads[3].T,
+        *grads[4:7],
+        grads[7].T,
+        gate,
+        upward,
+        down.T,
+        totals[:3],
+        totals[8 : 8 + heads, :buckets].T,
+    )
+
+
+def quick_fits(mesh):
+    return mesh.shape["ctx"] == 16 and mesh.shape["head"] == 2
 
 
 def as_sent(shard):
@@ -389,6 +1426,7 @@
 
 
 def solution(mesh):
+    body = quick_device if quick_fits(mesh) else per_device
     placed = (
         P("ctx", None),
         P("ctx", None),
@@ -410,7 +1448,7 @@
         P("ctx", None),
     )
     return jax.shard_map(
-        per_device,
+        body,
         mesh=mesh,
         in_specs=placed,
         out_specs=(

time: 2530 us -> 296 us (0.12)
  waiting for transfers between devices: 1750 us -> 0 us
  blocking collectives: 491 us -> 0 us
  Pallas kernels: 0 us -> 260 us
  matrix products: 126 us -> 0 us
  local copies, waits for them, and re-layouts: 103 us -> 29.2 us
    reduce_scatter x11 -> x0, waiting for transfers between devices: 1260 us -> none  [the longest x1 149 us: per_device(): lax.psum_scatter(self_terms, 'ctx', scatter_dimension=0, tiled=True)]
    all_gather x10 -> x0, blocking collectives: 416 us -> none  [the longest x1 45.9 us: per_device(): lax.all_gather(self_key, 'ctx', axis=0, tiled=True)]
    unnamed x25 -> x0, waiting for transfers between devices: 261 us -> none
    pallas_call x0 -> x3, Pallas kernels: none -> 260 us  [call(): return dict(zip(outs, made(*ins.values()), strict=True))]
    all_gather x5 -> x0, waiting for transfers between devices: 176 us -> none  [the longest x1 60.6 us: per_device(): lax.all_gather(up_proj, 'ctx', axis=0, tiled=True)]
    dot_general x87 -> x0, matrix products: 126 us -> none  [the longest x8 37 us: bias_scores(): jnp.einsum('qkb,bh->hqk', steps, rises, precision=HIGH)]
    psum x1 -> x0, blocking collectives: 75.2 us -> none  [per_device(): lax.psum((jnp.stack((gain_one, gain_two, gain_three)), bias_grad), 'ctx')]
    psum x5 -> x0, waiting for transfers between devices: 48.2 us -> none  [join_heads(): lax.psum(as_sent(parts), 'head')]
  transfers between devices with their start and end apart: 23 -> 0, of which waited for: 19 -> 0; matrix products, arithmetic and copies ran while one was open for 6% -> 0% of each run, Pallas kernels for 0% -> 0%
where the time goes in v1:
time: 296 us; the launch traced here: 294 us
  Pallas kernels  260 us (88%)
  local copies, waits for them, and re-layouts  29.2 us (10%)
  other arithmetic  4.38 us (1%)
    pallas_call x3, Pallas kernels, call(): return dict(zip(outs, made(*ins.values()), strict=True))  260 us
    unnamed x34, local copies, waits for them, and re-layouts  18.6 us

profile of v1, /device:TPU:0, one launch (start us, length us, event | category | flops | bytes accessed | tf_op | source)
XLA Modules:
  0.0 294.1 jit_solution(15852571397660557062)
XLA Ops:
  0.6 1.3 fusion
  1.9 1.3 subtract_multiply_fusion
  3.3 0.9 convert_reduce_fusion.1
  4.2 1.3 concatenate.9.refs_4_
  5.5 0.1 broadcast_subtract_fusion
  5.5 0.1 convert_reduce_fusion
  5.6 0.7 compare_select_fusion.refs_3_
  6.3 0.8 constant_dynamic-update-slice_fusion.7
  7.1 0.8 constant_dynamic-update-slice_fusion.6
  7.9 0.8 constant_dynamic-update-slice_fusion.5
  8.7 0.8 constant_dynamic-update-slice_fusion.4
  9.4 0.8 constant_dynamic-update-slice_fusion.3
  10.2 0.8 constant_dynamic-update-slice_fusion.2
  11.0 0.8 constant_dynamic-update-slice_fusion.1
  11.8 0.8 constant_dynamic-update-slice_fusion.refs_4_
  12.6 0.7 constant_dynamic-update-slice_fusion.19
  13.3 0.7 constant_dynamic-update-slice_fusion.18
  14.0 0.7 constant_dynamic-update-slice_fusion.17
  14.8 0.7 constant_dynamic-update-slice_fusion.16
  15.5 0.8 constant_dynamic-update-slice_fusion.15
  16.3 0.7 constant_dynamic-update-slice_fusion.14
  17.0 0.7 constant_dynamic-update-slice_fusion.13
  17.8 0.7 constant_dynamic-update-slice_fusion.12
  18.5 0.7 constant_dynamic-update-slice_fusion.11
  19.2 0.7 constant_dynamic-update-slice_fusion.10
  20.0 0.7 constant_dynamic-update-slice_fusion.9
  20.7 0.7 constant_dynamic-update-slice_fusion.8.refs_5_
  21.4 0.0 copy-done.2
  21.5 0.7 copy-done.3
  22.2 81.9 %shard_map.297 = (bf16[768,3072]{1,0:T(8,128)(2,1)}, bf16[768,768]{1,0:T(8,128)(2,1)}, bf16[2048,768]{1,0:T(8,128)(2,1)}, bf16[1024,768]{1,0:T(8,128)(2,1)}, bf16[512,768]{1,0:T(8,128)(2,1)}) custom-call(f32[128,768]{1,0:T(8,128)} %refs_0_.5, bf16[64,768]{1,0:T(8,128)(2,1)} %refs_1_.3, f32[3,768]{1,0:T(4,128)} %refs_1_.5, f32[128,768]{1,0:T(8,128)} %refs_2_.3, ...), custom_call_target="tpu_custom_call" | custom-call | tf_op jit(solution)/shard_map/pallas_call | solution.py:545
  104.1 90.0 %shard_map.298 = (f32[128,768]{1,0:T(8,128)}, bf16[768,3072]{1,0:T(8,128)(2,1)}, bf16[768,768]{1,0:T(8,128)(2,1)}, bf16[2048,768]{1,0:T(8,128)(2,1)}, bf16[1024,...) custom-call(f32[128,768]{1,0:T(8,128)} %refs_0_.5, f32[3,768]{1,0:T(4,128)} %refs_1_.5, ...), custom_call_target="tpu_custom_call" | custom-call | tf_op jit(solution)/shard_map/pallas_call | solution.py:545
  194.1 87.9 %shard_map.299 = (f32[48,3072]{1,0:T(8,128)}, f32[48,3072]{1,0:T(8,128)}, f32[128,768]{1,0:T(8,128)}, f32[64,768]{1,0:T(8,128)}, f32[16,768]{1,0:T(8,128)}) custom-call(f32[128,768]{1,0:T(8,128)} %refs_0_.5, f32[3,768]{1,0:T(4,128)} %refs_1_.5, f32[128,768]{1,0:T(8,128)} %get-tuple-element.39.refs_2_, bf16[768,3072]{1,0:T(8,128)(2,1)} %get-tuple-element.40.refs_3_, ...), custom_call_target="tpu_custom_call" | custom-call | tf_op jit(solution)/shard_map/pallas_call | solution.py:545
  282.0 0.0 copy-start
  282.0 0.0 copy-start.1
  282.0 1.3 slice_bitcast_fusion.2
  283.3 1.3 slice.98
  284.7 2.0 slice_bitcast_fusion
  286.7 1.5 reshape.77
  288.2 1.6 slice_reduce_fusion
  289.8 0.7 copy.36
  290.5 0.7 copy.35
  291.2 0.7 copy.34
  292.0 0.0 copy-done
  292.0 0.7 copy.58
  292.7 0.0 copy-done.1
  292.7 0.7 copy.59
  293.5 0.0 copy-done.4
  293.5 0.7 copy.60
  (5 shorter events, 0.0 us)
Async XLA Ops:
  12.6 8.9 %copy-start.2 = (bf16[48,3072]{1,0:T(8,128)(2,1)}, bf16[48,3072]{1,0:T(8,128)(2,1)S(1)}, u32[]{:S(2)}) copy-start(bf16[48,3072]{1,0:T(8,128)(2,1)S(1)} %constant_dynamic-update-slice_fusion.refs_4_) | copy-start | bytes 884740
  21.5 0.7 copy-start.3
  282.0 10.0 %copy-start = (f32[128,768]{1,0:T(8,128)S(1)}, f32[128,768]{1,0:T(8,128)}, u32[]{:S(2)}) copy-start(f32[128,768]{1,0:T(8,128)} %get-tuple-element.77) | copy-start | bytes 1179652
  282.0 10.7 %copy-start.1 = (f32[128,768]{1,0:T(8,128)S(1)}, f32[128,768]{1,0:T(8,128)}, u32[]{:S(2)}) copy-start(f32[128,768]{1,0:T(8,128)} %get-tuple-element.78) | copy-start | bytes 1179652
  284.7 8.8 %copy-start.4 = (f32[64,768]{1,0:T(8,128)S(1)}, f32[64,768]{1,0:T(8,128)}, u32[]{:S(2)}) copy-start(f32[64,768]{1,0:T(8,128)} %get-tuple-element.79) | copy-start | bytes 589828

commit v2 on v0

--- a/solution.py
+++ b/solution.py
@@ -1,13 +1,1078 @@
+import functools
 import math
 
 import jax
 import jax.numpy as jnp
 from jax import lax
+from jax.experimental import pallas as pl
+from jax.experimental.pallas import tpu as pltpu
 from jax.sharding import PartitionSpec as P
 
 EPS = 1e-06
 NEG = -1e30
 HIGH = lax.Precision.HIGHEST
+LOW = jnp.bfloat16
+F32 = jnp.float32
+MESH = pl.DeviceIdType.MESH
+VMEM_LIMIT = 66_000_000
+
+
+def dot(left, right, **kw):
+    return jnp.dot(left, right, preferred_element_type=F32, **kw)
+
+
+def dot_nt(left, right, **kw):
+    return lax.dot_general(left, right, (((1,), (1,)), ((), ())), preferred_element_type=F32, **kw)
+
+
+def dot_tn(left, right, **kw):
+    return lax.dot_general(left, right, (((0,), (0,)), ((), ())), preferred_element_type=F32, **kw)
+
+
+def rms_forward(rows, gain):
+    return rows * lax.rsqrt(jnp.mean(rows * rows, axis=-1, keepdims=True) + EPS) * gain
+
+
+def rms_backward(rows, gain, grad):
+    scale = lax.rsqrt(jnp.mean(rows * rows, axis=-1, keepdims=True) + EPS)
+    scaled = gain * grad
+    inner = jnp.mean(scaled * rows, axis=-1, keepdims=True)
+    row_grad = scale * scaled - rows * (scale * scale * scale * inner)
+    gain_grad = jnp.sum(grad * rows * scale, axis=0, keepdims=True)
+    return row_grad, gain_grad
+
+
+def aligned(value, step):
+    return value if isinstance(value, int) else pl.multiple_of(value, step)
+
+
+class Place:
+    def __init__(self, count):
+        self.count = count
+        self.here = lax.axis_index("ctx")
+        self.core = lax.axis_index("head")
+        self.other = 1 - self.core
+        self.plane = lax.rem(self.here, 4)
+        self.level = self.here // 4
+        self.fx = self.flip(self.here, 0)
+        self.fy = self.flip(self.here, 1)
+        self.fxy = self.flip(self.fx, 1)
+        self.above = [lax.rem(self.here + 4 * k, count) for k in range(4)]
+        self.below = [lax.rem(self.here + count - 4 * k, count) for k in range(4)]
+
+    def flip(self, index, axis):
+        if axis == 0:
+            return index + 1 - 2 * lax.rem(index, 2)
+        return index + 2 - 4 * lax.rem(index // 2, 2)
+
+    def near(self, half):
+        return (self.fx, self.fy) if half == 0 else (self.fy, self.fx)
+
+    def greet(self, chips, partner):
+        barrier = pltpu.get_barrier_semaphore()
+        total = len(chips) + (1 if partner else 0)
+        for chip in chips:
+            pl.semaphore_signal(
+                barrier, inc=1, device_id=(chip, self.core), device_id_type=MESH
+            )
+        if partner:
+            pl.semaphore_signal(
+                barrier, inc=1, device_id=(self.here, self.other), device_id_type=MESH
+            )
+        pl.semaphore_wait(barrier, total)
+
+
+class Wire:
+    def __init__(self, place, send_sem, recv_sem):
+        self.place, self.send_sem, self.recv_sem = place, send_sem, recv_sem
+        self.sent = []
+        self.used = 0
+
+    def slots(self, count):
+        base = self.used
+        self.used += count
+        assert self.used <= self.send_sem.shape[0], self.used
+        return base
+
+    def copy(self, src, dst, slot, chip, core):
+        return pltpu.make_async_remote_copy(
+            src_ref=src,
+            dst_ref=dst,
+            send_sem=self.send_sem.at[slot],
+            recv_sem=self.recv_sem.at[slot],
+            device_id=(chip, core),
+            device_id_type=MESH,
+        )
+
+    def send(self, src, dst, slot, chip=None, core=None):
+        chip = self.place.here if chip is None else chip
+        core = self.place.core if core is None else core
+        made = self.copy(src, dst, slot, chip, core)
+        made.start()
+        self.sent.append(made)
+
+    def swap(self, src, dst, slot):
+        self.send(src, dst, slot, None, self.place.other)
+
+    def got(self, dst, slot):
+        place = self.place
+        self.copy(dst, dst, slot, place.here, place.other).wait_recv()
+
+    def drain(self):
+        for made in self.sent:
+            made.wait_send()
+        self.sent = []
+
+
+class Gather:
+    def __init__(self, wire, view, share, halves=2):
+        self.wire, self.view, self.share = wire, view, share
+        self.base = [wire.slots(15) for _ in range(halves)]
+        self.side = [wire.slots(16) for _ in range(halves)] if share else None
+        self.halves = range(halves)
+
+    def _out(self, half, block, slot, chip):
+        ref = self.view(half, block)
+        self.wire.send(ref, ref, self.base[half] + slot, chip)
+
+    def _in(self, half, block, slot):
+        self.wire.got(self.view(half, block), self.base[half] + slot)
+        if self.share:
+            ref = self.view(half, block)
+            self.wire.swap(ref, ref, self.side[half] + slot)
+
+    def start(self):
+        place = self.wire.place
+        for half in self.halves:
+            near, far = place.near(half)
+            for k in (1, 2, 3):
+                self._out(half, place.here, k - 1, place.above[k])
+            self._out(half, place.here, 3, near)
+            self._out(half, place.here, 7, far)
+
+    def pass_level(self):
+        place = self.wire.place
+        for k in (1, 2, 3):
+            for half in self.halves:
+                near, far = place.near(half)
+                self._in(half, place.below[k], k - 1)
+                self._out(half, place.below[k], 3 + k, near)
+                self._out(half, place.below[k], 7 + k, far)
+
+    def pass_near(self):
+        place = self.wire.place
+        for k in range(4):
+            for half in self.halves:
+                _, far = place.near(half)
+                block = place.flip(place.below[k], half)
+                self._in(half, block, 3 + k)
+                self._out(half, block, 11 + k, far)
+
+    def finish(self):
+        place = self.wire.place
+        for k in range(4):
+            for half in self.halves:
+                block = place.flip(place.below[k], 1 - half)
+                self._in(half, block, 7 + k)
+                self._in(half, place.flip(block, half), 11 + k)
+
+    def finish_share(self):
+        if not self.share:
+            return
+        place = self.wire.place
+        for k in range(4):
+            for half in self.halves:
+                block = place.below[k]
+                if k:
+                    self._share_in(half, block, k - 1)
+                self._share_in(half, place.flip(block, half), 3 + k)
+                block = place.flip(block, 1 - half)
+                self._share_in(half, block, 7 + k)
+                self._share_in(half, place.flip(block, half), 11 + k)
+
+    def _share_in(self, half, block, slot):
+        self.wire.got(self.share(half, block), self.side[half] + slot)
+
+
+class Scatter:
+    def __init__(self, wire, view, buf, out, halves=2):
+        self.wire, self.view, self.out = wire, view, out
+        self.far_buf = lambda half, slot: buf(half).at[slot]
+        self.near_buf = lambda half, slot: buf(half).at[8 + slot]
+        self.level_buf = lambda half, slot: buf(half).at[12 + slot]
+        self.base = [wire.slots(15) for _ in range(halves)]
+        self.halves = range(halves)
+
+    def start(self, levels=(1, 2, 3, 0)):
+        place = self.wire.place
+        for k in levels:
+            for half in self.halves:
+                _, far = place.near(half)
+                away = place.flip(place.below[k], 1 - half)
+                for pair, block in ((1, place.flip(away, half)), (0, away)):
+                    slot = 2 * k + pair
+                    self.wire.send(
+                        self.view(half, block),
+                        self.far_buf(half, slot),
+                        self.base[half] + slot,
+                        far,
+                    )
+
+    def pass_near(self):
+        place = self.wire.place
+        for k in (1, 2, 3, 0):
+            for half in self.halves:
+                near, _ = place.near(half)
+                block = place.flip(place.below[k], half)
+                slot = 2 * k + 1
+                self.wire.got(self.far_buf(half, slot), self.base[half] + slot)
+                ref = self.view(half, block)
+                ref[...] = (
+                    ref[...].astype(F32) + self.far_buf(half, slot)[...].astype(F32)
+                ).astype(LOW)
+                self.wire.send(ref, self.near_buf(half, k), self.base[half] + 8 + k, near)
+
+    def pass_level(self):
+        place = self.wire.place
+        for k in (1, 2, 3):
+            for half in self.halves:
+                self._add(half, k)
+                ref = self.view(half, place.below[k])
+                self.wire.send(
+                    ref, self.level_buf(half, k - 1), self.base[half] + 11 + k, place.below[k]
+                )
+
+    def _add(self, half, k):
+        place = self.wire.place
+        self.wire.got(self.far_buf(half, 2 * k), self.base[half] + 2 * k)
+        self.wire.got(self.near_buf(half, k), self.base[half] + 8 + k)
+        ref = self.view(half, place.below[k])
+        total = (
+            ref[...].astype(F32)
+            + self.far_buf(half, 2 * k)[...].astype(F32)
+            + self.near_buf(half, k)[...].astype(F32)
+        )
+        if k:
+            ref[...] = total.astype(LOW)
+        return total
+
+    def finish(self):
+        for half in self.halves:
+            total = self._add(half, 0)
+            for k in (1, 2, 3):
+                self.wire.got(self.level_buf(half, k - 1), self.base[half] + 11 + k)
+                total = total + self.level_buf(half, k - 1)[...].astype(F32)
+            self.out(half, total)
+
+
+def lane_split(rows):
+    lane = lax.broadcasted_iota(jnp.int32, rows.shape, 1)
+    low = lane < rows.shape[1] // 2
+    zero = jnp.zeros_like(rows)
+    return jnp.concatenate((jnp.where(low, rows, zero), jnp.where(low, zero, rows)), axis=0)
+
+
+def lane_join(rows):
+    count, width = rows.shape[0] // 2, rows.shape[1]
+    lane = lax.broadcasted_iota(jnp.int32, (count, width), 1)
+    return jnp.where(lane < width // 2, rows[:count], rows[count:])
+
+
+def pair_attend(tok, pairs, chunk, q_ref, kv_ref, s_ref, e_ref, rl_ref, mixed_ref, bias_ref, between):
+    keys = kv_ref.shape[0]
+    total = pairs * 128
+
+    for j in range(pairs):
+        cols = slice(j * 128, (j + 1) * 128)
+        vcols = slice(total + j * 128, total + (j + 1) * 128)
+        q_cat = lane_split(q_ref[:, cols])
+
+        def score(c, top):
+            rows = pl.ds(aligned(c * chunk, chunk), chunk)
+            s = dot_nt(q_cat, kv_ref[rows, cols])
+            if bias_ref is not None:
+                tiles = []
+                for half in range(2):
+                    row = []
+                    for b in range(chunk // tok):
+                        vec = bias_ref[c * (chunk // tok) + b, 2 * j + half : 2 * j + half + 1, :]
+                        wide = jnp.broadcast_to(vec, (tok, 2 * tok))
+                        row.append(pltpu.roll(wide, 0, 1, stride=1, stride_axis=0)[:, :tok])
+                    tiles.append(jnp.concatenate(row, axis=1))
+                s = s + jnp.concatenate(tiles, axis=0)
+            s_ref[:, rows] = s
+            for b in range(chunk // 128):
+                top = jnp.maximum(top, s[:, b * 128 : (b + 1) * 128])
+            return top
+
+        top = lax.fori_loop(0, keys // chunk, score, jnp.full((2 * tok, 128), NEG, F32))
+        peak = jnp.max(top, axis=1, keepdims=True)
+
+        def weigh(c, state):
+            acc, run = state
+            rows = pl.ds(aligned(c * chunk, chunk), chunk)
+            e = jnp.exp(s_ref[:, rows] - peak)
+            for b in range(chunk // 128):
+                run = run + e[:, b * 128 : (b + 1) * 128]
+            low = e.astype(LOW)
+            e_ref[j, :, rows] = low
+            return (acc + dot(low, kv_ref[rows, vcols]), run)
+
+        zero = jnp.zeros((2 * tok, 128), F32)
+        acc, run = lax.fori_loop(0, keys // chunk, weigh, (zero, zero))
+        rl = 1.0 / jnp.sum(run, axis=1, keepdims=True)
+        rl_ref[j] = rl
+        mixed_ref[:, cols] = lane_join(acc * rl).astype(LOW)
+        between(j)
+
+
+class PairBack:
+    def __init__(self, tok, pairs, q, kv, e, rl, mixed, grad, kv_grad, diag, qc, gc, dl, dq):
+        self.tok, self.pairs, self.kv, self.e = tok, pairs, kv, e
+        self.kv_grad, self.diag, self.qc, self.gc, self.dl, self.dq = kv_grad, diag, qc, gc, dl, dq
+        self.total = pairs * 128
+        for j in range(pairs):
+            cols = slice(j * 128, (j + 1) * 128)
+            rl_j = rl[j]
+            grads = lane_split(grad[:, cols].astype(F32))
+            qc[j] = lane_split(q[:, cols])
+            gc[j] = (grads * rl_j).astype(LOW)
+            values = lane_split(mixed[:, cols].astype(F32))
+            dl[j] = jnp.sum(grads * values, axis=1, keepdims=True) * rl_j
+            dq[j] = jnp.zeros(dq.shape[1:], F32)
+
+    def chunk(self, start, count):
+        tok, kv, qc, gc = self.tok, self.kv, self.qc, self.gc
+        rows = pl.ds(aligned(start, count), count)
+        flip = (
+            lax.broadcasted_iota(jnp.int32, (tok, tok), 0)
+            + lax.broadcasted_iota(jnp.int32, (tok, tok), 1)
+            == tok - 1
+        ).astype(LOW)
+
+        def one_pair(j, carry):
+            cols = pl.ds(aligned(j * 128, 128), 128)
+            vcols = pl.ds(aligned(self.total + j * 128, 128), 128)
+            low_e = self.e[j, :, rows]
+            dp = dot_nt(gc[j], kv[rows, vcols])
+            ds = (low_e.astype(F32) * (dp - self.dl[j])).astype(LOW)
+            if self.diag is not None:
+                for half in range(2):
+                    turned = dot(flip, ds[half * tok : (half + 1) * tok])
+                    for b in range(count // tok):
+                        tile = turned[:, b * tok : (b + 1) * tok]
+                        wide = jnp.concatenate((tile, jnp.zeros_like(tile)), axis=1)
+                        wide = pltpu.roll(wide, tok + 1, 1, stride=1, stride_axis=0)
+                        self.diag[start // tok + b, pl.ds(2 * j + half, 1), :] = jnp.sum(
+                            wide, axis=0, keepdims=True
+                        )
+            self.kv_grad[rows, cols] = dot_tn(ds, qc[j]).astype(LOW)
+            self.kv_grad[rows, vcols] = dot_tn(low_e, gc[j]).astype(LOW)
+            self.dq[j] = self.dq[j] + dot(ds, kv[rows, cols])
+            return carry
+
+        lax.fori_loop(0, self.pairs, one_pair, 0)
+
+    def finish(self, q_grad):
+        for j in range(self.pairs):
+            q_grad[:, j * 128 : (j + 1) * 128] = lane_join(self.dq[j]).astype(LOW)
+
+
+def bucket_rows(buckets_ref, order_ref, here, table_rows, ids_ref):
+    count, tok = buckets_ref.shape
+    turn = (
+        lax.broadcasted_iota(jnp.int32, (tok, tok), 0)
+        + lax.broadcasted_iota(jnp.int32, (tok, tok), 1)
+        == tok - 1
+    ).astype(LOW)
+    table_rows[:count, :] = jnp.full((count, tok), -1.0, F32)
+    table_rows[count:, :] = dot(buckets_ref[...].astype(LOW), turn)
+    own = order_ref[here]
+
+    def one(block, carry):
+        at = own - order_ref[block] + count
+        wide = jnp.concatenate(
+            (table_rows[pl.ds(at - 1, 1), :], table_rows[pl.ds(at, 1), :]), axis=1
+        )
+        ids_ref[pl.ds(block, 1), :] = pltpu.roll(wide, 1, 1)
+        return carry
+
+    lax.fori_loop(0, count, one, 0)
+
+
+def bucket_masks(ids_ref, block, buckets):
+    ids = ids_ref[pl.ds(block, 1), :]
+    row = lax.broadcasted_iota(jnp.int32, (buckets, ids.shape[1]), 0).astype(F32)
+    return ids, (row == ids).astype(F32)
+
+
+def bias_vectors(ids_ref, table_ref, bias_ref):
+    buckets, heads = table_ref.shape
+
+    def one(block, carry):
+        ids, mask = bucket_masks(ids_ref, block, buckets)
+        vec = dot_tn(table_ref[...], mask, precision=HIGH)
+        bias_ref[block, :heads, :] = jnp.where(ids >= 0, vec, NEG)
+        return carry
+
+    lax.fori_loop(0, ids_ref.shape[0], one, 0)
+
+
+def bucket_sums(ids_ref, diag_ref, buckets):
+    def one(block, total):
+        _, mask = bucket_masks(ids_ref, block, buckets)
+        return total + dot_nt(mask, diag_ref[block], precision=HIGH)
+
+    start = jnp.zeros((buckets, diag_ref.shape[1]), F32)
+    return lax.fori_loop(0, ids_ref.shape[0], one, start)
+
+
+def rows_loop(count, step, body):
+    def one(index, carry):
+        body(pl.ds(aligned(index * step, step), step))
+        return carry
+
+    lax.fori_loop(0, count // step, one, 0)
+
+
+GELU_A = 0.7978845608028654
+GELU_B = 0.044715
+
+
+def gelu_parts(value):
+    square = value * value
+    wave = jnp.tanh(GELU_A * (value + GELU_B * value * square))
+    half = 0.5 * (1.0 + wave)
+    slope = half + 0.5 * value * (1.0 - wave * wave) * (GELU_A * (1.0 + 3.0 * GELU_B * square))
+    return value * half, slope
+
+
+def core_sum(wire, part, out_buf, in_buf):
+    slot = wire.slots(1)
+    out_buf[...] = part.astype(LOW)
+    wire.swap(out_buf, in_buf, slot)
+    wire.got(in_buf, slot)
+    return out_buf[...].astype(F32) + in_buf[...].astype(F32)
+
+
+class PlaneSum:
+    def __init__(self, wire, tok, part, core_buf, plane_buf, whole):
+        self.wire, self.tok = wire, tok
+        self.part, self.core_buf, self.plane_buf, self.whole = part, core_buf, plane_buf, whole
+        self.base = wire.slots(8)
+        self.half = whole.shape[1] // 2
+        place = wire.place
+        self.chips = (place.here, place.fx, place.fy, place.fxy)
+
+    def cols(self, core):
+        return pl.ds(aligned(core * self.half, 128), self.half)
+
+    def rows(self, k):
+        return pl.ds(aligned(lax.rem(self.chips[k], 4) * self.tok, self.tok), self.tok)
+
+    def start(self, k):
+        away = self.cols(self.wire.place.other)
+        rows = self.rows(k)
+        self.wire.swap(self.part.at[rows, away], self.core_buf.at[rows, :], self.base + k)
+
+    def middle(self, k):
+        wire, rows = self.wire, self.rows(k)
+        wire.got(self.core_buf.at[rows, :], self.base + k)
+        total = self.part[rows, self.cols(wire.place.core)].astype(F32)
+        total = total + self.core_buf[rows, :].astype(F32)
+        self.core_buf[rows, :] = total.astype(LOW)
+        if k:
+            wire.send(
+                self.core_buf.at[rows, :],
+                self.plane_buf.at[k - 1],
+                self.base + 3 + k,
+                self.chips[k],
+            )
+
+    def finish(self):
+        place, wire = self.wire.place, self.wire
+        total = self.core_buf[self.rows(0), :].astype(F32)
+        for k in (1, 2, 3):
+            wire.got(self.plane_buf.at[k - 1], self.base + 3 + k)
+            total = total + self.plane_buf[k - 1].astype(F32)
+        mine = self.cols(place.core)
+        self.whole[:, mine] = total.astype(LOW)
+        wire.swap(self.whole.at[:, mine], self.whole.at[:, mine], self.base + 7)
+
+    def finish_core(self):
+        self.wire.got(self.whole.at[:, self.cols(self.wire.place.other)], self.base + 7)
+
+
+class PlaneGather:
+    def __init__(self, wire, tok, ref):
+        self.wire, self.tok, self.ref = wire, tok, ref
+        self.half = ref.shape[1] // 2
+        self.base = wire.slots(8)
+        place = wire.place
+        self.chips = (place.here, place.fx, place.fy, place.fxy)
+
+    def view(self, k, core):
+        rows = pl.ds(aligned(lax.rem(self.chips[k], 4) * self.tok, self.tok), self.tok)
+        return self.ref.at[rows, pl.ds(aligned(core * self.half, 128), self.half)]
+
+    def start(self):
+        own = self.view(0, self.wire.place.core)
+        for k in (1, 2, 3):
+            self.wire.send(own, own, self.base + k, self.chips[k])
+
+    def share(self, k):
+        ref = self.view(k, self.wire.place.core)
+        self.wire.got(ref, self.base + k)
+        self.wire.swap(ref, ref, self.base + 4 + k)
+
+    def finish(self, k):
+        self.wire.got(self.view(k, self.wire.place.other), self.base + 4 + k)
+
+
+class Sizes:
+    def __init__(self, ctx, tok, enc, model, wide, units):
+        self.ctx, self.tok, self.enc, self.model, self.wide = ctx, tok, enc, model, wide
+        self.rows = model // ctx
+        self.units = units
+        self.quarter = units // 4
+        self.pairs = wide // 128
+        self.levels = ctx // 4
+        self.attn_cols = 8 * wide
+        self.mlp_cols = 3 * units
+        self.part = 3 * self.quarter
+        self.names = ("q", "k", "v", "cq", "ck", "cv", "o", "co")
+        self.col = {n: slice(i * wide, (i + 1) * wide) for i, n in enumerate(self.names)}
+        self.col["kv"] = slice(wide, 3 * wide)
+        self.col["ckv"] = slice(4 * wide, 6 * wide)
+        self.cuts = {
+            "s": self.halves(0, 3 * wide, 0),
+            "c": self.halves(3 * wide, 6 * wide, 1),
+            "o": self.halves(6 * wide, 7 * wide, 0),
+            "co": self.halves(7 * wide, 8 * wide, 1),
+        }
+
+    def halves(self, first, last, up):
+        tiles = (last - first) // 128
+        middle = first + (tiles + up) // 2 * 128
+        return ((first, middle), (middle, last))
+
+
+def named(kernel, names):
+    def body(*refs):
+        kernel(**dict(zip(names, refs, strict=True)))
+
+    return body
+
+
+def wire_sems(count):
+    return {
+        "send_sem": pltpu.SemaphoreType.DMA((count,)),
+        "recv_sem": pltpu.SemaphoreType.DMA((count,)),
+    }
+
+
+def turned(block):
+    count = block.shape[1]
+    eye = (
+        lax.broadcasted_iota(jnp.int32, (count, count), 0)
+        == lax.broadcasted_iota(jnp.int32, (count, count), 1)
+    ).astype(LOW)
+    return dot_nt(eye, block).astype(LOW)
+
+
+def layer_kernel(
+    size, layer_in, encoded, sq, sk, sv, so, cq, ck, cv, co, gate_w, up_w, down_w, gains,
+    table, buckets, order, out_grad,
+    layer_out, input_grad, enc_grad, WG, mb, totals, bias_totals,
+    WA, WM, wm, X, E, GR, PW, PM,
+    q, kv, mkv, probes, s, e1, e2, rl1, rl2, mixed1, mixed2, table_rows, ids, bias, diag,
+    after_self, after_cross, cross_grad, self_grad, n2, N3, act, GU, PN, PO, low, mixed_grad,
+    q_grad, kv_grad, mkv_grad, ca, cb, pn_core, pn_plane, pn_whole, po_core, po_plane, po_whole,
+    qc, gc, dl, dq, bs0, bs1, bc0, bc1, bo0, bo1, bp0, bp1, bx, be, px, pe, NG, NE, ml, ps,
+    s1, s2, sr, sl, t1, t2, tr, tl, send_sem, recv_sem,
+):
+    place = Place(size.ctx)
+    wire = Wire(place, send_sem, recv_sem)
+    tok, enc, rows, half_d = size.tok, size.enc, size.rows, size.model // 2
+    col, model, quarter = size.col, size.model, size.quarter
+    ctx_tok, ctx_enc = X.shape[0], E.shape[0]
+    plane_chips = (place.fx, place.fy, place.fxy)
+    XG, EG = kv, mkv
+
+    def block_rows(block, count):
+        return pl.ds(aligned(block * count, 16), count)
+
+    here_rows = block_rows(place.here, tok)
+    own_weights = block_rows(place.here, rows)
+    my_part = pl.ds(aligned(place.plane * size.part, 128), size.part)
+    mine = pl.ds(aligned(place.core * half_d, 128), half_d)
+    away = pl.ds(aligned(place.other * half_d, 128), half_d)
+
+    def token_view(ref, count, core):
+        def view(half, block):
+            return ref.at[
+                pl.ds(aligned(block * count + half * (count // 2), 16), count // 2),
+                pl.ds(aligned(core * half_d, 128), half_d),
+            ]
+
+        return view
+
+    def weight_view(ref, name):
+        def view(half, block):
+            first, last = size.cuts[name][half]
+            return ref.at[block_rows(block, rows), first:last]
+
+        return view
+
+    gx = Gather(wire, token_view(X, tok, place.core), token_view(X, tok, place.other))
+    ge = Gather(wire, token_view(E, enc, place.core), token_view(E, enc, place.other))
+    gs, gc_, go, gp = (Gather(wire, weight_view(WA, n), None) for n in ("s", "c", "o", "co"))
+    gg = PlaneGather(wire, tok, GR)
+    spread = PlaneGather(wire, tok, N3)
+    sum_n = PlaneSum(wire, tok, PN, pn_core, pn_plane, pn_whole)
+    sum_o = PlaneSum(wire, tok, PO, po_core, po_plane, po_whole)
+    mg_plane, mg_level, ms_level, ms_plane = (wire.slots(3) for _ in range(4))
+
+    place.greet(place.above[1:] + list(plane_chips), True)
+    X[here_rows, :] = rms_forward(layer_in[...], gains[0:1]).astype(LOW)
+    gx.start()
+    for name, ref in zip(("q", "k", "v", "cq", "ck", "cv"), (sq, sk, sv, cq, ck, cv)):
+        WA[own_weights, col[name]] = ref[...]
+    gs.start()
+    WA[own_weights, col["o"]] = turned(so[...])
+    WA[own_weights, col["co"]] = turned(co[...])
+    E[block_rows(place.here, enc), :] = encoded[...]
+    plane_rows = block_rows(place.plane, tok)
+    GR[plane_rows, :] = out_grad[...].astype(LOW)
+    gx.pass_level()
+    down_t = turned(down_w[...])
+    for p in range(4):
+        cols = slice(p * quarter, (p + 1) * quarter)
+        base = p * size.part
+        wm[:, base : base + quarter] = gate_w[:, cols]
+        wm[:, base + quarter : base + 2 * quarter] = up_w[:, cols]
+        wm[:, base + 2 * quarter : base + 3 * quarter] = down_t[:, cols]
+    WM[own_weights, :] = wm[:, my_part]
+    bucket_rows(buckets, order, place.here, table_rows, ids)
+    bias_vectors(ids, table, bias)
+    diag[...] = jnp.zeros_like(diag)
+    gx.pass_near()
+    gs.pass_level()
+    for k, chip in enumerate(plane_chips):
+        wire.send(
+            wm.at[:, pl.ds(aligned(lax.rem(chip, 4) * size.part, 128), size.part)],
+            WM.at[own_weights, :],
+            mg_plane + k,
+            chip,
+        )
+    gs.pass_near()
+    go.start()
+    ge.start()
+    gx.finish()
+    gx.finish_share()
+    gc_.start()
+    go.pass_level()
+    ge.pass_level()
+    gs.finish()
+
+    def project(rows_):
+        kv[rows_, :] = dot(X[rows_, :], WA[:, col["kv"]]).astype(LOW)
+
+    def project_enc(rows_):
+        mkv[rows_, :] = dot(E[rows_, :], WA[:, col["ckv"]]).astype(LOW)
+
+    q[...] = dot(X[here_rows, :], WA[:, col["q"]]).astype(LOW)
+    rows_loop(ctx_tok, 256, project)
+
+    def during_self(j):
+        if j == 0:
+            go.pass_near()
+            ge.pass_near()
+            gc_.pass_level()
+        elif j == 1:
+            gp.start()
+            for k, chip in enumerate(plane_chips):
+                wire.got(WM.at[block_rows(chip, rows), :], mg_plane + k)
+            own = WM.at[block_rows(place.level, 4 * rows), :]
+            for k in (1, 2, 3):
+                wire.send(own, own, mg_level + k - 1, place.above[k])
+            go.finish()
+        else:
+            ge.finish()
+
+    pair_attend(tok, size.pairs, 512, q, kv, s, e1, rl1, mixed1, bias, during_self)
+    part = dot_nt(mixed1[...], WA[:, col["o"]])
+    gc_.pass_near()
+    gp.pass_level()
+    gg.start()
+    after_self[...] = layer_in[...] + core_sum(wire, part, ca.at[0], cb.at[0])
+    n2[...] = rms_forward(after_self[...], gains[1:2]).astype(LOW)
+    ge.finish_share()
+    gp.pass_near()
+    gc_.finish()
+
+    rows_loop(ctx_enc, 256, project_enc)
+    probes[...] = dot(n2[...], WA[:, col["cq"]]).astype(LOW)
+
+    def during_cross(j):
+        if j == 1:
+            for k in (1, 2, 3):
+                gg.share(k)
+
+    pair_attend(tok, size.pairs, 512, probes, mkv, s, e2, rl2, mixed2, None, during_cross)
+    gp.finish()
+    part = dot_nt(mixed2[...], WA[:, col["co"]])
+    after_cross[...] = after_self[...] + core_sum(wire, part, ca.at[1], cb.at[1])
+
+    N3[plane_rows, :] = rms_forward(after_cross[...], gains[2:3]).astype(LOW)
+    spread.start()
+    for k in (1, 2, 3):
+        level = place.below[k] // 4
+        wire.got(WM.at[block_rows(level, 4 * rows), :], mg_level + k - 1)
+
+    def units(k):
+        rows_ = spread_rows(k)
+        pre = dot(N3[rows_, :], WM[:, : 2 * quarter])
+        gate, upper = pre[:, :quarter], pre[:, quarter:]
+        value, slope = gelu_parts(gate)
+        act[rows_, :] = (value * upper).astype(LOW)
+        grad = dot(GR[rows_, :], WM[:, 2 * quarter :])
+        GU[rows_, :quarter] = (grad * upper * slope).astype(LOW)
+        GU[rows_, quarter:] = (grad * value).astype(LOW)
+        PN[rows_, :] = dot_nt(GU[rows_, :], WM[:, : 2 * quarter]).astype(LOW)
+
+    def spread_rows(k):
+        return sum_n.rows(k)
+
+    for k in (1, 2, 3):
+        gg.finish(k)
+    units(0)
+    sum_n.start(0)
+    spread.share(1)
+    spread.share(2)
+    spread.finish(1)
+    units(1)
+    sum_n.start(1)
+    spread.share(3)
+    spread.finish(2)
+    units(2)
+    sum_n.start(2)
+    sum_n.middle(1)
+    spread.finish(3)
+    units(3)
+    sum_n.start(3)
+    sum_n.middle(2)
+
+    def back_out(k):
+        rows_ = spread_rows(k)
+        PO[rows_, :] = dot_nt(act[rows_, :], WM[:, 2 * quarter :]).astype(LOW)
+
+    def unit_grads(cols):
+        PM[cols, : 2 * quarter] = dot_tn(N3[:, cols], GU[...]).astype(LOW)
+        PM[cols, 2 * quarter :] = dot_tn(GR[:, cols], act[...]).astype(LOW)
+
+    back_out(0)
+    sum_n.middle(3)
+    sum_n.middle(0)
+    rows_loop(model, 128, unit_grads)
+    for k in (1, 2, 3):
+        wire.send(
+            PM.at[block_rows(place.above[k] // 4, 4 * rows), :],
+            ml.at[k - 1],
+            ms_level + k - 1,
+            place.above[k],
+        )
+    sum_n.finish()
+    for k in (1, 2, 3):
+        back_out(k)
+    for k in range(4):
+        sum_o.start(k)
+    sum_n.finish_core()
+    extra, gain_three = rms_backward(after_cross[...], gains[2:3], pn_whole[...].astype(F32))
+    cross_grad[...] = out_grad[...] + extra
+    low[...] = cross_grad[...].astype(LOW)
+    mixed_grad[...] = dot(low[...], WA[:, col["co"]]).astype(LOW)
+    for k in (1, 2, 3, 0):
+        sum_o.middle(k)
+
+    def out_grads(left, right, target):
+        def body(cols):
+            PW[cols, target] = dot_tn(left[:, cols], right[...]).astype(LOW)
+
+        rows_loop(model, 128, body)
+
+    def weight_stream(name, *bufs):
+        def out(half, total):
+            first, last = size.cuts[name][half]
+            WG[:, first:last] = total
+
+        return Scatter(wire, weight_view(PW, name), lambda half: bufs[half], out)
+
+    def token_out(ref, count):
+        def out(half, total):
+            ref[half * (count // 2) : (half + 1) * (count // 2), mine] = total
+
+        return out
+
+    sp = weight_stream("co", bp0, bp1)
+    so_ = weight_stream("o", bo0, bo1)
+    sc = weight_stream("c", bc0, bc1)
+    sw = weight_stream("s", bs0, bs1)
+    sx = Scatter(wire, token_view(XG, tok, place.core), lambda half: bx.at[half], token_out(NG, tok))
+    se = Scatter(wire, token_view(EG, enc, place.core), lambda half: be.at[half], token_out(NE, enc))
+    x_base, e_base = wire.slots(4), wire.slots(4)
+
+    def pair_start(ref, recv, count, base, k):
+        at = block_rows(place.below[k] // 4, 4 * count)
+        wire.swap(ref.at[at, away], recv.at[at, :], base + k)
+
+    def pair_ready(ref, recv, count, base, k):
+        at = block_rows(place.below[k] // 4, 4 * count)
+        wire.got(recv.at[at, :], base + k)
+        ref[at, mine] = (ref[at, mine].astype(F32) + recv[at, :].astype(F32)).astype(LOW)
+
+    out_grads(low, mixed2, col["co"])
+    sp.start()
+    back = PairBack(
+        tok, size.pairs, probes, mkv, e2, rl2, mixed2, mixed_grad, mkv_grad, None, qc, gc, dl, dq
+    )
+    for c in range(ctx_enc // 512):
+        back.chunk(c * 512, 512)
+    back.finish(q_grad)
+    part = dot_nt(q_grad[...], WA[:, col["cq"]])
+    slot = wire.slots(1)
+    ca[2] = part.astype(LOW)
+    wire.swap(ca.at[2], cb.at[2], slot)
+    sp.pass_near()
+
+    def enc_rows(rows_):
+        EG[rows_, :] = dot_nt(mkv_grad[rows_, :], WA[:, col["ckv"]]).astype(LOW)
+
+    rows_loop(ctx_enc, 256, enc_rows)
+    for k in (1, 2, 3, 0):
+        pair_start(EG, pe, enc, e_base, k)
+    wire.got(cb.at[2], slot)
+    n_grad = ca[2].astype(F32) + cb[2].astype(F32)
+    extra, gain_two = rms_backward(after_self[...], gains[1:2], n_grad)
+    self_grad[...] = cross_grad[...] + extra
+    low[...] = self_grad[...].astype(LOW)
+    mixed_grad[...] = dot(low[...], WA[:, col["o"]]).astype(LOW)
+    out_grads(n2, q_grad, col["cq"])
+    out_grads(E, mkv_grad, col["ckv"])
+    sc.start()
+    for k in (1, 2, 3, 0):
+        pair_ready(EG, pe, enc, e_base, k)
+        se.start((k,))
+    out_grads(low, mixed1, col["o"])
+    so_.start()
+    sp.pass_level()
+
+    back = PairBack(
+        tok, size.pairs, q, kv, e1, rl1, mixed1, mixed_grad, kv_grad, diag, qc, gc, dl, dq
+    )
+
+    def tok_rows(k):
+        for part_ in range(2):
+            at = pl.ds(aligned(place.below[k] // 4 * 4 * tok + part_ * 2 * tok, 16), 2 * tok)
+            XG[at, :] = dot_nt(kv_grad[at, :], WA[:, col["kv"]]).astype(LOW)
+
+    n2[...] = X[here_rows, :]
+    back.chunk(place.below[1] // 4 * 4 * tok, 4 * tok)
+    tok_rows(1)
+    pair_start(XG, px, tok, x_base, 1)
+    sc.pass_near()
+    back.chunk(place.below[2] // 4 * 4 * tok, 4 * tok)
+    tok_rows(2)
+    pair_start(XG, px, tok, x_base, 2)
+    pair_ready(XG, px, tok, x_base, 1)
+    sx.start((1,))
+    se.pass_near()
+    back.chunk(place.below[3] // 4 * 4 * tok, 4 * tok)
+    tok_rows(3)
+    pair_start(XG, px, tok, x_base, 3)
+    pair_ready(XG, px, tok, x_base, 2)
+    sx.start((2,))
+    so_.pass_near()
+    back.chunk(place.level * 4 * tok, 4 * tok)
+    back.finish(q_grad)
+    tok_rows(0)
+    own = dot_nt(q_grad[...], WA[:, col["q"]]) + XG[here_rows, :].astype(F32)
+    XG[here_rows, :] = own.astype(LOW)
+    pair_start(XG, px, tok, x_base, 0)
+    pair_ready(XG, px, tok, x_base, 3)
+    sx.start((3,))
+    out_grads(n2, q_grad, col["q"])
+    pair_ready(XG, px, tok, x_base, 0)
+    sx.start((0,))
+    out_grads(X, kv_grad, col["kv"])
+    sw.start()
+
+    sc.pass_level()
+    se.pass_level()
+    so_.pass_level()
+    total = PM[block_rows(place.level, 4 * rows), :].astype(F32)
+    for k in (1, 2, 3):
+        wire.got(ml.at[k - 1], ms_level + k - 1)
+        total = total + ml[k - 1].astype(F32)
+    ps[...] = total.astype(LOW)
+    for k, chip in enumerate(plane_chips):
+        wire.send(
+            ps.at[block_rows(lax.rem(chip, 4), rows), :], mb.at[:, my_part], ms_plane + k, chip
+        )
+    mb[:, my_part] = ps[block_rows(place.plane, rows), :]
+    sx.pass_near()
+    sums = bucket_sums(ids, diag, table.shape[0])
+    t1[...] = jnp.concatenate(
+        (sums, jnp.zeros((sums.shape[0], t1.shape[1] - sums.shape[1]), F32)), axis=1
+    )
+    sx.pass_level()
+    sw.pass_near()
+    sx.finish()
+    x_slot, e_slot, o_slot = wire.slots(1), wire.slots(1), wire.slots(1)
+    wire.swap(NG.at[:, mine], NG.at[:, mine], x_slot)
+    se.finish()
+    wire.swap(NE.at[:, mine], NE.at[:, mine], e_slot)
+    sum_o.finish()
+    sw.pass_level()
+    wire.got(NG.at[:, away], x_slot)
+    extra, gain_one = rms_backward(layer_in[...], gains[0:1], NG[...])
+    input_grad[...] = self_grad[...] + extra
+    s1[...] = jnp.concatenate(
+        (gain_one, gain_two, gain_three, jnp.zeros((5, model), F32)), axis=0
+    )
+    small = wire.slots(10)
+    wire.send(s1, sr.at[0], small, place.fx)
+    wire.send(t1, tr.at[0], small + 5, place.fx)
+    sum_o.finish_core()
+    layer_out[...] = after_cross[...] + po_whole[...].astype(F32)
+    wire.got(NE.at[:, away], e_slot)
+    enc_grad[...] = NE[...]
+    wire.got(sr.at[0], small)
+    wire.got(tr.at[0], small + 5)
+    s2[...] = s1[...] + sr[0]
+    t2[...] = t1[...] + tr[0]
+    wire.send(s2, sr.at[1], small + 1, place.fy)
+    wire.send(t2, tr.at[1], small + 6, place.fy)
+    sp.finish()
+    sc.finish()
+    so_.finish()
+    wire.got(sr.at[1], small + 1)
+    wire.got(tr.at[1], small + 6)
+    sl[pl.ds(place.level, 1)] = (s2[...] + sr[1])[None]
+    tl[pl.ds(place.level, 1)] = (t2[...] + tr[1])[None]
+    for k in (1, 2, 3):
+        wire.send(sl.at[place.level], sl.at[place.level], small + 1 + k, place.above[k])
+        wire.send(tl.at[place.level], tl.at[place.level], small + 6 + k, place.above[k])
+    sw.finish()
+    for k, chip in enumerate(plane_chips):
+        cols = pl.ds(aligned(lax.rem(chip, 4) * size.part, 128), size.part)
+        wire.got(mb.at[:, cols], ms_plane + k)
+    for k in (1, 2, 3):
+        level = place.below[k] // 4
+        wire.got(sl.at[level], small + 1 + k)
+        wire.got(tl.at[level], small + 6 + k)
+    totals[...] = (sl[0] + sl[1]) + (sl[2] + sl[3])
+    bias_totals[...] = (tl[0] + tl[1]) + (tl[2] + tl[3])
+    wire.drain()
+
+
+def quick_device(
+    layer_in, encoded, self_query, self_key, self_value, self_out, cross_query, cross_key,
+    cross_value, cross_out, gate_proj, up_proj, down_proj, norm_gains, position_bias,
+    bucket_ids, block_order, out_grad,
+):
+    tok, model = layer_in.shape
+    enc = encoded.shape[0]
+    wide, units = self_query.shape[1], gate_proj.shape[1]
+    ctx = block_order.shape[0]
+    buckets, heads = position_bias.shape
+    size = Sizes(ctx, tok, enc, model, wide, units)
+    rows, quarter, pairs = size.rows, size.quarter, size.pairs
+    tok_all, enc_all, tok4 = ctx * tok, ctx * enc, 4 * tok
+
+    def vmem(*shape, dtype=LOW):
+        return pltpu.VMEM(shape, dtype)
+
+    def full(*shape):
+        return pltpu.VMEM(shape, F32)
+
+    def streams(name):
+        return [vmem(15, rows, last - first) for first, last in size.cuts[name]]
+
+    ins = {
+        "layer_in": layer_in, "encoded": encoded, "sq": self_query, "sk": self_key,
+        "sv": self_value, "so": self_out, "cq": cross_query, "ck": cross_key,
+        "cv": cross_value, "co": cross_out, "gate_w": gate_proj, "up_w": up_proj,
+        "down_w": down_proj, "gains": norm_gains, "table": position_bias,
+        "buckets": bucket_ids.reshape(ctx, tok), "order": block_order, "out_grad": out_grad,
+    }
+    outs = {
+        "layer_out": ((tok, model), F32), "input_grad": ((tok, model), F32),
+        "enc_grad": ((enc, model), F32), "WG": ((rows, size.attn_cols), F32),
+        "mb": ((rows, size.mlp_cols), LOW), "totals": ((8, model), F32),
+        "bias_totals": ((buckets, 128), F32),
+    }
+    (bs0, bs1), (bc0, bc1) = streams("s"), streams("c")
+    (bo0, bo1), (bp0, bp1) = streams("o"), streams("co")
+    scratch = {
+        "WA": vmem(model, size.attn_cols), "WM": vmem(model, size.part),
+        "wm": vmem(rows, size.mlp_cols), "X": vmem(tok_all, model), "E": vmem(enc_all, model),
+        "GR": vmem(tok4, model), "PW": vmem(model, size.attn_cols),
+        "PM": vmem(model, size.part),
+        "q": vmem(tok, wide), "kv": vmem(tok_all, 2 * wide), "mkv": vmem(enc_all, 2 * wide),
+        "probes": vmem(tok, wide), "s": full(2 * tok, tok_all),
+        "e1": vmem(pairs, 2 * tok, tok_all), "e2": vmem(pairs, 2 * tok, enc_all),
+        "rl1": full(pairs, 2 * tok, 1), "rl2": full(pairs, 2 * tok, 1),
+        "mixed1": vmem(tok, wide), "mixed2": vmem(tok, wide), "table_rows": full(2 * ctx, tok),
+        "ids": full(ctx, 2 * tok), "bias": full(ctx, 8, 2 * tok), "diag": full(ctx, 8, 2 * tok),
+        "after_self": full(tok, model), "after_cross": full(tok, model),
+        "cross_grad": full(tok, model), "self_grad": full(tok, model), "n2": vmem(tok, model),
+        "N3": vmem(tok4, model), "act": vmem(tok4, quarter), "GU": vmem(tok4, 2 * quarter),
+        "PN": vmem(tok4, model), "PO": vmem(tok4, model), "low": vmem(tok, model),
+        "mixed_grad": vmem(tok, wide), "q_grad": vmem(tok, wide),
+        "kv_grad": vmem(tok_all, 2 * wide), "mkv_grad": vmem(enc_all, 2 * wide),
+        "ca": vmem(3, tok, model), "cb": vmem(3, tok, model),
+        "pn_core": vmem(tok4, model // 2), "pn_plane": vmem(3, tok, model // 2),
+        "pn_whole": vmem(tok, model), "po_core": vmem(tok4, model // 2),
+        "po_plane": vmem(3, tok, model // 2), "po_whole": vmem(tok, model),
+        "qc": vmem(pairs, 2 * tok, 128), "gc": vmem(pairs, 2 * tok, 128),
+        "dl": full(pairs, 2 * tok, 1), "dq": full(pairs, 2 * tok, 128),
+        "bs0": bs0, "bs1": bs1, "bc0": bc0, "bc1": bc1, "bo0": bo0, "bo1": bo1,
+        "bp0": bp0, "bp1": bp1, "bx": vmem(2, 15, tok // 2, model // 2),
+        "be": vmem(2, 15, enc // 2, model // 2), "px": vmem(tok_all, model // 2),
+        "pe": vmem(enc_all, model // 2), "NG": full(tok, model), "NE": full(enc, model),
+        "ml": vmem(3, 4 * rows, size.part), "ps": vmem(4 * rows, size.part),
+        "s1": full(8, model), "s2": full(8, model), "sr": full(2, 8, model),
+        "sl": full(4, 8, model), "t1": full(buckets, 128), "t2": full(buckets, 128),
+        "tr": full(2, buckets, 128), "tl": full(4, buckets, 128), **wire_sems(512),
+    }
+    names = list(ins) + list(outs) + list(scratch)
+    made = pl.pallas_call(
+        named(functools.partial(layer_kernel, size), names),
+        out_shape=tuple(jax.ShapeDtypeStruct(*spec) for spec in outs.values()),
+        in_specs=[
+            pl.BlockSpec(memory_space=pltpu.SMEM if name == "order" else pltpu.VMEM)
+            for name in ins
+        ],
+        out_specs=tuple(pl.BlockSpec(memory_space=pltpu.VMEM) for _ in outs),
+        scratch_shapes=list(scratch.values()),
+        compiler_params=pltpu.CompilerParams(
+            collective_id=1, has_side_effects=True, vmem_limit_bytes=VMEM_LIMIT
+        ),
+    )(*ins.values())
+    layer_out, input_grad, enc_grad, wg, mg, totals, bias_totals = made
+    grads = {name: wg[:, size.col[name]] for name in size.names}
+    mlp = mg.reshape(rows, 4, 3, quarter)
+    gate, upward, down = (mlp[:, :, i].reshape(rows, units).astype(F32) for i in range(3))
+    return (
+        layer_out, input_grad, enc_grad, grads["q"], grads["k"], grads["v"], grads["o"].T,
+        grads["cq"], grads["ck"], grads["cv"], grads["co"].T, gate, upward, down.T,
+        totals[:3], bias_totals[:, :heads],
+    )
+
+
+def quick_fits(mesh):
+    return mesh.shape["ctx"] == 16 and mesh.shape["head"] == 2
 
 
 def as_sent(shard):
@@ -389,6 +1454,7 @@
 
 
 def solution(mesh):
+    body = quick_device if quick_fits(mesh) else per_device
     placed = (
         P("ctx", None),
         P("ctx", None),
@@ -410,7 +1476,7 @@
         P("ctx", None),
     )
     return jax.shard_map(
-        per_device,
+        body,
         mesh=mesh,
         in_specs=placed,
         out_specs=(

time: 2530 us -> 221 us (0.09)
  waiting for transfers between devices: 1750 us -> 0 us
  blocking collectives: 491 us -> 0 us
  Pallas kernels: 0 us -> 205 us
  matrix products: 126 us -> 0 us
  local copies, waits for them, and re-layouts: 103 us -> 12.8 us
  other arithmetic: 28.6 us -> 1.7 us
    reduce_scatter x11 -> x0, waiting for transfers between devices: 1260 us -> none  [the longest x1 149 us: per_device(): lax.psum_scatter(self_terms, 'ctx', scatter_dimension=0, tiled=True)]
    all_gather x10 -> x0, blocking collectives: 416 us -> none  [the longest x1 45.9 us: per_device(): lax.all_gather(self_key, 'ctx', axis=0, tiled=True)]
    unnamed x25 -> x0, waiting for transfers between devices: 261 us -> none
    pallas_call x0 -> x1, Pallas kernels: none -> 205 us  [quick_device(): pl.pallas_call(named(functools.partial(layer_kernel, size), names), out_s...]
    all_gather x5 -> x0, waiting for transfers between devices: 176 us -> none  [the longest x1 60.6 us: per_device(): lax.all_gather(up_proj, 'ctx', axis=0, tiled=True)]
    dot_general x87 -> x0, matrix products: 126 us -> none  [the longest x8 37 us: bias_scores(): jnp.einsum('qkb,bh->hqk', steps, rises, precision=HIGH)]
    psum x1 -> x0, blocking collectives: 75.2 us -> none  [per_device(): lax.psum((jnp.stack((gain_one, gain_two, gain_three)), bias_grad), 'ctx')]
    psum x5 -> x0, waiting for transfers between devices: 48.2 us -> none  [join_heads(): lax.psum(as_sent(parts), 'head')]
  transfers between devices with their start and end apart: 23 -> 0, of which waited for: 19 -> 0; matrix products, arithmetic and copies ran while one was open for 6% -> 0% of each run, Pallas kernels for 0% -> 0%
where the time goes in v2:
time: 221 us; the launch traced here: 220 us
  Pallas kernels  205 us (93%)
  local copies, waits for them, and re-layouts  12.8 us (6%)
    pallas_call x1, Pallas kernels, quick_device(): pl.pallas_call(named(functools.partial(layer_kernel, size), names), out_s...  205 us
    unnamed x29, local copies, waits for them, and re-layouts  9.77 us

profile of v2, /device:TPU:0, one launch (start us, length us, event | category | flops | bytes accessed | tf_op | source)
XLA Modules:
  0.0 220.1 jit_solution(12233701276040132239)
XLA Ops:
  0.6 0.0 copy-start.4
  0.7 1.7 copy.41.refs_12_
  2.4 0.0 copy-done.4
  2.4 0.0 copy-start.5
  2.4 0.7 copy.39.refs_5_
  3.1 0.0 copy-done.5
  3.2 0.0 copy-start.8
  3.2 0.7 copy.40.refs_9_
  3.9 0.0 copy-done.8
  3.9 0.7 copy.42.refs_14_
  4.6 205.0 %shard_map.297 = (f32[128,768]{1,0:T(8,128)}, f32[128,768]{1,0:T(8,128)}, f32[64,768]{1,0:T(8,128)}, f32[48,3072]{1,0:T(8,128)}, bf16[48,3072]{1,0:T(8,128)(2,1)}, /*index=5*/f32[8,768]{1,0:T(8,128)}, f32[32,128]{1,0:T(8,128)}) custom-call(f32[128,768]{1,0:T(8,128)} %refs_0_.1, bf16[64,768]{1,0:T(8,128)(2,1)} %refs_1_.1, bf16[48,384]{1,0:T(8,128)(2,1)} %refs_2_.1, ...), custom_call_target="tpu_custom_call" | custom-call | tf_op jit(solution)/shard_map/pallas_call | solution.py:1050
  209.6 0.0 copy-start.2
  209.6 2.0 slice_bitcast_fusion
  211.6 0.0 copy-done.2
  211.6 0.4 reshape.45
  212.0 1.7 fusion
  213.7 0.7 copy.46
  214.4 0.0 copy-start.1
  214.4 0.7 copy.44
  215.1 0.0 copy-start.7
  215.2 0.7 copy.45
  215.9 0.0 copy-start.6
  215.9 0.0 copy-done.7
  215.9 0.6 slice.50
  216.5 0.1 copy-done.6
  216.6 0.7 copy.43
  217.2 0.0 copy-done.1
  217.3 0.0 copy-start
  217.3 0.7 copy.50
  218.0 0.4 copy-done
  218.4 0.0 copy-start.3
  218.4 0.7 copy.51
  219.1 0.3 copy-done.3
  219.5 0.7 copy.52
Async XLA Ops:
  0.6 1.8 copy-start.4
  2.4 0.8 copy-start.5
  3.2 0.8 copy-start.8
  209.6 2.0 copy-start.2
  214.4 2.8 %copy-start.1 = (f32[128,768]{1,0:T(8,128)S(1)}, f32[128,768]{1,0:T(8,128)}, u32[]{:S(2)}) copy-start(f32[128,768]{1,0:T(8,128)} %get-tuple-element.89) | copy-start | bytes 1179652
  215.1 0.7 copy-start.7
  215.9 0.7 copy-start.6
  217.3 1.1 copy-start
  218.4 1.1 copy-start.3

commit v3 on v2

--- a/solution.py
+++ b/solution.py
@@ -59,6 +59,13 @@
         self.fxy = self.flip(self.fx, 1)
         self.above = [lax.rem(self.here + 4 * k, count) for k in range(4)]
         self.below = [lax.rem(self.here + count - 4 * k, count) for k in range(4)]
+        self.top = count // 4 - 1
+        bottom, head = self.level == 0, self.level == self.top
+        self.nearest = (
+            jnp.where(bottom, 3, 1),
+            jnp.where(bottom, 2, jnp.where(head, 2, 3)),
+            jnp.where(bottom, 1, jnp.where(head, 3, 2)),
+        )
 
     def flip(self, index, axis):
         if axis == 0:
@@ -68,140 +75,191 @@
     def near(self, half):
         return (self.fx, self.fy) if half == 0 else (self.fy, self.fx)
 
-    def greet(self, chips, partner):
+    def signal(self, chips):
         barrier = pltpu.get_barrier_semaphore()
-        total = len(chips) + (1 if partner else 0)
         for chip in chips:
             pl.semaphore_signal(
                 barrier, inc=1, device_id=(chip, self.core), device_id_type=MESH
             )
-        if partner:
-            pl.semaphore_signal(
-                barrier, inc=1, device_id=(self.here, self.other), device_id_type=MESH
-            )
-        pl.semaphore_wait(barrier, total)
+        pl.semaphore_signal(barrier, inc=1, device_id=(self.here, self.other), device_id_type=MESH)
+
+    def meet(self, count):
+        pl.semaphore_wait(pltpu.get_barrier_semaphore(), count)
 
 
 class Wire:
     def __init__(self, place, send_sem, recv_sem):
         self.place, self.send_sem, self.recv_sem = place, send_sem, recv_sem
-        self.sent = []
         self.used = 0
+        self.send_used = 0
+        self.pending = []
 
     def slots(self, count):
         base = self.used
         self.used += count
-        assert self.used <= self.send_sem.shape[0], self.used
+        assert self.used <= self.recv_sem.shape[0], self.used
         return base
 
-    def copy(self, src, dst, slot, chip, core):
+    def sender(self, whole=None):
+        slot = self.send_used
+        self.send_used += 1
+        assert slot < self.send_sem.shape[0], slot
+        if whole is not None:
+            self.pending.append((slot, whole))
+        return slot
+
+    def copy(self, src, dst, out, slot, chip, core):
         return pltpu.make_async_remote_copy(
             src_ref=src,
             dst_ref=dst,
-            send_sem=self.send_sem.at[slot],
+            send_sem=self.send_sem.at[out],
             recv_sem=self.recv_sem.at[slot],
             device_id=(chip, core),
             device_id_type=MESH,
         )
 
-    def send(self, src, dst, slot, chip=None, core=None):
+    def send(self, src, dst, slot, chip=None, core=None, out=None):
         chip = self.place.here if chip is None else chip
         core = self.place.core if core is None else core
-        made = self.copy(src, dst, slot, chip, core)
-        made.start()
-        self.sent.append(made)
-
-    def swap(self, src, dst, slot):
-        self.send(src, dst, slot, None, self.place.other)
+        if out is None:
+            out = self.sender(src)
+        self.copy(src, dst, out, slot, chip, core).start()
+
+    def swap(self, src, dst, slot, out=None):
+        self.send(src, dst, slot, None, self.place.other, out)
 
     def got(self, dst, slot):
         place = self.place
-        self.copy(dst, dst, slot, place.here, place.other).wait_recv()
+        self.copy(dst, dst, 0, slot, place.here, place.other).wait_recv()
+
+    def sent(self, whole, out):
+        place = self.place
+        self.copy(whole, whole, out, 0, place.here, place.other).wait_send()
 
     def drain(self):
-        for made in self.sent:
-            made.wait_send()
-        self.sent = []
+        for out, whole in self.pending:
+            self.sent(whole, out)
+        self.pending = []
 
 
 class Gather:
-    def __init__(self, wire, view, share, halves=2):
-        self.wire, self.view, self.share = wire, view, share
-        self.base = [wire.slots(15) for _ in range(halves)]
-        self.side = [wire.slots(16) for _ in range(halves)] if share else None
-        self.halves = range(halves)
+    def __init__(self, wire, view, share, spare):
+        self.wire, self.view, self.share, self.spare = wire, view, share, spare
+        self.halves = range(2)
+        self.base = [wire.slots(8) for _ in self.halves]
+        self.out = [wire.sender(spare(half, 12)) for half in self.halves]
+        self.line_out = [wire.sender() for _ in self.halves]
+        if share:
+            self.side = [wire.slots(1) for _ in self.halves]
+            self.side_out = [wire.sender(spare(half, 15)) for half in self.halves]
+
+    def _line(self, half, block, slot, chip):
+        ref = self.view(half, block)
+        self.wire.send(ref, ref, self.base[half] + slot, chip, out=self.line_out[half])
 
     def _out(self, half, block, slot, chip):
         ref = self.view(half, block)
-        self.wire.send(ref, ref, self.base[half] + slot, chip)
-
-    def _in(self, half, block, slot):
-        self.wire.got(self.view(half, block), self.base[half] + slot)
+        self.wire.send(ref, ref, self.base[half] + slot, chip, out=self.out[half])
+
+    def _give(self, half, block):
         if self.share:
             ref = self.view(half, block)
-            self.wire.swap(ref, ref, self.side[half] + slot)
-
-    def start(self):
+            self.wire.swap(ref, ref, self.side[half], self.side_out[half])
+
+    def start_level(self):
+        place = self.wire.place
+        for half in self.halves:
+
+            @pl.when(place.level < place.top)
+            def _():
+                self._line(half, place.here, 0, place.here + 4)
+
+            @pl.when(place.level > 0)
+            def _():
+                self._line(half, place.here, 2, place.here - 4)
+
+    def start_plane(self):
         place = self.wire.place
         for half in self.halves:
             near, far = place.near(half)
-            for k in (1, 2, 3):
-                self._out(half, place.here, k - 1, place.above[k])
             self._out(half, place.here, 3, near)
             self._out(half, place.here, 7, far)
 
-    def pass_level(self):
+    def pass_level(self, steps=(0, 1, 2)):
         place = self.wire.place
-        for k in (1, 2, 3):
+        for step in steps:
+            k = place.nearest[step]
+            block = lax.rem(place.here + place.count - 4 * k, place.count)
+            rising = place.level >= k
+            onward = jnp.where(rising, place.level < place.top, place.level > 0)
+            chip = jnp.where(rising, place.here + 4, place.here - 4)
+            slot = jnp.where(rising, k, k - 2)
             for half in self.halves:
                 near, far = place.near(half)
-                self._in(half, place.below[k], k - 1)
-                self._out(half, place.below[k], 3 + k, near)
-                self._out(half, place.below[k], 7 + k, far)
-
-    def pass_near(self):
+                self.wire.got(self.view(half, block), self.base[half] + k - 1)
+
+                @pl.when(onward)
+                def _():
+                    self._line(half, block, slot, chip)
+
+                self._out(half, block, 3 + k, near)
+                self._out(half, block, 7, far)
+                self._give(half, block)
+
+    def pass_near(self, steps=(0, 1, 2, 3)):
         place = self.wire.place
-        for k in range(4):
+        for step in steps:
+            k = (0, *place.nearest)[step]
             for half in self.halves:
                 _, far = place.near(half)
-                block = place.flip(place.below[k], half)
-                self._in(half, block, 3 + k)
-                self._out(half, block, 11 + k, far)
+                block = lax.rem(place.here + place.count - 4 * k, place.count)
+                block = place.flip(block, half)
+                self.wire.got(self.view(half, block), self.base[half] + 3 + k)
+                self._out(half, block, 7, far)
+                self._give(half, block)
 
     def finish(self):
         place = self.wire.place
-        for k in range(4):
-            for half in self.halves:
-                block = place.flip(place.below[k], 1 - half)
-                self._in(half, block, 7 + k)
-                self._in(half, place.flip(block, half), 11 + k)
+        for half in self.halves:
+            self.wire.got(self.spare(half, 8), self.base[half] + 7)
+            if self.share:
+                for k in range(4):
+                    block = place.flip(place.below[k], 1 - half)
+                    self._give(half, block)
+                    self._give(half, place.flip(block, half))
 
     def finish_share(self):
-        if not self.share:
-            return
+        for half in self.halves:
+            self.wire.got(self.spare(half, 15), self.side[half])
+
+    def drain(self):
         place = self.wire.place
-        for k in range(4):
-            for half in self.halves:
-                block = place.below[k]
-                if k:
-                    self._share_in(half, block, k - 1)
-                self._share_in(half, place.flip(block, half), 3 + k)
-                block = place.flip(block, 1 - half)
-                self._share_in(half, block, 7 + k)
-                self._share_in(half, place.flip(block, half), 11 + k)
-
-    def _share_in(self, half, block, slot):
-        self.wire.got(self.share(half, block), self.side[half] + slot)
+        for half in self.halves:
+
+            @pl.when(jnp.logical_or(place.level == 0, place.level == place.top))
+            def _():
+                self.wire.sent(self.spare(half, 1), self.line_out[half])
+
+            @pl.when(jnp.logical_and(place.level > 0, place.level < place.top))
+            def _():
+                self.wire.sent(self.spare(half, 5), self.line_out[half])
 
 
 class Scatter:
-    def __init__(self, wire, view, buf, out, halves=2):
-        self.wire, self.view, self.out = wire, view, out
-        self.far_buf = lambda half, slot: buf(half).at[slot]
-        self.near_buf = lambda half, slot: buf(half).at[8 + slot]
-        self.level_buf = lambda half, slot: buf(half).at[12 + slot]
-        self.base = [wire.slots(15) for _ in range(halves)]
-        self.halves = range(halves)
+    def __init__(self, wire, view, buf, out):
+        self.wire, self.view, self.buf, self.out = wire, view, buf, out
+        self.halves = range(2)
+        self.base = [wire.slots(13) for _ in self.halves]
+        self.send_slot = [wire.sender(buf(half)) for half in self.halves]
+
+    def _send(self, half, block, place_in, slot, chip):
+        self.wire.send(
+            self.view(half, block),
+            self.buf(half).at[place_in],
+            self.base[half] + slot,
+            chip,
+            out=self.send_slot[half],
+        )
 
     def start(self, levels=(1, 2, 3, 0)):
         place = self.wire.place
@@ -210,58 +268,42 @@
                 _, far = place.near(half)
                 away = place.flip(place.below[k], 1 - half)
                 for pair, block in ((1, place.flip(away, half)), (0, away)):
-                    slot = 2 * k + pair
-                    self.wire.send(
-                        self.view(half, block),
-                        self.far_buf(half, slot),
-                        self.base[half] + slot,
-                        far,
-                    )
-
-    def pass_near(self):
+                    self._send(half, block, 2 * k + pair, 2 * k + pair, far)
+
+    def pass_near(self, levels=(1, 2, 3, 0)):
         place = self.wire.place
-        for k in (1, 2, 3, 0):
+        for k in levels:
             for half in self.halves:
                 near, _ = place.near(half)
                 block = place.flip(place.below[k], half)
                 slot = 2 * k + 1
-                self.wire.got(self.far_buf(half, slot), self.base[half] + slot)
+                self.wire.got(self.buf(half).at[slot], self.base[half] + slot)
                 ref = self.view(half, block)
-                ref[...] = (
-                    ref[...].astype(F32) + self.far_buf(half, slot)[...].astype(F32)
-                ).astype(LOW)
-                self.wire.send(ref, self.near_buf(half, k), self.base[half] + 8 + k, near)
-
-    def pass_level(self):
+                ref[...] = (ref[...].astype(F32) + self.buf(half)[slot].astype(F32)).astype(LOW)
+                self._send(half, block, 8 + k, 8 + k, near)
+
+    def pass_level(self, levels=(1, 2, 3)):
         place = self.wire.place
-        for k in (1, 2, 3):
+        for k in levels:
             for half in self.halves:
-                self._add(half, k)
                 ref = self.view(half, place.below[k])
-                self.wire.send(
-                    ref, self.level_buf(half, k - 1), self.base[half] + 11 + k, place.below[k]
-                )
-
-    def _add(self, half, k):
-        place = self.wire.place
-        self.wire.got(self.far_buf(half, 2 * k), self.base[half] + 2 * k)
-        self.wire.got(self.near_buf(half, k), self.base[half] + 8 + k)
-        ref = self.view(half, place.below[k])
-        total = (
-            ref[...].astype(F32)
-            + self.far_buf(half, 2 * k)[...].astype(F32)
-            + self.near_buf(half, k)[...].astype(F32)
-        )
-        if k:
-            ref[...] = total.astype(LOW)
-        return total
+                ref[...] = self._sum(half, k).astype(LOW)
+                self._send(half, place.below[k], 11 + k, 12, place.below[k])
+
+    def _sum(self, half, k):
+        place, buf = self.wire.place, self.buf(half)
+        self.wire.got(buf.at[2 * k], self.base[half] + 2 * k)
+        self.wire.got(buf.at[8 + k], self.base[half] + 8 + k)
+        total = self.view(half, place.below[k])[...].astype(F32)
+        return total + buf[2 * k].astype(F32) + buf[8 + k].astype(F32)
 
     def finish(self):
         for half in self.halves:
-            total = self._add(half, 0)
+            buf = self.buf(half)
+            total = self._sum(half, 0)
+            self.wire.got(buf.at[12:15], self.base[half] + 12)
             for k in (1, 2, 3):
-                self.wire.got(self.level_buf(half, k - 1), self.base[half] + 11 + k)
-                total = total + self.level_buf(half, k - 1)[...].astype(F32)
+                total = total + buf[11 + k].astype(F32)
             self.out(half, total)
 
 
@@ -295,7 +337,8 @@
                 for half in range(2):
                     row = []
                     for b in range(chunk // tok):
-                        vec = bias_ref[c * (chunk // tok) + b, 2 * j + half : 2 * j + half + 1, :]
+                        lanes = pl.ds(aligned((c * (chunk // tok) + b) * 2 * tok, 128), 2 * tok)
+                        vec = bias_ref[2 * j + half : 2 * j + half + 1, lanes]
                         wide = jnp.broadcast_to(vec, (tok, 2 * tok))
                         row.append(pltpu.roll(wide, 0, 1, stride=1, stride_axis=0)[:, :tok])
                     tiles.append(jnp.concatenate(row, axis=1))
@@ -363,7 +406,8 @@
                         tile = turned[:, b * tok : (b + 1) * tok]
                         wide = jnp.concatenate((tile, jnp.zeros_like(tile)), axis=1)
                         wide = pltpu.roll(wide, tok + 1, 1, stride=1, stride_axis=0)
-                        self.diag[start // tok + b, pl.ds(2 * j + half, 1), :] = jnp.sum(
+                        lanes = pl.ds(aligned(2 * start + b * 2 * tok, 128), 2 * tok)
+                        self.diag[pl.ds(2 * j + half, 1), lanes] = jnp.sum(
                             wide, axis=0, keepdims=True
                         )
             self.kv_grad[rows, cols] = dot_tn(ds, qc[j]).astype(LOW)
@@ -388,43 +432,30 @@
     table_rows[:count, :] = jnp.full((count, tok), -1.0, F32)
     table_rows[count:, :] = dot(buckets_ref[...].astype(LOW), turn)
     own = order_ref[here]
-
-    def one(block, carry):
+    for block in range(count):
         at = own - order_ref[block] + count
         wide = jnp.concatenate(
             (table_rows[pl.ds(at - 1, 1), :], table_rows[pl.ds(at, 1), :]), axis=1
         )
-        ids_ref[pl.ds(block, 1), :] = pltpu.roll(wide, 1, 1)
-        return carry
-
-    lax.fori_loop(0, count, one, 0)
-
-
-def bucket_masks(ids_ref, block, buckets):
-    ids = ids_ref[pl.ds(block, 1), :]
+        ids_ref[:, block * 2 * tok : (block + 1) * 2 * tok] = pltpu.roll(wide, 1, 1)
+
+
+def bucket_masks(ids_ref, buckets):
+    ids = ids_ref[...]
     row = lax.broadcasted_iota(jnp.int32, (buckets, ids.shape[1]), 0).astype(F32)
     return ids, (row == ids).astype(F32)
 
 
 def bias_vectors(ids_ref, table_ref, bias_ref):
-    buckets, heads = table_ref.shape
-
-    def one(block, carry):
-        ids, mask = bucket_masks(ids_ref, block, buckets)
-        vec = dot_tn(table_ref[...], mask, precision=HIGH)
-        bias_ref[block, :heads, :] = jnp.where(ids >= 0, vec, NEG)
-        return carry
-
-    lax.fori_loop(0, ids_ref.shape[0], one, 0)
+    heads, buckets = table_ref.shape
+    ids, mask = bucket_masks(ids_ref, buckets)
+    vec = dot(table_ref[...], mask, precision=HIGH)
+    bias_ref[:heads, :] = jnp.where(ids >= 0, vec, NEG)
 
 
 def bucket_sums(ids_ref, diag_ref, buckets):
-    def one(block, total):
-        _, mask = bucket_masks(ids_ref, block, buckets)
-        return total + dot_nt(mask, diag_ref[block], precision=HIGH)
-
-    start = jnp.zeros((buckets, diag_ref.shape[1]), F32)
-    return lax.fori_loop(0, ids_ref.shape[0], one, start)
+    _, mask = bucket_masks(ids_ref, buckets)
+    return dot_nt(diag_ref[...], mask, precision=HIGH)
 
 
 def rows_loop(count, step, body):
@@ -458,6 +489,7 @@
 class PlaneSum:
     def __init__(self, wire, tok, part, core_buf, plane_buf, whole):
         self.wire, self.tok = wire, tok
+        self.out = wire.sender(part)
         self.part, self.core_buf, self.plane_buf, self.whole = part, core_buf, plane_buf, whole
         self.base = wire.slots(8)
         self.half = whole.shape[1] // 2
@@ -473,7 +505,7 @@
     def start(self, k):
         away = self.cols(self.wire.place.other)
         rows = self.rows(k)
-        self.wire.swap(self.part.at[rows, away], self.core_buf.at[rows, :], self.base + k)
+        self.wire.swap(self.part.at[rows, away], self.core_buf.at[rows, :], self.base + k, self.out)
 
     def middle(self, k):
         wire, rows = self.wire, self.rows(k)
@@ -487,6 +519,7 @@
                 self.plane_buf.at[k - 1],
                 self.base + 3 + k,
                 self.chips[k],
+                out=self.out,
             )
 
     def finish(self):
@@ -497,7 +530,7 @@
             total = total + self.plane_buf[k - 1].astype(F32)
         mine = self.cols(place.core)
         self.whole[:, mine] = total.astype(LOW)
-        wire.swap(self.whole.at[:, mine], self.whole.at[:, mine], self.base + 7)
+        wire.swap(self.whole.at[:, mine], self.whole.at[:, mine], self.base + 7, self.out)
 
     def finish_core(self):
         self.wire.got(self.whole.at[:, self.cols(self.wire.place.other)], self.base + 7)
@@ -508,6 +541,7 @@
         self.wire, self.tok, self.ref = wire, tok, ref
         self.half = ref.shape[1] // 2
         self.base = wire.slots(8)
+        self.out = wire.sender(ref.at[: 3 * tok, :])
         place = wire.place
         self.chips = (place.here, place.fx, place.fy, place.fxy)
 
@@ -518,12 +552,12 @@
     def start(self):
         own = self.view(0, self.wire.place.core)
         for k in (1, 2, 3):
-            self.wire.send(own, own, self.base + k, self.chips[k])
+            self.wire.send(own, own, self.base + k, self.chips[k], out=self.out)
 
     def share(self, k):
         ref = self.view(k, self.wire.place.core)
         self.wire.got(ref, self.base + k)
-        self.wire.swap(ref, ref, self.base + 4 + k)
+        self.wire.swap(ref, ref, self.base + 4 + k, self.out)
 
     def finish(self, k):
         self.wire.got(self.view(k, self.wire.place.other), self.base + 4 + k)
@@ -564,20 +598,11 @@
     return body
 
 
-def wire_sems(count):
+def wire_sems(send, recv):
     return {
-        "send_sem": pltpu.SemaphoreType.DMA((count,)),
-        "recv_sem": pltpu.SemaphoreType.DMA((count,)),
+        "send_sem": pltpu.SemaphoreType.DMA((send,)),
+        "recv_sem": pltpu.SemaphoreType.DMA((recv,)),
     }
-
-
-def turned(block):
-    count = block.shape[1]
-    eye = (
-        lax.broadcasted_iota(jnp.int32, (count, count), 0)
-        == lax.broadcasted_iota(jnp.int32, (count, count), 1)
-    ).astype(LOW)
-    return dot_nt(eye, block).astype(LOW)
 
 
 def layer_kernel(
@@ -624,40 +649,83 @@
 
         return view
 
-    gx = Gather(wire, token_view(X, tok, place.core), token_view(X, tok, place.other))
-    ge = Gather(wire, token_view(E, enc, place.core), token_view(E, enc, place.other))
-    gs, gc_, go, gp = (Gather(wire, weight_view(WA, n), None) for n in ("s", "c", "o", "co"))
+    def token_spare(buf):
+        return lambda half, count: buf.at[half, 0:count]
+
+    def weight_spare(*bufs):
+        return lambda half, count: bufs[half].at[0:count]
+
+    def token_gather(ref, count, buf):
+        return Gather(
+            wire,
+            token_view(ref, count, place.core),
+            True,
+            token_spare(buf),
+        )
+
+    gx, ge = token_gather(X, tok, bx), token_gather(E, enc, be)
+    gs, gc_, go, gp = (
+        Gather(wire, weight_view(WA, name), False, weight_spare(*bufs))
+        for name, bufs in (("s", (bs0, bs1)), ("c", (bc0, bc1)), ("o", (bo0, bo1)), ("co", (bp0, bp1)))
+    )
     gg = PlaneGather(wire, tok, GR)
     spread = PlaneGather(wire, tok, N3)
     sum_n = PlaneSum(wire, tok, PN, pn_core, pn_plane, pn_whole)
     sum_o = PlaneSum(wire, tok, PO, po_core, po_plane, po_whole)
     mg_plane, mg_level, ms_level, ms_plane = (wire.slots(3) for _ in range(4))
 
-    place.greet(place.above[1:] + list(plane_chips), True)
+    place.signal(place.above[1:] + list(plane_chips))
     X[here_rows, :] = rms_forward(layer_in[...], gains[0:1]).astype(LOW)
-    gx.start()
-    for name, ref in zip(("q", "k", "v", "cq", "ck", "cv"), (sq, sk, sv, cq, ck, cv)):
+    for name, ref in zip(("q", "k", "v", "cq", "ck", "cv", "o", "co"), (sq, sk, sv, cq, ck, cv, so, co)):
         WA[own_weights, col[name]] = ref[...]
-    gs.start()
-    WA[own_weights, col["o"]] = turned(so[...])
-    WA[own_weights, col["co"]] = turned(co[...])
     E[block_rows(place.here, enc), :] = encoded[...]
+    place.meet(7)
+    gx.start_level()
+    gs.start_level()
+    gx.start_plane()
+    gs.start_plane()
     plane_rows = block_rows(place.plane, tok)
     GR[plane_rows, :] = out_grad[...].astype(LOW)
-    gx.pass_level()
-    down_t = turned(down_w[...])
     for p in range(4):
         cols = slice(p * quarter, (p + 1) * quarter)
-        base = p * size.part
-        wm[:, base : base + quarter] = gate_w[:, cols]
-        wm[:, base + quarter : base + 2 * quarter] = up_w[:, cols]
-        wm[:, base + 2 * quarter : base + 3 * quarter] = down_t[:, cols]
+        for i, ref in enumerate((gate_w, up_w, down_w)):
+            base = p * size.part + i * quarter
+            wm[:, base : base + quarter] = ref[:, cols]
     WM[own_weights, :] = wm[:, my_part]
+    gx.pass_near((0,))
+    gs.pass_near((0,))
+    gx.pass_level((0,))
+    gs.pass_level((0,))
+    gx.pass_level((1,))
+    gs.pass_level((1,))
+    gx.pass_near((1,))
+    gs.pass_near((1,))
+    gx.pass_level((2,))
+    go.start_level()
+    ge.start_level()
+    gs.pass_level((2,))
+    gc_.start_level()
+    gx.pass_near((2,))
+    gs.pass_near((2,))
+    gx.pass_near((3,))
+    gs.pass_near((3,))
+    go.start_plane()
+    ge.start_plane()
+    go.pass_level()
+    ge.pass_level()
+    go.pass_near((0,))
+    ge.pass_near((0,))
+    gc_.start_plane()
     bucket_rows(buckets, order, place.here, table_rows, ids)
     bias_vectors(ids, table, bias)
     diag[...] = jnp.zeros_like(diag)
-    gx.pass_near()
-    gs.pass_level()
+    gp.start_level()
+    gc_.pass_level((0, 1))
+    gx.finish()
+    gc_.pass_level((2,))
+    gp.start_plane()
+    gx.finish_share()
+    gs.finish()
     for k, chip in enumerate(plane_chips):
         wire.send(
             wm.at[:, pl.ds(aligned(lax.rem(chip, 4) * size.part, 128), size.part)],
@@ -665,15 +733,6 @@
             mg_plane + k,
             chip,
         )
-    gs.pass_near()
-    go.start()
-    ge.start()
-    gx.finish()
-    gx.finish_share()
-    gc_.start()
-    go.pass_level()
-    ge.pass_level()
-    gs.finish()
 
     def project(rows_):
         kv[rows_, :] = dot(X[rows_, :], WA[:, col["kv"]]).astype(LOW)
@@ -684,31 +743,30 @@
     q[...] = dot(X[here_rows, :], WA[:, col["q"]]).astype(LOW)
     rows_loop(ctx_tok, 256, project)
 
+    go.pass_near((1, 2, 3))
+    ge.pass_near((1, 2, 3))
+
     def during_self(j):
         if j == 0:
-            go.pass_near()
-            ge.pass_near()
-            gc_.pass_level()
+            gp.pass_level()
         elif j == 1:
-            gp.start()
+            gc_.pass_near()
             for k, chip in enumerate(plane_chips):
                 wire.got(WM.at[block_rows(chip, rows), :], mg_plane + k)
             own = WM.at[block_rows(place.level, 4 * rows), :]
             for k in (1, 2, 3):
                 wire.send(own, own, mg_level + k - 1, place.above[k])
-            go.finish()
         else:
-            ge.finish()
+            gg.start()
 
     pair_attend(tok, size.pairs, 512, q, kv, s, e1, rl1, mixed1, bias, during_self)
+    go.finish()
     part = dot_nt(mixed1[...], WA[:, col["o"]])
-    gc_.pass_near()
-    gp.pass_level()
-    gg.start()
     after_self[...] = layer_in[...] + core_sum(wire, part, ca.at[0], cb.at[0])
     n2[...] = rms_forward(after_self[...], gains[1:2]).astype(LOW)
+    gp.pass_near()
+    ge.finish()
     ge.finish_share()
-    gp.pass_near()
     gc_.finish()
 
     rows_loop(ctx_enc, 256, project_enc)
@@ -821,10 +879,11 @@
     sx = Scatter(wire, token_view(XG, tok, place.core), lambda half: bx.at[half], token_out(NG, tok))
     se = Scatter(wire, token_view(EG, enc, place.core), lambda half: be.at[half], token_out(NE, enc))
     x_base, e_base = wire.slots(4), wire.slots(4)
-
-    def pair_start(ref, recv, count, base, k):
+    x_out, e_out = wire.sender(px), wire.sender(pe)
+
+    def pair_start(ref, recv, count, base, k, out):
         at = block_rows(place.below[k] // 4, 4 * count)
-        wire.swap(ref.at[at, away], recv.at[at, :], base + k)
+        wire.swap(ref.at[at, away], recv.at[at, :], base + k, out)
 
     def pair_ready(ref, recv, count, base, k):
         at = block_rows(place.below[k] // 4, 4 * count)
@@ -844,28 +903,27 @@
     ca[2] = part.astype(LOW)
     wire.swap(ca.at[2], cb.at[2], slot)
     sp.pass_near()
+    out_grads(E, mkv_grad, col["ckv"])
+    out_grads(n2, q_grad, col["cq"])
+    sc.start()
 
     def enc_rows(rows_):
         EG[rows_, :] = dot_nt(mkv_grad[rows_, :], WA[:, col["ckv"]]).astype(LOW)
 
     rows_loop(ctx_enc, 256, enc_rows)
     for k in (1, 2, 3, 0):
-        pair_start(EG, pe, enc, e_base, k)
+        pair_start(EG, pe, enc, e_base, k, e_out)
     wire.got(cb.at[2], slot)
     n_grad = ca[2].astype(F32) + cb[2].astype(F32)
     extra, gain_two = rms_backward(after_self[...], gains[1:2], n_grad)
     self_grad[...] = cross_grad[...] + extra
     low[...] = self_grad[...].astype(LOW)
     mixed_grad[...] = dot(low[...], WA[:, col["o"]]).astype(LOW)
-    out_grads(n2, q_grad, col["cq"])
-    out_grads(E, mkv_grad, col["ckv"])
-    sc.start()
     for k in (1, 2, 3, 0):
         pair_ready(EG, pe, enc, e_base, k)
         se.start((k,))
     out_grads(low, mixed1, col["o"])
     so_.start()
-    sp.pass_level()
 
     back = PairBack(
         tok, size.pairs, q, kv, e1, rl1, mixed1, mixed_grad, kv_grad, diag, qc, gc, dl, dq
@@ -879,37 +937,39 @@
     n2[...] = X[here_rows, :]
     back.chunk(place.below[1] // 4 * 4 * tok, 4 * tok)
     tok_rows(1)
-    pair_start(XG, px, tok, x_base, 1)
-    sc.pass_near()
+    pair_start(XG, px, tok, x_base, 1, x_out)
+    sp.pass_level()
     back.chunk(place.below[2] // 4 * 4 * tok, 4 * tok)
     tok_rows(2)
-    pair_start(XG, px, tok, x_base, 2)
+    pair_start(XG, px, tok, x_base, 2, x_out)
     pair_ready(XG, px, tok, x_base, 1)
     sx.start((1,))
-    se.pass_near()
+    sc.pass_near()
     back.chunk(place.below[3] // 4 * 4 * tok, 4 * tok)
     tok_rows(3)
-    pair_start(XG, px, tok, x_base, 3)
+    pair_start(XG, px, tok, x_base, 3, x_out)
     pair_ready(XG, px, tok, x_base, 2)
     sx.start((2,))
-    so_.pass_near()
+    se.pass_near()
     back.chunk(place.level * 4 * tok, 4 * tok)
     back.finish(q_grad)
     tok_rows(0)
     own = dot_nt(q_grad[...], WA[:, col["q"]]) + XG[here_rows, :].astype(F32)
     XG[here_rows, :] = own.astype(LOW)
-    pair_start(XG, px, tok, x_base, 0)
+    pair_start(XG, px, tok, x_base, 0, x_out)
     pair_ready(XG, px, tok, x_base, 3)
     sx.start((3,))
+    so_.pass_near()
     out_grads(n2, q_grad, col["q"])
     pair_ready(XG, px, tok, x_base, 0)
     sx.start((0,))
     out_grads(X, kv_grad, col["kv"])
+    sx.pass_near((1, 2))
     sw.start()
 
     sc.pass_level()
+    sx.pass_near((3, 0))
     se.pass_level()
-    so_.pass_level()
     total = PM[block_rows(place.level, 4 * rows), :].astype(F32)
     for k in (1, 2, 3):
         wire.got(ml.at[k - 1], ms_level + k - 1)
@@ -920,19 +980,20 @@
             ps.at[block_rows(lax.rem(chip, 4), rows), :], mb.at[:, my_part], ms_plane + k, chip
         )
     mb[:, my_part] = ps[block_rows(place.plane, rows), :]
-    sx.pass_near()
-    sums = bucket_sums(ids, diag, table.shape[0])
+    sums = bucket_sums(ids, diag, table.shape[1])
     t1[...] = jnp.concatenate(
         (sums, jnp.zeros((sums.shape[0], t1.shape[1] - sums.shape[1]), F32)), axis=1
     )
+    so_.pass_level()
+    sw.pass_near((1, 2))
     sx.pass_level()
-    sw.pass_near()
+    sw.pass_near((3, 0))
+    sum_o.finish()
+    se.finish()
+    x_slot, e_slot = wire.slots(1), wire.slots(1)
+    wire.swap(NE.at[:, mine], NE.at[:, mine], e_slot)
     sx.finish()
-    x_slot, e_slot, o_slot = wire.slots(1), wire.slots(1), wire.slots(1)
     wire.swap(NG.at[:, mine], NG.at[:, mine], x_slot)
-    se.finish()
-    wire.swap(NE.at[:, mine], NE.at[:, mine], e_slot)
-    sum_o.finish()
     sw.pass_level()
     wire.got(NG.at[:, away], x_slot)
     extra, gain_one = rms_backward(layer_in[...], gains[0:1], NG[...])
@@ -973,7 +1034,25 @@
         wire.got(tl.at[level], small + 6 + k)
     totals[...] = (sl[0] + sl[1]) + (sl[2] + sl[3])
     bias_totals[...] = (tl[0] + tl[1]) + (tl[2] + tl[3])
+    for made in (gx, ge, gs, gc_, go, gp):
+        made.drain()
     wire.drain()
+
+
+def emit_kernel(size, layer_out, input_grad, enc_grad, WG, mb, totals, bias_totals, *outs):
+    for ref, out in zip((layer_out, input_grad, enc_grad), outs):
+        out[...] = ref[...]
+    for name, out in zip(size.names, outs[3:]):
+        out[...] = WG[:, size.col[name]]
+    for i, out in enumerate(outs[11:14]):
+        for p in range(4):
+            base = p * size.part + i * size.quarter
+            out[:, p * size.quarter : (p + 1) * size.quarter] = mb[
+                :, base : base + size.quarter
+            ].astype(F32)
+    outs[14][...] = totals[:3]
+    heads, buckets = outs[15].shape
+    outs[15][...] = bias_totals[:heads, :buckets]
 
 
 def quick_device(
@@ -1001,16 +1080,16 @@
 
     ins = {
         "layer_in": layer_in, "encoded": encoded, "sq": self_query, "sk": self_key,
-        "sv": self_value, "so": self_out, "cq": cross_query, "ck": cross_key,
-        "cv": cross_value, "co": cross_out, "gate_w": gate_proj, "up_w": up_proj,
-        "down_w": down_proj, "gains": norm_gains, "table": position_bias,
+        "sv": self_value, "so": self_out.T, "cq": cross_query, "ck": cross_key,
+        "cv": cross_value, "co": cross_out.T, "gate_w": gate_proj, "up_w": up_proj,
+        "down_w": down_proj.T, "gains": norm_gains, "table": position_bias.T,
         "buckets": bucket_ids.reshape(ctx, tok), "order": block_order, "out_grad": out_grad,
     }
     outs = {
         "layer_out": ((tok, model), F32), "input_grad": ((tok, model), F32),
         "enc_grad": ((enc, model), F32), "WG": ((rows, size.attn_cols), F32),
         "mb": ((rows, size.mlp_cols), LOW), "totals": ((8, model), F32),
-        "bias_totals": ((buckets, 128), F32),
+        "bias_totals": ((8, 128), F32),
     }
     (bs0, bs1), (bc0, bc1) = streams("s"), streams("c")
     (bo0, bo1), (bp0, bp1) = streams("o"), streams("co")
@@ -1024,7 +1103,7 @@
         "e1": vmem(pairs, 2 * tok, tok_all), "e2": vmem(pairs, 2 * tok, enc_all),
         "rl1": full(pairs, 2 * tok, 1), "rl2": full(pairs, 2 * tok, 1),
         "mixed1": vmem(tok, wide), "mixed2": vmem(tok, wide), "table_rows": full(2 * ctx, tok),
-        "ids": full(ctx, 2 * tok), "bias": full(ctx, 8, 2 * tok), "diag": full(ctx, 8, 2 * tok),
+        "ids": full(1, 2 * tok_all), "bias": full(8, 2 * tok_all), "diag": full(8, 2 * tok_all),
         "after_self": full(tok, model), "after_cross": full(tok, model),
         "cross_grad": full(tok, model), "self_grad": full(tok, model), "n2": vmem(tok, model),
         "N3": vmem(tok4, model), "act": vmem(tok4, quarter), "GU": vmem(tok4, 2 * quarter),
@@ -1043,8 +1122,7 @@
         "pe": vmem(enc_all, model // 2), "NG": full(tok, model), "NE": full(enc, model),
         "ml": vmem(3, 4 * rows, size.part), "ps": vmem(4 * rows, size.part),
         "s1": full(8, model), "s2": full(8, model), "sr": full(2, 8, model),
-        "sl": full(4, 8, model), "t1": full(buckets, 128), "t2": full(buckets, 128),
-        "tr": full(2, buckets, 128), "tl": full(4, buckets, 128), **wire_sems(512),
+        "sl": full(4, 8, model), "t1": full(8, 128), "t2": full(8, 128), "tr": full(2, 8, 128), "tl": full(4, 8, 128), **wire_sems(73, 323),
     }
     names = list(ins) + list(outs) + list(scratch)
     made = pl.pallas_call(
@@ -1060,14 +1138,22 @@
             collective_id=1, has_side_effects=True, vmem_limit_bytes=VMEM_LIMIT
         ),
     )(*ins.values())
-    layer_out, input_grad, enc_grad, wg, mg, totals, bias_totals = made
-    grads = {name: wg[:, size.col[name]] for name in size.names}
-    mlp = mg.reshape(rows, 4, 3, quarter)
-    gate, upward, down = (mlp[:, :, i].reshape(rows, units).astype(F32) for i in range(3))
+    specs = [
+        (tok, model), (tok, model), (enc, model), *((rows, wide),) * 8, *((rows, units),) * 3,
+        (3, model), (heads, buckets),
+    ]
+    parts = pl.pallas_call(
+        functools.partial(emit_kernel, size),
+        out_shape=tuple(jax.ShapeDtypeStruct(spec, F32) for spec in specs),
+        in_specs=[pl.BlockSpec(memory_space=pltpu.VMEM)] * len(made),
+        out_specs=tuple(pl.BlockSpec(memory_space=pltpu.VMEM) for _ in specs),
+    )(*made)
+    named_parts = dict(zip(size.names, parts[3:11]))
+    gate, upward, down, gains, bias_grad = parts[11:]
     return (
-        layer_out, input_grad, enc_grad, grads["q"], grads["k"], grads["v"], grads["o"].T,
-        grads["cq"], grads["ck"], grads["cv"], grads["co"].T, gate, upward, down.T,
-        totals[:3], bias_totals[:, :heads],
+        *parts[:3], named_parts["q"], named_parts["k"], named_parts["v"], named_parts["o"].T,
+        named_parts["cq"], named_parts["ck"], named_parts["cv"], named_parts["co"].T,
+        gate, upward, down.T, gains, bias_grad.T,
     )
 
 

time: 221 us -> 185 us (0.84)
  Pallas kernels: 205 us -> 184 us
  local copies, waits for them, and re-layouts: 12.8 us -> 0 us
    pallas_call x1, Pallas kernels: 205 us -> 181 us  [quick_device(): pl.pallas_call(named(functools.partial(layer_kernel, size), names), out_s...]
    unnamed x29 -> x0, local copies, waits for them, and re-layouts: 9.77 us -> none
    pallas_call x0 -> x1, Pallas kernels: none -> 2.84 us  [quick_device(): pl.pallas_call(functools.partial(emit_kernel, size), out_shape=tuple((jax...]
where the time goes in v3:
time: 185 us
  Pallas kernels  184 us (99%)
    pallas_call x1, Pallas kernels, quick_device(): pl.pallas_call(named(functools.partial(layer_kernel, size), names), out_s...  181 us

profile of v3, /device:TPU:0, one launch (start us, length us, event | category | flops | bytes accessed | tf_op | source)
XLA Modules:
  0.0 185.0 jit_solution(10118158280208717878)
XLA Ops:
  0.7 181.4 %shard_map.297 = (f32[128,768]{1,0:T(8,128)}, f32[128,768]{1,0:T(8,128)}, f32[64,768]{1,0:T(8,128)}, f32[48,3072]{1,0:T(8,128)}, bf16[48,3072]{1,0:T(8,128)(2,1)}, /*index=5*/f32[8,768]{1,0:T(8,128)}, f32[8,128]{1,0:T(8,128)}) custom-call(f32[128,768]{1,0:T(8,128)} %refs_0_.1, bf16[64,768]{1,0:T(8,128)(2,1)} %refs_1_.1, bf16[48,384]{1,0:T(8,128)(2,1)} %refs_2_.1, ...), custom_call_target="tpu_custom_call" | custom-call | tf_op jit(solution)/shard_map/pallas_call | solution.py:1128
  182.0 2.8 %shard_map.298 = (f32[128,768]{1,0:T(8,128)}, f32[128,768]{1,0:T(8,128)}, f32[64,768]{1,0:T(8,128)}, f32[48,384]{1,0:T(8,128)}, f32[48,384]{1,0:T(8,128)}, /*ind...) custom-call(f32[128,768]{1,0:T(8,128)} %get-tuple-element.39.layer_o, ...), custom_call_target="tpu_custom_call" | custom-call | tf_op jit(solution)/shard_map/pallas_call | solution.py:1145

commit v4 on v3

--- a/solution.py
+++ b/solution.py
@@ -185,38 +185,44 @@
             self._out(half, place.here, 3, near)
             self._out(half, place.here, 7, far)
 
-    def pass_level(self, steps=(0, 1, 2)):
+    def _level_block(self, step):
         place = self.wire.place
-        for step in steps:
-            k = place.nearest[step]
-            block = lax.rem(place.here + place.count - 4 * k, place.count)
-            rising = place.level >= k
-            onward = jnp.where(rising, place.level < place.top, place.level > 0)
-            chip = jnp.where(rising, place.here + 4, place.here - 4)
-            slot = jnp.where(rising, k, k - 2)
-            for half in self.halves:
-                near, far = place.near(half)
-                self.wire.got(self.view(half, block), self.base[half] + k - 1)
-
-                @pl.when(onward)
-                def _():
-                    self._line(half, block, slot, chip)
-
-                self._out(half, block, 3 + k, near)
-                self._out(half, block, 7, far)
-                self._give(half, block)
-
-    def pass_near(self, steps=(0, 1, 2, 3)):
+        k = place.nearest[step]
+        return k, lax.rem(place.here + place.count - 4 * k, place.count)
+
+    def pass_line(self, step):
         place = self.wire.place
-        for step in steps:
-            k = (0, *place.nearest)[step]
-            for half in self.halves:
-                _, far = place.near(half)
-                block = lax.rem(place.here + place.count - 4 * k, place.count)
-                block = place.flip(block, half)
-                self.wire.got(self.view(half, block), self.base[half] + 3 + k)
-                self._out(half, block, 7, far)
-                self._give(half, block)
+        k, block = self._level_block(step)
+        rising = place.level >= k
+        onward = jnp.where(rising, place.level < place.top, place.level > 0)
+        chip = jnp.where(rising, place.here + 4, place.here - 4)
+        slot = jnp.where(rising, k, k - 2)
+        for half in self.halves:
+            self.wire.got(self.view(half, block), self.base[half] + k - 1)
+
+            @pl.when(onward)
+            def _():
+                self._line(half, block, slot, chip)
+
+    def pass_plane(self, step):
+        place = self.wire.place
+        k, block = self._level_block(step)
+        for half in self.halves:
+            near, far = place.near(half)
+            self._out(half, block, 3 + k, near)
+            self._out(half, block, 7, far)
+            self._give(half, block)
+
+    def pass_near(self, step):
+        place = self.wire.place
+        k = (0, *place.nearest)[step]
+        block = lax.rem(place.here + place.count - 4 * k, place.count)
+        for half in self.halves:
+            _, far = place.near(half)
+            arrived = place.flip(block, half)
+            self.wire.got(self.view(half, arrived), self.base[half] + 3 + k)
+            self._out(half, arrived, 7, far)
+            self._give(half, arrived)
 
     def finish(self):
         place = self.wire.place
@@ -249,7 +255,7 @@
     def __init__(self, wire, view, buf, out):
         self.wire, self.view, self.buf, self.out = wire, view, buf, out
         self.halves = range(2)
-        self.base = [wire.slots(13) for _ in self.halves]
+        self.base = [wire.slots(9) for _ in self.halves]
         self.send_slot = [wire.sender(buf(half)) for half in self.halves]
 
     def _send(self, half, block, place_in, slot, chip):
@@ -261,39 +267,35 @@
             out=self.send_slot[half],
         )
 
-    def start(self, levels=(1, 2, 3, 0)):
+    def start(self, k):
         place = self.wire.place
-        for k in levels:
-            for half in self.halves:
-                _, far = place.near(half)
-                away = place.flip(place.below[k], 1 - half)
-                for pair, block in ((1, place.flip(away, half)), (0, away)):
-                    self._send(half, block, 2 * k + pair, 2 * k + pair, far)
-
-    def pass_near(self, levels=(1, 2, 3, 0)):
+        for half in self.halves:
+            _, far = place.near(half)
+            away = place.flip(place.below[k], 1 - half)
+            for pair, block in ((1, place.flip(away, half)), (0, away)):
+                self._send(half, block, 2 * k + pair, k, far)
+
+    def pass_near(self, k):
         place = self.wire.place
-        for k in levels:
-            for half in self.halves:
-                near, _ = place.near(half)
-                block = place.flip(place.below[k], half)
-                slot = 2 * k + 1
-                self.wire.got(self.buf(half).at[slot], self.base[half] + slot)
-                ref = self.view(half, block)
-                ref[...] = (ref[...].astype(F32) + self.buf(half)[slot].astype(F32)).astype(LOW)
-                self._send(half, block, 8 + k, 8 + k, near)
-
-    def pass_level(self, levels=(1, 2, 3)):
+        for half in self.halves:
+            near, _ = place.near(half)
+            block = place.flip(place.below[k], half)
+            pair = self.buf(half).at[2 * k : 2 * k + 2]
+            self.wire.got(pair, self.base[half] + k)
+            ref = self.view(half, block)
+            ref[...] = (ref[...].astype(F32) + pair[1].astype(F32)).astype(LOW)
+            self._send(half, block, 8 + k, 4 + k, near)
+
+    def pass_level(self, k):
         place = self.wire.place
-        for k in levels:
-            for half in self.halves:
-                ref = self.view(half, place.below[k])
-                ref[...] = self._sum(half, k).astype(LOW)
-                self._send(half, place.below[k], 11 + k, 12, place.below[k])
+        for half in self.halves:
+            ref = self.view(half, place.below[k])
+            ref[...] = self._sum(half, k).astype(LOW)
+            self._send(half, place.below[k], 11 + k, 8, place.below[k])
 
     def _sum(self, half, k):
         place, buf = self.wire.place, self.buf(half)
-        self.wire.got(buf.at[2 * k], self.base[half] + 2 * k)
-        self.wire.got(buf.at[8 + k], self.base[half] + 8 + k)
+        self.wire.got(buf.at[8 + k], self.base[half] + 4 + k)
         total = self.view(half, place.below[k])[...].astype(F32)
         return total + buf[2 * k].astype(F32) + buf[8 + k].astype(F32)
 
@@ -301,7 +303,7 @@
         for half in self.halves:
             buf = self.buf(half)
             total = self._sum(half, 0)
-            self.wire.got(buf.at[12:15], self.base[half] + 12)
+            self.wire.got(buf.at[12:15], self.base[half] + 8)
             for k in (1, 2, 3):
                 total = total + buf[11 + k].astype(F32)
             self.out(half, total)
@@ -551,7 +553,7 @@
 
     def start(self):
         own = self.view(0, self.wire.place.core)
-        for k in (1, 2, 3):
+        for k in (3, 1, 2):
             self.wire.send(own, own, self.base + k, self.chips[k], out=self.out)
 
     def share(self, k):
@@ -674,16 +676,27 @@
     sum_o = PlaneSum(wire, tok, PO, po_core, po_plane, po_whole)
     mg_plane, mg_level, ms_level, ms_plane = (wire.slots(3) for _ in range(4))
 
+    def units_out():
+        for k, chip in enumerate(plane_chips):
+            wire.send(
+                wm.at[:, pl.ds(aligned(lax.rem(chip, 4) * size.part, 128), size.part)],
+                WM.at[own_weights, :],
+                mg_plane + k,
+                chip,
+            )
+
+    def units_up():
+        for k, chip in enumerate(plane_chips):
+            wire.got(WM.at[block_rows(chip, rows), :], mg_plane + k)
+        own = WM.at[block_rows(place.level, 4 * rows), :]
+        for k in (1, 2, 3):
+            wire.send(own, own, mg_level + k - 1, place.above[k])
+
     place.signal(place.above[1:] + list(plane_chips))
     X[here_rows, :] = rms_forward(layer_in[...], gains[0:1]).astype(LOW)
     for name, ref in zip(("q", "k", "v", "cq", "ck", "cv", "o", "co"), (sq, sk, sv, cq, ck, cv, so, co)):
         WA[own_weights, col[name]] = ref[...]
     E[block_rows(place.here, enc), :] = encoded[...]
-    place.meet(7)
-    gx.start_level()
-    gs.start_level()
-    gx.start_plane()
-    gs.start_plane()
     plane_rows = block_rows(place.plane, tok)
     GR[plane_rows, :] = out_grad[...].astype(LOW)
     for p in range(4):
@@ -692,47 +705,69 @@
             base = p * size.part + i * quarter
             wm[:, base : base + quarter] = ref[:, cols]
     WM[own_weights, :] = wm[:, my_part]
-    gx.pass_near((0,))
-    gs.pass_near((0,))
-    gx.pass_level((0,))
-    gs.pass_level((0,))
-    gx.pass_level((1,))
-    gs.pass_level((1,))
-    gx.pass_near((1,))
-    gs.pass_near((1,))
-    gx.pass_level((2,))
+    place.meet(7)
+    gx.start_level()
+    gs.start_level()
+    gx.start_plane()
+    gs.start_plane()
+    gx.pass_near(0)
+    gx.pass_line(0)
+    gx.pass_plane(0)
+    gs.pass_near(0)
+    gs.pass_line(0)
+    gs.pass_plane(0)
+    gx.pass_line(1)
+    gx.pass_plane(1)
+    gs.pass_line(1)
+    gs.pass_plane(1)
     go.start_level()
     ge.start_level()
-    gs.pass_level((2,))
+    gx.pass_near(1)
+    gs.pass_near(1)
+    gx.pass_line(2)
+    gx.pass_plane(2)
+    gs.pass_line(2)
+    gs.pass_plane(2)
     gc_.start_level()
-    gx.pass_near((2,))
-    gs.pass_near((2,))
-    gx.pass_near((3,))
-    gs.pass_near((3,))
+    gp.start_level()
+    gx.pass_near(2)
+    gs.pass_near(2)
+    gx.pass_near(3)
+    gs.pass_near(3)
     go.start_plane()
     ge.start_plane()
-    go.pass_level()
-    ge.pass_level()
-    go.pass_near((0,))
-    ge.pass_near((0,))
     gc_.start_plane()
+    units_out()
     bucket_rows(buckets, order, place.here, table_rows, ids)
     bias_vectors(ids, table, bias)
     diag[...] = jnp.zeros_like(diag)
-    gp.start_level()
-    gc_.pass_level((0, 1))
+    go.pass_line(0)
+    go.pass_plane(0)
+    ge.pass_line(0)
+    ge.pass_plane(0)
+    gc_.pass_line(0)
+    gp.pass_line(0)
+    go.pass_line(1)
+    go.pass_plane(1)
+    ge.pass_line(1)
+    ge.pass_plane(1)
+    gc_.pass_line(1)
+    gp.pass_line(1)
+    go.pass_line(2)
+    go.pass_plane(2)
+    ge.pass_line(2)
+    ge.pass_plane(2)
+    gc_.pass_line(2)
+    gp.pass_line(2)
+    gc_.pass_plane(0)
+    gc_.pass_plane(1)
+    gc_.pass_plane(2)
     gx.finish()
-    gc_.pass_level((2,))
-    gp.start_plane()
+    go.pass_near(0)
+    ge.pass_near(0)
     gx.finish_share()
     gs.finish()
-    for k, chip in enumerate(plane_chips):
-        wire.send(
-            wm.at[:, pl.ds(aligned(lax.rem(chip, 4) * size.part, 128), size.part)],
-            WM.at[own_weights, :],
-            mg_plane + k,
-            chip,
-        )
+    units_up()
 
     def project(rows_):
         kv[rows_, :] = dot(X[rows_, :], WA[:, col["kv"]]).astype(LOW)
@@ -740,31 +775,41 @@
     def project_enc(rows_):
         mkv[rows_, :] = dot(E[rows_, :], WA[:, col["ckv"]]).astype(LOW)
 
+    def project_level(level):
+        for part_ in range(2):
+            project(slice((2 * level + part_) * 2 * tok, (2 * level + part_ + 1) * 2 * tok))
+
     q[...] = dot(X[here_rows, :], WA[:, col["q"]]).astype(LOW)
-    rows_loop(ctx_tok, 256, project)
-
-    go.pass_near((1, 2, 3))
-    ge.pass_near((1, 2, 3))
+    project_level(0)
+    project_level(1)
+    project_level(2)
+    project_level(3)
+    go.pass_near(1)
+    go.pass_near(2)
+    go.pass_near(3)
+    ge.pass_near(1)
+    ge.pass_near(2)
+    ge.pass_near(3)
 
     def during_self(j):
         if j == 0:
-            gp.pass_level()
+            gc_.pass_near(0)
+            gc_.pass_near(1)
         elif j == 1:
-            gc_.pass_near()
-            for k, chip in enumerate(plane_chips):
-                wire.got(WM.at[block_rows(chip, rows), :], mg_plane + k)
-            own = WM.at[block_rows(place.level, 4 * rows), :]
-            for k in (1, 2, 3):
-                wire.send(own, own, mg_level + k - 1, place.above[k])
-        else:
+            gc_.pass_near(2)
+            gc_.pass_near(3)
+            gp.start_plane()
+            gp.pass_plane(0)
+            gp.pass_plane(1)
+            gp.pass_plane(2)
+        elif j == 2:
             gg.start()
+            go.finish()
 
     pair_attend(tok, size.pairs, 512, q, kv, s, e1, rl1, mixed1, bias, during_self)
-    go.finish()
     part = dot_nt(mixed1[...], WA[:, col["o"]])
     after_self[...] = layer_in[...] + core_sum(wire, part, ca.at[0], cb.at[0])
     n2[...] = rms_forward(after_self[...], gains[1:2]).astype(LOW)
-    gp.pass_near()
     ge.finish()
     ge.finish_share()
     gc_.finish()
@@ -773,7 +818,12 @@
     probes[...] = dot(n2[...], WA[:, col["cq"]]).astype(LOW)
 
     def during_cross(j):
-        if j == 1:
+        if j == 0:
+            gp.pass_near(0)
+            gp.pass_near(1)
+            gp.pass_near(2)
+            gp.pass_near(3)
+        elif j == 1:
             for k in (1, 2, 3):
                 gg.share(k)
 
@@ -802,24 +852,25 @@
     def spread_rows(k):
         return sum_n.rows(k)
 
-    for k in (1, 2, 3):
-        gg.finish(k)
     units(0)
     sum_n.start(0)
     spread.share(1)
+    spread.share(3)
     spread.share(2)
+    gg.finish(3)
+    spread.finish(3)
+    units(3)
+    sum_n.start(3)
+    gg.finish(1)
     spread.finish(1)
     units(1)
     sum_n.start(1)
-    spread.share(3)
+    sum_n.middle(3)
+    gg.finish(2)
     spread.finish(2)
     units(2)
     sum_n.start(2)
     sum_n.middle(1)
-    spread.finish(3)
-    units(3)
-    sum_n.start(3)
-    sum_n.middle(2)
 
     def back_out(k):
         rows_ = spread_rows(k)
@@ -830,7 +881,7 @@
         PM[cols, 2 * quarter :] = dot_tn(GR[:, cols], act[...]).astype(LOW)
 
     back_out(0)
-    sum_n.middle(3)
+    sum_n.middle(2)
     sum_n.middle(0)
     rows_loop(model, 128, unit_grads)
     for k in (1, 2, 3):
@@ -850,9 +901,6 @@
     cross_grad[...] = out_grad[...] + extra
     low[...] = cross_grad[...].astype(LOW)
     mixed_grad[...] = dot(low[...], WA[:, col["co"]]).astype(LOW)
-    for k in (1, 2, 3, 0):
-        sum_o.middle(k)
-
     def out_grads(left, right, target):
         def body(cols):
             PW[cols, target] = dot_tn(left[:, cols], right[...]).astype(LOW)
@@ -890,22 +938,105 @@
         wire.got(recv.at[at, :], base + k)
         ref[at, mine] = (ref[at, mine].astype(F32) + recv[at, :].astype(F32)).astype(LOW)
 
+    x_slot, e_slot, cross_slot, small = (wire.slots(n) for n in (1, 1, 1, 10))
+
+    def units_down():
+        total = PM[block_rows(place.level, 4 * rows), :].astype(F32)
+        for k in (1, 2, 3):
+            wire.got(ml.at[k - 1], ms_level + k - 1)
+            total = total + ml[k - 1].astype(F32)
+        ps[...] = total.astype(LOW)
+        for k, chip in enumerate(plane_chips):
+            wire.send(
+                ps.at[block_rows(lax.rem(chip, 4), rows), :], mb.at[:, my_part], ms_plane + k, chip
+            )
+        mb[:, my_part] = ps[block_rows(place.plane, rows), :]
+
+    def units_back():
+        for k, chip in enumerate(plane_chips):
+            cols = pl.ds(aligned(lax.rem(chip, 4) * size.part, 128), size.part)
+            wire.got(mb.at[:, cols], ms_plane + k)
+
+    def result_out():
+        for k in (3, 1, 2, 0):
+            sum_o.middle(k)
+
+    def result_back():
+        sum_o.finish_core()
+        layer_out[...] = after_cross[...] + po_whole[...].astype(F32)
+
+    def tokens_back():
+        sx.finish()
+        wire.swap(NG.at[:, mine], NG.at[:, mine], x_slot)
+
+    def encoder_back():
+        se.finish()
+        wire.swap(NE.at[:, mine], NE.at[:, mine], e_slot)
+
+    def input_back():
+        wire.got(NG.at[:, away], x_slot)
+        extra, gain_one = rms_backward(layer_in[...], gains[0:1], NG[...])
+        input_grad[...] = self_grad[...] + extra
+        s1[...] = jnp.concatenate(
+            (gain_one, gain_two, gain_three, jnp.zeros((5, model), F32)), axis=0
+        )
+
+    def small_first():
+        wire.send(s1, sr.at[0], small, place.fx)
+        wire.send(t1, tr.at[0], small + 5, place.fx)
+
+    def small_second():
+        wire.got(sr.at[0], small)
+        wire.got(tr.at[0], small + 5)
+        s2[...] = s1[...] + sr[0]
+        t2[...] = t1[...] + tr[0]
+        wire.send(s2, sr.at[1], small + 1, place.fy)
+        wire.send(t2, tr.at[1], small + 6, place.fy)
+
+    def small_third():
+        wire.got(sr.at[1], small + 1)
+        wire.got(tr.at[1], small + 6)
+        sl[pl.ds(place.level, 1)] = (s2[...] + sr[1])[None]
+        tl[pl.ds(place.level, 1)] = (t2[...] + tr[1])[None]
+        for k in (1, 2, 3):
+            wire.send(sl.at[place.level], sl.at[place.level], small + 1 + k, place.above[k])
+            wire.send(tl.at[place.level], tl.at[place.level], small + 6 + k, place.above[k])
+
+    def small_last():
+        for k in (1, 2, 3):
+            level = place.below[k] // 4
+            wire.got(sl.at[level], small + 1 + k)
+            wire.got(tl.at[level], small + 6 + k)
+        totals[...] = (sl[0] + sl[1]) + (sl[2] + sl[3])
+        bias_totals[...] = (tl[0] + tl[1]) + (tl[2] + tl[3])
+
+    result_out()
     out_grads(low, mixed2, col["co"])
-    sp.start()
+    sp.start(1)
+    sp.start(2)
     back = PairBack(
         tok, size.pairs, probes, mkv, e2, rl2, mixed2, mixed_grad, mkv_grad, None, qc, gc, dl, dq
     )
-    for c in range(ctx_enc // 512):
+    for c in range(ctx_enc // 1024):
+        back.chunk(c * 512, 512)
+    sp.start(0)
+    for c in range(ctx_enc // 1024, ctx_enc // 512):
         back.chunk(c * 512, 512)
     back.finish(q_grad)
+    sp.start(3)
     part = dot_nt(q_grad[...], WA[:, col["cq"]])
-    slot = wire.slots(1)
     ca[2] = part.astype(LOW)
-    wire.swap(ca.at[2], cb.at[2], slot)
-    sp.pass_near()
+    wire.swap(ca.at[2], cb.at[2], cross_slot)
+    sp.pass_near(1)
+    sp.pass_near(2)
     out_grads(E, mkv_grad, col["ckv"])
+    sp.pass_near(0)
+    sp.pass_near(3)
     out_grads(n2, q_grad, col["cq"])
-    sc.start()
+    sc.start(3)
+    sc.start(2)
+    sp.pass_level(2)
+    sc.start(1)
 
     def enc_rows(rows_):
         EG[rows_, :] = dot_nt(mkv_grad[rows_, :], WA[:, col["ckv"]]).astype(LOW)
@@ -913,7 +1044,7 @@
     rows_loop(ctx_enc, 256, enc_rows)
     for k in (1, 2, 3, 0):
         pair_start(EG, pe, enc, e_base, k, e_out)
-    wire.got(cb.at[2], slot)
+    wire.got(cb.at[2], cross_slot)
     n_grad = ca[2].astype(F32) + cb[2].astype(F32)
     extra, gain_two = rms_backward(after_self[...], gains[1:2], n_grad)
     self_grad[...] = cross_grad[...] + extra
@@ -921,9 +1052,13 @@
     mixed_grad[...] = dot(low[...], WA[:, col["o"]]).astype(LOW)
     for k in (1, 2, 3, 0):
         pair_ready(EG, pe, enc, e_base, k)
-        se.start((k,))
+    se.start(3)
     out_grads(low, mixed1, col["o"])
-    so_.start()
+    se.start(1)
+    se.start(2)
+    so_.start(1)
+    sum_o.finish()
+    sc.pass_near(3)
 
     back = PairBack(
         tok, size.pairs, q, kv, e1, rl1, mixed1, mixed_grad, kv_grad, diag, qc, gc, dl, dq
@@ -938,19 +1073,19 @@
     back.chunk(place.below[1] // 4 * 4 * tok, 4 * tok)
     tok_rows(1)
     pair_start(XG, px, tok, x_base, 1, x_out)
-    sp.pass_level()
     back.chunk(place.below[2] // 4 * 4 * tok, 4 * tok)
     tok_rows(2)
     pair_start(XG, px, tok, x_base, 2, x_out)
     pair_ready(XG, px, tok, x_base, 1)
-    sx.start((1,))
-    sc.pass_near()
+    sc.pass_near(2)
+    so_.start(2)
     back.chunk(place.below[3] // 4 * 4 * tok, 4 * tok)
     tok_rows(3)
     pair_start(XG, px, tok, x_base, 3, x_out)
     pair_ready(XG, px, tok, x_base, 2)
-    sx.start((2,))
-    se.pass_near()
+    so_.start(3)
+    sc.pass_near(1)
+    so_.start(0)
     back.chunk(place.level * 4 * tok, 4 * tok)
     back.finish(q_grad)
     tok_rows(0)
@@ -958,82 +1093,75 @@
     XG[here_rows, :] = own.astype(LOW)
     pair_start(XG, px, tok, x_base, 0, x_out)
     pair_ready(XG, px, tok, x_base, 3)
-    sx.start((3,))
-    so_.pass_near()
+    sp.pass_level(1)
+    so_.pass_near(2)
+    sx.start(2)
     out_grads(n2, q_grad, col["q"])
     pair_ready(XG, px, tok, x_base, 0)
-    sx.start((0,))
-    out_grads(X, kv_grad, col["kv"])
-    sx.pass_near((1, 2))
-    sw.start()
-
-    sc.pass_level()
-    sx.pass_near((3, 0))
-    se.pass_level()
-    total = PM[block_rows(place.level, 4 * rows), :].astype(F32)
-    for k in (1, 2, 3):
-        wire.got(ml.at[k - 1], ms_level + k - 1)
-        total = total + ml[k - 1].astype(F32)
-    ps[...] = total.astype(LOW)
-    for k, chip in enumerate(plane_chips):
-        wire.send(
-            ps.at[block_rows(lax.rem(chip, 4), rows), :], mb.at[:, my_part], ms_plane + k, chip
-        )
-    mb[:, my_part] = ps[block_rows(place.plane, rows), :]
+    so_.pass_near(1)
+    sc.pass_level(2)
+    out_grads(X, kv_grad.at[:, : size.wide], col["k"])
+    sx.start(3)
+    out_grads(X, kv_grad.at[:, size.wide :], col["v"])
+    so_.pass_level(2)
+    sx.pass_near(2)
+    sw.start(1)
+    sx.pass_level(2)
+    se.pass_near(1)
+    sx.start(1)
+    sw.pass_near(1)
+    sw.start(2)
+    se.pass_near(2)
+    sc.pass_level(1)
+    se.start(0)
+    sx.pass_near(3)
+    se.pass_level(1)
+    sp.pass_level(3)
+    se.pass_near(3)
+    sw.pass_level(1)
+    sx.pass_near(1)
+    se.pass_level(2)
     sums = bucket_sums(ids, diag, table.shape[1])
     t1[...] = jnp.concatenate(
         (sums, jnp.zeros((sums.shape[0], t1.shape[1] - sums.shape[1]), F32)), axis=1
     )
-    so_.pass_level()
-    sw.pass_near((1, 2))
-    sx.pass_level()
-    sw.pass_near((3, 0))
-    sum_o.finish()
-    se.finish()
-    x_slot, e_slot = wire.slots(1), wire.slots(1)
-    wire.swap(NE.at[:, mine], NE.at[:, mine], e_slot)
-    sx.finish()
-    wire.swap(NG.at[:, mine], NG.at[:, mine], x_slot)
-    sw.pass_level()
-    wire.got(NG.at[:, away], x_slot)
-    extra, gain_one = rms_backward(layer_in[...], gains[0:1], NG[...])
-    input_grad[...] = self_grad[...] + extra
-    s1[...] = jnp.concatenate(
-        (gain_one, gain_two, gain_three, jnp.zeros((5, model), F32)), axis=0
-    )
-    small = wire.slots(10)
-    wire.send(s1, sr.at[0], small, place.fx)
-    wire.send(t1, tr.at[0], small + 5, place.fx)
-    sum_o.finish_core()
-    layer_out[...] = after_cross[...] + po_whole[...].astype(F32)
+
+    se.pass_near(0)
+    sx.pass_level(3)
+    sw.pass_near(2)
+    sx.pass_level(1)
+    sx.start(0)
+    sp.finish()
+    so_.pass_near(3)
+    so_.pass_level(1)
+    sw.start(3)
+    so_.pass_near(0)
+    sx.pass_near(0)
+    sc.pass_level(3)
+    sc.start(0)
+    se.pass_level(3)
+    sw.start(0)
+    sw.pass_level(2)
+    tokens_back()
+    input_back()
+    small_first()
+    result_back()
+    sw.pass_near(3)
+    sw.pass_near(0)
+    small_second()
+    so_.pass_level(3)
+    units_down()
+    sw.pass_level(3)
+    so_.finish()
+    small_third()
+    sc.pass_near(0)
+    encoder_back()
+    units_back()
+    sw.finish()
+    small_last()
+    sc.finish()
     wire.got(NE.at[:, away], e_slot)
     enc_grad[...] = NE[...]
-    wire.got(sr.at[0], small)
-    wire.got(tr.at[0], small + 5)
-    s2[...] = s1[...] + sr[0]
-    t2[...] = t1[...] + tr[0]
-    wire.send(s2, sr.at[1], small + 1, place.fy)
-    wire.send(t2, tr.at[1], small + 6, place.fy)
-    sp.finish()
-    sc.finish()
-    so_.finish()
-    wire.got(sr.at[1], small + 1)
-    wire.got(tr.at[1], small + 6)
-    sl[pl.ds(place.level, 1)] = (s2[...] + sr[1])[None]
-    tl[pl.ds(place.level, 1)] = (t2[...] + tr[1])[None]
-    for k in (1, 2, 3):
-        wire.send(sl.at[place.level], sl.at[place.level], small + 1 + k, place.above[k])
-        wire.send(tl.at[place.level], tl.at[place.level], small + 6 + k, place.above[k])
-    sw.finish()
-    for k, chip in enumerate(plane_chips):
-        cols = pl.ds(aligned(lax.rem(chip, 4) * size.part, 128), size.part)
-        wire.got(mb.at[:, cols], ms_plane + k)
-    for k in (1, 2, 3):
-        level = place.below[k] // 4
-        wire.got(sl.at[level], small + 1 + k)
-        wire.got(tl.at[level], small + 6 + k)
-    totals[...] = (sl[0] + sl[1]) + (sl[2] + sl[3])
-    bias_totals[...] = (tl[0] + tl[1]) + (tl[2] + tl[3])
     for made in (gx, ge, gs, gc_, go, gp):
         made.drain()
     wire.drain()
@@ -1122,7 +1250,7 @@
         "pe": vmem(enc_all, model // 2), "NG": full(tok, model), "NE": full(enc, model),
         "ml": vmem(3, 4 * rows, size.part), "ps": vmem(4 * rows, size.part),
         "s1": full(8, model), "s2": full(8, model), "sr": full(2, 8, model),
-        "sl": full(4, 8, model), "t1": full(8, 128), "t2": full(8, 128), "tr": full(2, 8, 128), "tl": full(4, 8, 128), **wire_sems(73, 323),
+        "sl": full(4, 8, model), "t1": full(8, 128), "t2": full(8, 128), "tr": full(2, 8, 128), "tl": full(4, 8, 128), **wire_sems(73, 275),
     }
     names = list(ins) + list(outs) + list(scratch)
     made = pl.pallas_call(

time: 185 us -> 176 us (0.951)
  Pallas kernels: 184 us -> 175 us
    pallas_call x1, Pallas kernels: 181 us -> 172 us  [quick_device(): pl.pallas_call(named(functools.partial(layer_kernel, size), names), out_s...]
where the time goes in v4:
time: 176 us
  Pallas kernels  175 us (99%)
    pallas_call x1, Pallas kernels, quick_device(): pl.pallas_call(named(functools.partial(layer_kernel, size), names), out_s...  172 us

profile of v4, /device:TPU:0, one launch (start us, length us, event | category | flops | bytes accessed | tf_op | source)
XLA Modules:
  0.0 175.9 jit_solution(3123572663617279263)
XLA Ops:
  0.7 172.2 %shard_map.297 = (f32[128,768]{1,0:T(8,128)}, f32[128,768]{1,0:T(8,128)}, f32[64,768]{1,0:T(8,128)}, f32[48,3072]{1,0:T(8,128)}, bf16[48,3072]{1,0:T(8,128)(2,1)}, /*index=5*/f32[8,768]{1,0:T(8,128)}, f32[8,128]{1,0:T(8,128)}) custom-call(f32[128,768]{1,0:T(8,128)} %refs_0_.1, bf16[64,768]{1,0:T(8,128)(2,1)} %refs_1_.1, bf16[48,384]{1,0:T(8,128)(2,1)} %refs_2_.1, ...), custom_call_target="tpu_custom_call" | custom-call | tf_op jit(solution)/shard_map/pallas_call | solution.py:1256
  172.8 2.8 %shard_map.298 = (f32[128,768]{1,0:T(8,128)}, f32[128,768]{1,0:T(8,128)}, f32[64,768]{1,0:T(8,128)}, f32[48,384]{1,0:T(8,128)}, f32[48,384]{1,0:T(8,128)}, /*ind...) custom-call(f32[128,768]{1,0:T(8,128)} %get-tuple-element.39.layer_o, ...), custom_call_target="tpu_custom_call" | custom-call | tf_op jit(solution)/shard_map/pallas_call | solution.py:1273

commit v5 on v4

--- a/solution.py
+++ b/solution.py
@@ -146,25 +146,25 @@
     def __init__(self, wire, view, share, spare):
         self.wire, self.view, self.share, self.spare = wire, view, share, spare
         self.halves = range(2)
-        self.base = [wire.slots(8) for _ in self.halves]
-        self.out = [wire.sender(spare(half, 12)) for half in self.halves]
-        self.line_out = [wire.sender() for _ in self.halves]
+        self.base = wire.slots(8)
+        self.out = wire.sender(spare(12))
+        self.line_out = wire.sender()
         if share:
-            self.side = [wire.slots(1) for _ in self.halves]
-            self.side_out = [wire.sender(spare(half, 15)) for half in self.halves]
+            self.side = wire.slots(1)
+            self.side_out = wire.sender(spare(15))
 
     def _line(self, half, block, slot, chip):
         ref = self.view(half, block)
-        self.wire.send(ref, ref, self.base[half] + slot, chip, out=self.line_out[half])
+        self.wire.send(ref, ref, self.base + slot, chip, out=self.line_out)
 
     def _out(self, half, block, slot, chip):
         ref = self.view(half, block)
-        self.wire.send(ref, ref, self.base[half] + slot, chip, out=self.out[half])
+        self.wire.send(ref, ref, self.base + slot, chip, out=self.out)
 
     def _give(self, half, block):
         if self.share:
             ref = self.view(half, block)
-            self.wire.swap(ref, ref, self.side[half], self.side_out[half])
+            self.wire.swap(ref, ref, self.side, self.side_out)
 
     def start_level(self):
         place = self.wire.place
@@ -197,8 +197,8 @@
         onward = jnp.where(rising, place.level < place.top, place.level > 0)
         chip = jnp.where(rising, place.here + 4, place.here - 4)
         slot = jnp.where(rising, k, k - 2)
+        self.wire.got(self.spare(1), self.base + k - 1)
         for half in self.halves:
-            self.wire.got(self.view(half, block), self.base[half] + k - 1)
 
             @pl.when(onward)
             def _():
@@ -217,17 +217,17 @@
         place = self.wire.place
         k = (0, *place.nearest)[step]
         block = lax.rem(place.here + place.count - 4 * k, place.count)
+        self.wire.got(self.spare(1), self.base + 3 + k)
         for half in self.halves:
             _, far = place.near(half)
             arrived = place.flip(block, half)
-            self.wire.got(self.view(half, arrived), self.base[half] + 3 + k)
             self._out(half, arrived, 7, far)
             self._give(half, arrived)
 
     def finish(self):
         place = self.wire.place
+        self.wire.got(self.spare(8), self.base + 7)
         for half in self.halves:
-            self.wire.got(self.spare(half, 8), self.base[half] + 7)
             if self.share:
                 for k in range(4):
                     block = place.flip(place.below[k], 1 - half)
@@ -235,36 +235,34 @@
                     self._give(half, place.flip(block, half))
 
     def finish_share(self):
-        for half in self.halves:
-            self.wire.got(self.spare(half, 15), self.side[half])
+        self.wire.got(self.spare(15), self.side)
 
     def drain(self):
         place = self.wire.place
-        for half in self.halves:
-
-            @pl.when(jnp.logical_or(place.level == 0, place.level == place.top))
-            def _():
-                self.wire.sent(self.spare(half, 1), self.line_out[half])
-
-            @pl.when(jnp.logical_and(place.level > 0, place.level < place.top))
-            def _():
-                self.wire.sent(self.spare(half, 5), self.line_out[half])
+
+        @pl.when(jnp.logical_or(place.level == 0, place.level == place.top))
+        def _():
+            self.wire.sent(self.spare(1), self.line_out)
+
+        @pl.when(jnp.logical_and(place.level > 0, place.level < place.top))
+        def _():
+            self.wire.sent(self.spare(5), self.line_out)
 
 
 class Scatter:
-    def __init__(self, wire, view, buf, out):
-        self.wire, self.view, self.buf, self.out = wire, view, buf, out
+    def __init__(self, wire, view, buf, out, spare):
+        self.wire, self.view, self.buf, self.out, self.spare = wire, view, buf, out, spare
         self.halves = range(2)
-        self.base = [wire.slots(9) for _ in self.halves]
-        self.send_slot = [wire.sender(buf(half)) for half in self.halves]
+        self.base = wire.slots(9)
+        self.send_slot = wire.sender(spare(15))
 
     def _send(self, half, block, place_in, slot, chip):
         self.wire.send(
             self.view(half, block),
             self.buf(half).at[place_in],
-            self.base[half] + slot,
+            self.base + slot,
             chip,
-            out=self.send_slot[half],
+            out=self.send_slot,
         )
 
     def start(self, k):
@@ -277,35 +275,34 @@
 
     def pass_near(self, k):
         place = self.wire.place
+        self.wire.got(self.spare(2), self.base + k)
         for half in self.halves:
             near, _ = place.near(half)
             block = place.flip(place.below[k], half)
-            pair = self.buf(half).at[2 * k : 2 * k + 2]
-            self.wire.got(pair, self.base[half] + k)
             ref = self.view(half, block)
-            ref[...] = (ref[...].astype(F32) + pair[1].astype(F32)).astype(LOW)
+            ref[...] = (ref[...].astype(F32) + self.buf(half)[2 * k + 1].astype(F32)).astype(LOW)
             self._send(half, block, 8 + k, 4 + k, near)
 
     def pass_level(self, k):
         place = self.wire.place
+        self.wire.got(self.spare(1), self.base + 4 + k)
         for half in self.halves:
             ref = self.view(half, place.below[k])
             ref[...] = self._sum(half, k).astype(LOW)
             self._send(half, place.below[k], 11 + k, 8, place.below[k])
 
     def _sum(self, half, k):
-        place, buf = self.wire.place, self.buf(half)
-        self.wire.got(buf.at[8 + k], self.base[half] + 4 + k)
-        total = self.view(half, place.below[k])[...].astype(F32)
+        buf = self.buf(half)
+        total = self.view(half, self.wire.place.below[k])[...].astype(F32)
         return total + buf[2 * k].astype(F32) + buf[8 + k].astype(F32)
 
     def finish(self):
+        self.wire.got(self.spare(1), self.base + 4)
+        self.wire.got(self.spare(3), self.base + 8)
         for half in self.halves:
-            buf = self.buf(half)
             total = self._sum(half, 0)
-            self.wire.got(buf.at[12:15], self.base[half] + 8)
             for k in (1, 2, 3):
-                total = total + buf[11 + k].astype(F32)
+                total = total + self.buf(half)[11 + k].astype(F32)
             self.out(half, total)
 
 
@@ -553,7 +550,7 @@
 
     def start(self):
         own = self.view(0, self.wire.place.core)
-        for k in (3, 1, 2):
+        for k in (1, 2, 3):
             self.wire.send(own, own, self.base + k, self.chips[k], out=self.out)
 
     def share(self, k):
@@ -652,23 +649,17 @@
         return view
 
     def token_spare(buf):
-        return lambda half, count: buf.at[half, 0:count]
-
-    def weight_spare(*bufs):
-        return lambda half, count: bufs[half].at[0:count]
-
-    def token_gather(ref, count, buf):
-        return Gather(
-            wire,
-            token_view(ref, count, place.core),
-            True,
-            token_spare(buf),
-        )
-
-    gx, ge = token_gather(X, tok, bx), token_gather(E, enc, be)
+        return lambda count: buf.at[:, 0:count]
+
+    def weight_spare(name):
+        (first, _), (_, last) = size.cuts[name]
+        return lambda count: WA.at[0 : count * rows, first:last]
+
+    gx = Gather(wire, token_view(X, tok, place.core), True, token_spare(bx))
+    ge = Gather(wire, token_view(E, enc, place.core), True, token_spare(be))
     gs, gc_, go, gp = (
-        Gather(wire, weight_view(WA, name), False, weight_spare(*bufs))
-        for name, bufs in (("s", (bs0, bs1)), ("c", (bc0, bc1)), ("o", (bo0, bo1)), ("co", (bp0, bp1)))
+        Gather(wire, weight_view(WA, name), False, weight_spare(name))
+        for name in ("s", "c", "o", "co")
     )
     gg = PlaneGather(wire, tok, GR)
     spread = PlaneGather(wire, tok, N3)
@@ -823,10 +814,6 @@
             gp.pass_near(1)
             gp.pass_near(2)
             gp.pass_near(3)
-        elif j == 1:
-            for k in (1, 2, 3):
-                gg.share(k)
-
     pair_attend(tok, size.pairs, 512, probes, mkv, s, e2, rl2, mixed2, None, during_cross)
     gp.finish()
     part = dot_nt(mixed2[...], WA[:, col["co"]])
@@ -854,23 +841,25 @@
 
     units(0)
     sum_n.start(0)
+    for k in (1, 2, 3):
+        gg.share(k)
     spread.share(1)
-    spread.share(3)
     spread.share(2)
-    gg.finish(3)
-    spread.finish(3)
-    units(3)
-    sum_n.start(3)
     gg.finish(1)
     spread.finish(1)
     units(1)
     sum_n.start(1)
-    sum_n.middle(3)
     gg.finish(2)
     spread.finish(2)
     units(2)
     sum_n.start(2)
     sum_n.middle(1)
+    spread.share(3)
+    gg.finish(3)
+    spread.finish(3)
+    units(3)
+    sum_n.start(3)
+    sum_n.middle(2)
 
     def back_out(k):
         rows_ = spread_rows(k)
@@ -881,8 +870,12 @@
         PM[cols, 2 * quarter :] = dot_tn(GR[:, cols], act[...]).astype(LOW)
 
     back_out(0)
-    sum_n.middle(2)
+    sum_n.middle(3)
     sum_n.middle(0)
+    for k in (1, 2, 3):
+        back_out(k)
+    for k in range(4):
+        sum_o.start(k)
     rows_loop(model, 128, unit_grads)
     for k in (1, 2, 3):
         wire.send(
@@ -891,11 +884,9 @@
             ms_level + k - 1,
             place.above[k],
         )
+    for k in (3, 1, 2, 0):
+        sum_o.middle(k)
     sum_n.finish()
-    for k in (1, 2, 3):
-        back_out(k)
-    for k in range(4):
-        sum_o.start(k)
     sum_n.finish_core()
     extra, gain_three = rms_backward(after_cross[...], gains[2:3], pn_whole[...].astype(F32))
     cross_grad[...] = out_grad[...] + extra
@@ -912,7 +903,9 @@
             first, last = size.cuts[name][half]
             WG[:, first:last] = total
 
-        return Scatter(wire, weight_view(PW, name), lambda half: bufs[half], out)
+        return Scatter(
+            wire, weight_view(PW, name), lambda half: bufs[half], out, weight_spare(name)
+        )
 
     def token_out(ref, count):
         def out(half, total):
@@ -924,8 +917,14 @@
     so_ = weight_stream("o", bo0, bo1)
     sc = weight_stream("c", bc0, bc1)
     sw = weight_stream("s", bs0, bs1)
-    sx = Scatter(wire, token_view(XG, tok, place.core), lambda half: bx.at[half], token_out(NG, tok))
-    se = Scatter(wire, token_view(EG, enc, place.core), lambda half: be.at[half], token_out(NE, enc))
+    sx = Scatter(
+        wire, token_view(XG, tok, place.core), lambda half: bx.at[half], token_out(NG, tok),
+        token_spare(bx),
+    )
+    se = Scatter(
+        wire, token_view(EG, enc, place.core), lambda half: be.at[half], token_out(NE, enc),
+        token_spare(be),
+    )
     x_base, e_base = wire.slots(4), wire.slots(4)
     x_out, e_out = wire.sender(px), wire.sender(pe)
 
@@ -957,10 +956,6 @@
             cols = pl.ds(aligned(lax.rem(chip, 4) * size.part, 128), size.part)
             wire.got(mb.at[:, cols], ms_plane + k)
 
-    def result_out():
-        for k in (3, 1, 2, 0):
-            sum_o.middle(k)
-
     def result_back():
         sum_o.finish_core()
         layer_out[...] = after_cross[...] + po_whole[...].astype(F32)
@@ -1010,7 +1005,6 @@
         totals[...] = (sl[0] + sl[1]) + (sl[2] + sl[3])
         bias_totals[...] = (tl[0] + tl[1]) + (tl[2] + tl[3])
 
-    result_out()
     out_grads(low, mixed2, col["co"])
     sp.start(1)
     sp.start(2)
@@ -1019,24 +1013,18 @@
     )
     for c in range(ctx_enc // 1024):
         back.chunk(c * 512, 512)
-    sp.start(0)
+    sp.start(3)
     for c in range(ctx_enc // 1024, ctx_enc // 512):
         back.chunk(c * 512, 512)
     back.finish(q_grad)
-    sp.start(3)
+    sp.pass_near(1)
     part = dot_nt(q_grad[...], WA[:, col["cq"]])
     ca[2] = part.astype(LOW)
     wire.swap(ca.at[2], cb.at[2], cross_slot)
-    sp.pass_near(1)
-    sp.pass_near(2)
     out_grads(E, mkv_grad, col["ckv"])
-    sp.pass_near(0)
     sp.pass_near(3)
     out_grads(n2, q_grad, col["cq"])
-    sc.start(3)
     sc.start(2)
-    sp.pass_level(2)
-    sc.start(1)
 
     def enc_rows(rows_):
         EG[rows_, :] = dot_nt(mkv_grad[rows_, :], WA[:, col["ckv"]]).astype(LOW)
@@ -1044,6 +1032,7 @@
     rows_loop(ctx_enc, 256, enc_rows)
     for k in (1, 2, 3, 0):
         pair_start(EG, pe, enc, e_base, k, e_out)
+    sc.start(1)
     wire.got(cb.at[2], cross_slot)
     n_grad = ca[2].astype(F32) + cb[2].astype(F32)
     extra, gain_two = rms_backward(after_self[...], gains[1:2], n_grad)
@@ -1052,13 +1041,16 @@
     mixed_grad[...] = dot(low[...], WA[:, col["o"]]).astype(LOW)
     for k in (1, 2, 3, 0):
         pair_ready(EG, pe, enc, e_base, k)
-    se.start(3)
+    sc.start(3)
     out_grads(low, mixed1, col["o"])
-    se.start(1)
     se.start(2)
+    sp.pass_near(2)
+    so_.start(0)
+    sp.pass_level(1)
+    sc.pass_near(2)
+    so_.start(3)
+    sc.pass_near(1)
     so_.start(1)
-    sum_o.finish()
-    sc.pass_near(3)
 
     back = PairBack(
         tok, size.pairs, q, kv, e1, rl1, mixed1, mixed_grad, kv_grad, diag, qc, gc, dl, dq
@@ -1077,15 +1069,19 @@
     tok_rows(2)
     pair_start(XG, px, tok, x_base, 2, x_out)
     pair_ready(XG, px, tok, x_base, 1)
-    sc.pass_near(2)
-    so_.start(2)
+    sc.pass_near(3)
+    se.start(0)
+    se.start(1)
     back.chunk(place.below[3] // 4 * 4 * tok, 4 * tok)
     tok_rows(3)
     pair_start(XG, px, tok, x_base, 3, x_out)
     pair_ready(XG, px, tok, x_base, 2)
-    so_.start(3)
-    sc.pass_near(1)
-    so_.start(0)
+    sc.pass_level(1)
+    sx.start(2)
+    se.pass_near(2)
+    sx.start(1)
+    so_.start(2)
+    sc.pass_level(2)
     back.chunk(place.level * 4 * tok, 4 * tok)
     back.finish(q_grad)
     tok_rows(0)
@@ -1093,72 +1089,69 @@
     XG[here_rows, :] = own.astype(LOW)
     pair_start(XG, px, tok, x_base, 0, x_out)
     pair_ready(XG, px, tok, x_base, 3)
-    sp.pass_level(1)
-    so_.pass_near(2)
-    sx.start(2)
     out_grads(n2, q_grad, col["q"])
     pair_ready(XG, px, tok, x_base, 0)
+    sx.pass_near(2)
+    se.pass_near(1)
+    sx.start(3)
+    sp.pass_level(2)
+    out_grads(X, kv_grad, col["kv"])
     so_.pass_near(1)
-    sc.pass_level(2)
-    out_grads(X, kv_grad.at[:, : size.wide], col["k"])
-    sx.start(3)
-    out_grads(X, kv_grad.at[:, size.wide :], col["v"])
-    so_.pass_level(2)
-    sx.pass_near(2)
+    so_.pass_near(2)
+    se.start(3)
+    sw.start(3)
     sw.start(1)
     sx.pass_level(2)
-    se.pass_near(1)
-    sx.start(1)
-    sw.pass_near(1)
-    sw.start(2)
-    se.pass_near(2)
-    sc.pass_level(1)
-    se.start(0)
+    so_.pass_near(3)
+    se.pass_near(3)
+    sx.pass_near(1)
     sx.pass_near(3)
     se.pass_level(1)
+    sc.pass_level(3)
+    se.pass_level(2)
+    so_.pass_level(1)
+    so_.pass_level(3)
+    sw.start(2)
+    sx.pass_level(1)
+    sx.start(0)
+    sx.pass_level(3)
+    so_.pass_near(0)
+    sum_o.finish()
+    sw.pass_near(1)
+    sw.pass_near(2)
     sp.pass_level(3)
-    se.pass_near(3)
+    so_.pass_level(2)
+    sx.pass_near(0)
+    sp.start(0)
     sw.pass_level(1)
-    sx.pass_near(1)
-    se.pass_level(2)
+    sw.start(0)
+    se.pass_level(3)
+    se.pass_near(0)
     sums = bucket_sums(ids, diag, table.shape[1])
     t1[...] = jnp.concatenate(
         (sums, jnp.zeros((sums.shape[0], t1.shape[1] - sums.shape[1]), F32)), axis=1
     )
 
-    se.pass_near(0)
-    sx.pass_level(3)
-    sw.pass_near(2)
-    sx.pass_level(1)
-    sx.start(0)
-    sp.finish()
-    so_.pass_near(3)
-    so_.pass_level(1)
-    sw.start(3)
-    so_.pass_near(0)
-    sx.pass_near(0)
-    sc.pass_level(3)
-    sc.start(0)
-    se.pass_level(3)
-    sw.start(0)
+    tokens_back()
     sw.pass_level(2)
-    tokens_back()
+    sw.pass_near(3)
     input_back()
     small_first()
+    sc.start(0)
+    small_second()
+    sw.pass_near(0)
+    so_.finish()
+    sw.pass_level(3)
+    units_down()
+    sp.pass_near(0)
+    sc.pass_near(0)
+    small_third()
+    sw.finish()
+    sp.finish()
     result_back()
-    sw.pass_near(3)
-    sw.pass_near(0)
-    small_second()
-    so_.pass_level(3)
-    units_down()
-    sw.pass_level(3)
-    so_.finish()
-    small_third()
-    sc.pass_near(0)
     encoder_back()
+    small_last()
     units_back()
-    sw.finish()
-    small_last()
     sc.finish()
     wire.got(NE.at[:, away], e_slot)
     enc_grad[...] = NE[...]
@@ -1250,7 +1243,7 @@
         "pe": vmem(enc_all, model // 2), "NG": full(tok, model), "NE": full(enc, model),
         "ml": vmem(3, 4 * rows, size.part), "ps": vmem(4 * rows, size.part),
         "s1": full(8, model), "s2": full(8, model), "sr": full(2, 8, model),
-        "sl": full(4, 8, model), "t1": full(8, 128), "t2": full(8, 128), "tr": full(2, 8, 128), "tl": full(4, 8, 128), **wire_sems(73, 275),
+        "sl": full(4, 8, model), "t1": full(8, 128), "t2": full(8, 128), "tr": full(2, 8, 128), "tl": full(4, 8, 128), **wire_sems(53, 171),
     }
     names = list(ins) + list(outs) + list(scratch)
     made = pl.pallas_call(

time: 176 us -> 171 us (0.972)
  Pallas kernels: 175 us -> 170 us
    pallas_call x1, Pallas kernels: 172 us -> 168 us  [quick_device(): pl.pallas_call(named(functools.partial(layer_kernel, size), names), out_s...]
where the time goes in v5:
time: 171 us
  Pallas kernels  170 us (99%)
    pallas_call x1, Pallas kernels, quick_device(): pl.pallas_call(named(functools.partial(layer_kernel, size), names), out_s...  168 us

profile of v5, /device:TPU:0, one launch (start us, length us, event | category | flops | bytes accessed | tf_op | source)
XLA Modules:
  0.0 171.2 jit_solution(11495035990854950113)
XLA Ops:
  0.7 167.6 %shard_map.297 = (f32[128,768]{1,0:T(8,128)}, f32[128,768]{1,0:T(8,128)}, f32[64,768]{1,0:T(8,128)}, f32[48,3072]{1,0:T(8,128)}, bf16[48,3072]{1,0:T(8,128)(2,1)}, /*index=5*/f32[8,768]{1,0:T(8,128)}, f32[8,128]{1,0:T(8,128)}) custom-call(f32[128,768]{1,0:T(8,128)} %refs_0_.1, bf16[64,768]{1,0:T(8,128)(2,1)} %refs_1_.1, bf16[48,384]{1,0:T(8,128)(2,1)} %refs_2_.1, ...), custom_call_target="tpu_custom_call" | custom-call | tf_op jit(solution)/shard_map/pallas_call | solution.py:1249
  168.2 2.8 %shard_map.298 = (f32[128,768]{1,0:T(8,128)}, f32[128,768]{1,0:T(8,128)}, f32[64,768]{1,0:T(8,128)}, f32[48,384]{1,0:T(8,128)}, f32[48,384]{1,0:T(8,128)}, /*ind...) custom-call(f32[128,768]{1,0:T(8,128)} %get-tuple-element.39.layer_o, ...), custom_call_target="tpu_custom_call" | custom-call | tf_op jit(solution)/shard_map/pallas_call | solution.py:1266

commit v6 on v5

--- a/solution.py
+++ b/solution.py
@@ -605,15 +605,15 @@
 
 
 def layer_kernel(
-    size, layer_in, encoded, sq, sk, sv, so, cq, ck, cv, co, gate_w, up_w, down_w, gains,
-    table, buckets, order, out_grad,
+    size, layer_src, encoded, sq, sk, sv, so, cq, ck, cv, co, gate_w, up_w, down_w, gains_src,
+    table_src, buckets_src, order_src, out_grad_src,
     layer_out, input_grad, enc_grad, WG, mb, totals, bias_totals,
-    WA, WM, wm, X, E, GR, PW, PM,
+    layer_in, gains, table, buckets, order, out_grad, WA, WM, wm, X, E, GR, PW, PM,
     q, kv, mkv, probes, s, e1, e2, rl1, rl2, mixed1, mixed2, table_rows, ids, bias, diag,
     after_self, after_cross, cross_grad, self_grad, n2, N3, act, GU, PN, PO, low, mixed_grad,
     q_grad, kv_grad, mkv_grad, ca, cb, pn_core, pn_plane, pn_whole, po_core, po_plane, po_whole,
     qc, gc, dl, dq, bs0, bs1, bc0, bc1, bo0, bo1, bp0, bp1, bx, be, px, pe, NG, NE, ml, ps,
-    s1, s2, sr, sl, t1, t2, tr, tl, send_sem, recv_sem,
+    s1, s2, sr, sl, t1, t2, tr, tl, local, send_sem, recv_sem,
 ):
     place = Place(size.ctx)
     wire = Wire(place, send_sem, recv_sem)
@@ -684,23 +684,56 @@
             wire.send(own, own, mg_level + k - 1, place.above[k])
 
     place.signal(place.above[1:] + list(plane_chips))
+    attention = size.attn_cols
+    first = 3 * size.wide
+
+    def load(slot, *pairs):
+        for src, dst in pairs:
+            pltpu.make_async_copy(src, dst, local.at[slot]).start()
+
+    def loaded(slot, whole):
+        pltpu.make_async_copy(whole, whole, local.at[slot]).wait()
+
+    def own_columns(name):
+        return WA.at[own_weights, col[name]]
+
+    load(0, (layer_src, layer_in))
+    load(1, (gains_src, gains))
+    load(2, *((ref, own_columns(n)) for n, ref in (("q", sq), ("k", sk), ("v", sv))))
+    load(3, *((ref, own_columns(n)) for n, ref in (("cq", cq), ("ck", ck), ("cv", cv), ("o", so), ("co", co))))
+    load(4, (encoded, E.at[block_rows(place.here, enc), :]))
+    load(
+        5,
+        *(
+            (ref.at[:, p * quarter : (p + 1) * quarter], wm.at[:, base : base + quarter])
+            for p in range(4)
+            for i, ref in enumerate((gate_w, up_w, down_w))
+            for base in (p * size.part + i * quarter,)
+        ),
+    )
+    load(6, (out_grad_src, out_grad))
+    load(7, (table_src, table))
+    load(8, (buckets_src, buckets))
+    load(9, (order_src, order))
+    loaded(0, layer_in)
+    loaded(1, gains)
     X[here_rows, :] = rms_forward(layer_in[...], gains[0:1]).astype(LOW)
-    for name, ref in zip(("q", "k", "v", "cq", "ck", "cv", "o", "co"), (sq, sk, sv, cq, ck, cv, so, co)):
-        WA[own_weights, col[name]] = ref[...]
-    E[block_rows(place.here, enc), :] = encoded[...]
-    plane_rows = block_rows(place.plane, tok)
-    GR[plane_rows, :] = out_grad[...].astype(LOW)
-    for p in range(4):
-        cols = slice(p * quarter, (p + 1) * quarter)
-        for i, ref in enumerate((gate_w, up_w, down_w)):
-            base = p * size.part + i * quarter
-            wm[:, base : base + quarter] = ref[:, cols]
-    WM[own_weights, :] = wm[:, my_part]
+    loaded(2, WA.at[own_weights, 0:first])
     place.meet(7)
     gx.start_level()
     gs.start_level()
     gx.start_plane()
     gs.start_plane()
+    loaded(3, WA.at[own_weights, first:attention])
+    loaded(4, E.at[block_rows(place.here, enc), :])
+    loaded(5, wm)
+    WM[own_weights, :] = wm[:, my_part]
+    loaded(6, out_grad)
+    plane_rows = block_rows(place.plane, tok)
+    GR[plane_rows, :] = out_grad[...].astype(LOW)
+    loaded(7, table)
+    loaded(8, buckets)
+    loaded(9, order)
     gx.pass_near(0)
     gx.pass_line(0)
     gx.pass_plane(0)
@@ -794,7 +827,6 @@
             gp.pass_plane(1)
             gp.pass_plane(2)
         elif j == 2:
-            gg.start()
             go.finish()
 
     pair_attend(tok, size.pairs, 512, q, kv, s, e1, rl1, mixed1, bias, during_self)
@@ -814,6 +846,7 @@
             gp.pass_near(1)
             gp.pass_near(2)
             gp.pass_near(3)
+            gg.start()
     pair_attend(tok, size.pairs, 512, probes, mkv, s, e2, rl2, mixed2, None, during_cross)
     gp.finish()
     part = dot_nt(mixed2[...], WA[:, col["co"]])
@@ -1200,11 +1233,12 @@
         return [vmem(15, rows, last - first) for first, last in size.cuts[name]]
 
     ins = {
-        "layer_in": layer_in, "encoded": encoded, "sq": self_query, "sk": self_key,
+        "layer_src": layer_in, "encoded": encoded, "sq": self_query, "sk": self_key,
         "sv": self_value, "so": self_out.T, "cq": cross_query, "ck": cross_key,
         "cv": cross_value, "co": cross_out.T, "gate_w": gate_proj, "up_w": up_proj,
-        "down_w": down_proj.T, "gains": norm_gains, "table": position_bias.T,
-        "buckets": bucket_ids.reshape(ctx, tok), "order": block_order, "out_grad": out_grad,
+        "down_w": down_proj.T, "gains_src": norm_gains, "table_src": position_bias.T,
+        "buckets_src": bucket_ids.reshape(ctx, tok), "order_src": block_order,
+        "out_grad_src": out_grad,
     }
     outs = {
         "layer_out": ((tok, model), F32), "input_grad": ((tok, model), F32),
@@ -1215,6 +1249,9 @@
     (bs0, bs1), (bc0, bc1) = streams("s"), streams("c")
     (bo0, bo1), (bp0, bp1) = streams("o"), streams("co")
     scratch = {
+        "layer_in": full(tok, model), "gains": full(*norm_gains.shape),
+        "table": full(heads, buckets), "buckets": pltpu.VMEM((ctx, tok), jnp.int32),
+        "order": pltpu.SMEM((ctx,), jnp.int32), "out_grad": full(tok, model),
         "WA": vmem(model, size.attn_cols), "WM": vmem(model, size.part),
         "wm": vmem(rows, size.mlp_cols), "X": vmem(tok_all, model), "E": vmem(enc_all, model),
         "GR": vmem(tok4, model), "PW": vmem(model, size.attn_cols),
@@ -1243,14 +1280,15 @@
         "pe": vmem(enc_all, model // 2), "NG": full(tok, model), "NE": full(enc, model),
         "ml": vmem(3, 4 * rows, size.part), "ps": vmem(4 * rows, size.part),
         "s1": full(8, model), "s2": full(8, model), "sr": full(2, 8, model),
-        "sl": full(4, 8, model), "t1": full(8, 128), "t2": full(8, 128), "tr": full(2, 8, 128), "tl": full(4, 8, 128), **wire_sems(53, 171),
+        "sl": full(4, 8, model), "t1": full(8, 128), "t2": full(8, 128), "tr": full(2, 8, 128), "tl": full(4, 8, 128),
+        "local": pltpu.SemaphoreType.DMA((10,)), **wire_sems(53, 171),
     }
     names = list(ins) + list(outs) + list(scratch)
     made = pl.pallas_call(
         named(functools.partial(layer_kernel, size), names),
         out_shape=tuple(jax.ShapeDtypeStruct(*spec) for spec in outs.values()),
         in_specs=[
-            pl.BlockSpec(memory_space=pltpu.SMEM if name == "order" else pltpu.VMEM)
+            pl.BlockSpec(memory_space=pl.ANY)
             for name in ins
         ],
         out_specs=tuple(pl.BlockSpec(memory_space=pltpu.VMEM) for _ in outs),

time: 171 us -> 169 us (0.988)
  Pallas kernels: 170 us -> 168 us
    pallas_call x1, Pallas kernels: 168 us -> 166 us  [quick_device(): pl.pallas_call(named(functools.partial(layer_kernel, size), names), out_s...]
where the time goes in v6:
time: 169 us
  Pallas kernels  168 us (99%)
    pallas_call x1, Pallas kernels, quick_device(): pl.pallas_call(named(functools.partial(layer_kernel, size), names), out_s...  166 us

profile of v6, /device:TPU:0, one launch (start us, length us, event | category | flops | bytes accessed | tf_op | source)
XLA Modules:
  0.0 169.3 jit_solution(18177714095508644610)
XLA Ops:
  0.7 165.6 %shard_map.297 = (f32[128,768]{1,0:T(8,128)}, f32[128,768]{1,0:T(8,128)}, f32[64,768]{1,0:T(8,128)}, f32[48,3072]{1,0:T(8,128)}, bf16[48,3072]{1,0:T(8,128)(2,1)}, /*index=5*/f32[8,768]{1,0:T(8,128)}, f32[8,128]{1,0:T(8,128)}) custom-call(f32[128,768]{1,0:T(8,128)} %refs_0_.1, bf16[64,768]{1,0:T(8,128)(2,1)} %refs_1_.1, bf16[48,384]{1,0:T(8,128)(2,1)} %refs_2_.1, ...), custom_call_target="tpu_custom_call" | custom-call | tf_op jit(solution)/shard_map/pallas_call | solution.py:1287
  166.3 2.8 %shard_map.298 = (f32[128,768]{1,0:T(8,128)}, f32[128,768]{1,0:T(8,128)}, f32[64,768]{1,0:T(8,128)}, f32[48,384]{1,0:T(8,128)}, f32[48,384]{1,0:T(8,128)}, /*ind...) custom-call(f32[128,768]{1,0:T(8,128)} %get-tuple-element.39.layer_o, ...), custom_call_target="tpu_custom_call" | custom-call | tf_op jit(solution)/shard_map/pallas_call | solution.py:1304

commit v7 on v6

--- a/solution.py
+++ b/solution.py
@@ -917,8 +917,6 @@
             ms_level + k - 1,
             place.above[k],
         )
-    for k in (3, 1, 2, 0):
-        sum_o.middle(k)
     sum_n.finish()
     sum_n.finish_core()
     extra, gain_three = rms_backward(after_cross[...], gains[2:3], pn_whole[...].astype(F32))
@@ -1050,6 +1048,8 @@
     for c in range(ctx_enc // 1024, ctx_enc // 512):
         back.chunk(c * 512, 512)
     back.finish(q_grad)
+    for k in (3, 1, 2, 0):
+        sum_o.middle(k)
     sp.pass_near(1)
     part = dot_nt(q_grad[...], WA[:, col["cq"]])
     ca[2] = part.astype(LOW)

time: 169 us -> 169 us (level)
  no operation moved by 1% of the time
where the time goes in v7:
time: 169 us; the launch traced here: 168 us
  Pallas kernels  168 us (99%)
    pallas_call x1, Pallas kernels, quick_device(): pl.pallas_call(named(functools.partial(layer_kernel, size), names), out_s...  165 us

profile of v7, /device:TPU:0, one launch (start us, length us, event | category | flops | bytes accessed | tf_op | source)
XLA Modules:
  0.0 168.4 jit_solution(8565362161238631702)
XLA Ops:
  0.7 164.7 %shard_map.297 = (f32[128,768]{1,0:T(8,128)}, f32[128,768]{1,0:T(8,128)}, f32[64,768]{1,0:T(8,128)}, f32[48,3072]{1,0:T(8,128)}, bf16[48,3072]{1,0:T(8,128)(2,1)}, /*index=5*/f32[8,768]{1,0:T(8,128)}, f32[8,128]{1,0:T(8,128)}) custom-call(f32[128,768]{1,0:T(8,128)} %refs_0_.1, bf16[64,768]{1,0:T(8,128)(2,1)} %refs_1_.1, bf16[48,384]{1,0:T(8,128)(2,1)} %refs_2_.1, ...), custom_call_target="tpu_custom_call" | custom-call | tf_op jit(solution)/shard_map/pallas_call | solution.py:1287
  165.4 2.8 %shard_map.298 = (f32[128,768]{1,0:T(8,128)}, f32[128,768]{1,0:T(8,128)}, f32[64,768]{1,0:T(8,128)}, f32[48,384]{1,0:T(8,128)}, f32[48,384]{1,0:T(8,128)}, /*ind...) custom-call(f32[128,768]{1,0:T(8,128)} %get-tuple-element.39.layer_o, ...), custom_call_target="tpu_custom_call" | custom-call | tf_op jit(solution)/shard_map/pallas_call | solution.py:1304
